TPU v7x, 256 devices: a whole 4x4x8 slice. The times are simulated.
256 devices in a mesh: rows: 64 (over y, z, core), rhs: 4 (over x).
Axes of the slice: x: 4, y: 4, z: 8, core: 2. Of those that a mesh axis runs over, the one named last changes fastest.
Arguments:
- rhs: float32 [65536, 2048], P('rows', 'rhs'), parts along dimension 1, may hold values from -6 to 6
- leaf_inverse: float32 [65536, 1024], P('rows'), may hold values from -0.1875 to 0.1875
- basis_left: float32 [3, 65536, 128], P(None, 'rows'), may hold values from -0.5 to 0.5
- basis_right: float32 [3, 65536, 128], P(None, 'rows'), may hold values from -0.03125 to 0.03125
- cores: float32 [7, 256, 256], replicated, may hold values from -0.375 to 0.375
Outputs:
- solution: float32 [65536, 2048], P('rows', 'rhs'), parts along dimension 1
There are 4 independent parts, one for each index of `rhs`. A program takes and returns all parts, laid end to end along the dimension named above; an argument that names none is the same for every part. Nothing has to cross between parts.
All inputs are finite; a program needn't handle non-finite values.
Results may differ from a plain program's by a relative error of at most 0.00011.
Values sent between devices are 32-bit elements; how exact they have to be, the bound alone decides.
No kernel may reach another device: no remote copies, remote signals or barrier semaphores. Data moves between devices by JAX's collectives and lax.ppermute only.
A program may use at most 64 MiB of HBM per device.

v0:
```python
import jax
import jax.numpy as jnp
from jax import lax
from jax.sharding import PartitionSpec as P

LEVELS = 3


def swapped(x, axis, apart):
    return lax.ppermute(x, axis, [(i, i ^ 1 << apart) for i in range(lax.axis_size(axis))])


def on_device(rhs, leaf_inverse, basis_left, basis_right, cores):
    highest = lax.Precision.HIGHEST
    current = jnp.dot(leaf_inverse, rhs, precision=highest, preferred_element_type=jnp.float32)
    devices = lax.axis_size("rows")
    tree_depth = devices.bit_length() - 1
    position = lax.axis_index("rows")
    rank_size = basis_left.shape[2]
    for level_index in range(LEVELS, 0, -1):
        span_devices = devices >> level_index
        child_index = position // span_devices
        node_index = child_index // 2
        half_index = child_index % 2
        partial_value = lax.dot_general(
            basis_right[level_index - 1],
            current,
            (((0,), (0,)), ((), ())),
            precision=highest,
            preferred_element_type=jnp.float32,
        )
        child_total = partial_value
        for bit_number in range(tree_depth - level_index):
            child_total = child_total + swapped(child_total, "rows", bit_number)
        sibling = swapped(child_total, "rows", tree_depth - level_index)
        stacked = jnp.where(
            half_index == 0,
            jnp.concatenate([child_total, sibling], axis=0),
            jnp.concatenate([sibling, child_total], axis=0),
        )
        core_block = lax.dynamic_index_in_dim(
            cores, 2 ** (level_index - 1) - 1 + node_index, 0, keepdims=False
        )
        core_rows = lax.dynamic_slice_in_dim(core_block, half_index * rank_size, rank_size, 0)
        coefficients = jnp.dot(
            core_rows, stacked, precision=highest, preferred_element_type=jnp.float32
        )
        current = current - jnp.dot(
            basis_left[level_index - 1],
            coefficients,
            precision=highest,
            preferred_element_type=jnp.float32,
        )
    return current


def solution(mesh):
    placed = (P("rows", "rhs"), P("rows", None), P(None, "rows", None), P(None, "rows", None), P())
    return jax.shard_map(
        on_device, mesh=mesh, in_specs=placed, out_specs=P("rows", "rhs"), check_vma=False
    )
```

profile of v0, /device:TPU:4, one launch (start us, length us, event | category | flops | bytes accessed | tf_op | source)
XLA Modules:
  0.0 186.6 jit_solution(489066136894527179)
XLA Ops:
  0.0 0.0 copy-start
  0.0 1.6 copy-done
  1.6 8.6 %fusion.45 = f32[1024,512]{1,0:T(8,128)S(1)} fusion(f32[1024,1024]{1,0:T(8,128)} %param.6, f32[1024,512]{1,0:T(8,128)S(1)} %copy-done), kind=kOutput, calls=%fused_computation.54 | convolution fusion | flops 6442450944 | bytes 8388608 | tf_op jit(solution)/shard_map/dot_general | solution.py:15
  10.2 0.0 copy-start.3
  10.2 2.9 %convolution_bitcast_fusion.2 = f32[128,512]{1,0:T(8,128)S(1)} fusion(f32[1024,512]{1,0:T(8,128)S(1)} %fusion.45, f32[3,1024,128]{2,1,0:T(8,128)} %param.8), kind=kOutput, calls=%fused_computation.5 | convolution fusion | flops 805306368 | bytes 2883584 | tf_op jit(solution)/shard_map/dot_general | solution.py:25
  13.1 0.1 collective-permute-start
  13.2 1.5 collective-permute-done
  14.8 2.0 %collective-permute-start.1 = (f32[128,512]{1,0:T(8,128)S(1)}, f32[128,512]{1,0:T(8,128)S(1)}, u32[]{:S(2)}, u32[]{:S(2)}) collective-permute-start(f32[128,512]{1,0:T(8,128)S(1)} %add.87), channel_id=1, source_target_pairs={{0,8},{4,12},{8,0},{12,4},{16,24},{20,28},{24,16},{28,20},{32,40},... | collective-permute-start | bytes 786440 | tf_op jit(solution)/shard_map/ppermute | solution.py:10
  16.8 6.6 %collective-permute-done.1 = f32[128,512]{1,0:T(8,128)S(1)} collective-permute-done((f32[128,512]{1,0:T(8,128)S(1)}, f32[128,512]{1,0:T(8,128)S(1)}, u32[]{:S(2)}, u32[]{:S(2)}) %collective-permute-start.1) | collective-permute-done | bytes 262176 | tf_op jit(solution)/shard_map/ppermute | solution.py:10
  23.4 0.0 copy-done.3
  23.5 3.4 %collective-permute-start.2 = (f32[128,512]{1,0:T(8,128)S(1)}, f32[128,512]{1,0:T(8,128)S(1)}, u32[]{:S(2)}, u32[]{:S(2)}) collective-permute-start(f32[128,512]{1,0:T(8,128)S(1)} %add.88), channel_id=1, source_target_pairs={{0,16},{4,20},{8,24},{12,28},{16,0},{20,4},{24,8},{28,12},{32,48},... | collective-permute-start | bytes 786440 | tf_op jit(solution)/shard_map/ppermute | solution.py:10
  26.8 11.5 %collective-permute-done.2 = f32[128,512]{1,0:T(8,128)S(1)} collective-permute-done((f32[128,512]{1,0:T(8,128)S(1)}, f32[128,512]{1,0:T(8,128)S(1)}, u32[]{:S(2)}, u32[]{:S(2)}) %collective-permute-start.2) | collective-permute-done | bytes 262176 | tf_op jit(solution)/shard_map/ppermute | solution.py:10
  38.4 6.3 %collective-permute-start.3 = (f32[128,512]{1,0:T(8,128)S(1)}, f32[128,512]{1,0:T(8,128)S(1)}, u32[]{:S(2)}, u32[]{:S(2)}) collective-permute-start(f32[128,512]{1,0:T(8,128)S(1)} %add.89), channel_id=1, source_target_pairs={{0,32},{4,36},{8,40},{12,44},{16,48},{20,52},{24,56},{28,60},{32,0... | collective-permute-start | bytes 786440 | tf_op jit(solution)/shard_map/ppermute | solution.py:10
  44.7 11.7 %collective-permute-done.3 = f32[128,512]{1,0:T(8,128)S(1)} collective-permute-done((f32[128,512]{1,0:T(8,128)S(1)}, f32[128,512]{1,0:T(8,128)S(1)}, u32[]{:S(2)}, u32[]{:S(2)}) %collective-permute-start.3) | collective-permute-done | bytes 262176 | tf_op jit(solution)/shard_map/ppermute | solution.py:10
  56.4 1.4 fusion
  57.8 3.6 %bitcast_subtract_fusion.2 = f32[1024,512]{1,0:T(8,128)S(1)} fusion(f32[1024,512]{1,0:T(8,128)} %copy-done.3, f32[128,512]{1,0:T(8,128)S(1)} %fusion, f32[3,1024,128]{2,1,0:T(8,128)} %param.7), kind=kOutput, calls=%fused_computation.2 | convolution fusion | flops 805830656 | bytes 4980736 | tf_op jit(solution)/shard_map/dot_general | solution.py:48
  61.4 0.0 copy-start.2
  61.4 2.9 %convolution_bitcast_fusion.1 = f32[128,512]{1,0:T(8,128)S(1)} fusion(f32[1024,512]{1,0:T(8,128)S(1)} %bitcast_subtract_fusion.2, f32[3,1024,128]{2,1,0:T(8,128)} %param.8), kind=kOutput, calls=%fused_computation.4 | convolution fusion | flops 805306368 | bytes 2883584 | tf_op jit(solution)/shard_map/dot_general | solution.py:25
  64.3 0.1 collective-permute-start.4
  64.4 1.5 collective-permute-done.4
  65.9 0.1 collective-permute-start.5
  66.0 8.3 %collective-permute-done.5 = f32[128,512]{1,0:T(8,128)S(1)} collective-permute-done((f32[128,512]{1,0:T(8,128)S(1)}, f32[128,512]{1,0:T(8,128)S(1)}, u32[]{:S(2)}, u32[]{:S(2)}) %collective-permute-start.5) | collective-permute-done | bytes 262176 | tf_op jit(solution)/shard_map/ppermute | solution.py:10
  74.4 0.0 copy-done.2
  74.4 2.4 %collective-permute-start.6 = (f32[128,512]{1,0:T(8,128)S(1)}, f32[128,512]{1,0:T(8,128)S(1)}, u32[]{:S(2)}, u32[]{:S(2)}) collective-permute-start(f32[128,512]{1,0:T(8,128)S(1)} %add.94), channel_id=1, source_target_pairs={{0,16},{4,20},{8,24},{12,28},{16,0},{20,4},{24,8},{28,12},{32,48},... | collective-permute-start | bytes 786440 | tf_op jit(solution)/shard_map/ppermute | solution.py:10
  76.9 11.8 %collective-permute-done.6 = f32[128,512]{1,0:T(8,128)S(1)} collective-permute-done((f32[128,512]{1,0:T(8,128)S(1)}, f32[128,512]{1,0:T(8,128)S(1)}, u32[]{:S(2)}, u32[]{:S(2)}) %collective-permute-start.6) | collective-permute-done | bytes 262176 | tf_op jit(solution)/shard_map/ppermute | solution.py:10
  88.7 3.1 %collective-permute-start.7 = (f32[128,512]{1,0:T(8,128)S(1)}, f32[128,512]{1,0:T(8,128)S(1)}, u32[]{:S(2)}, u32[]{:S(2)}) collective-permute-start(f32[128,512]{1,0:T(8,128)S(1)} %add.95), channel_id=1, source_target_pairs={{0,32},{4,36},{8,40},{12,44},{16,48},{20,52},{24,56},{28,60},{32,0... | collective-permute-start | bytes 786440 | tf_op jit(solution)/shard_map/ppermute | solution.py:10
  91.9 14.0 %collective-permute-done.7 = f32[128,512]{1,0:T(8,128)S(1)} collective-permute-done((f32[128,512]{1,0:T(8,128)S(1)}, f32[128,512]{1,0:T(8,128)S(1)}, u32[]{:S(2)}, u32[]{:S(2)}) %collective-permute-start.7) | collective-permute-done | bytes 262176 | tf_op jit(solution)/shard_map/ppermute | solution.py:10
  105.9 1.7 collective-permute-start.8
  107.6 6.4 %collective-permute-done.8 = f32[128,512]{1,0:T(8,128)S(1)} collective-permute-done((f32[128,512]{1,0:T(8,128)S(1)}, f32[128,512]{1,0:T(8,128)S(1)}, u32[]{:S(2)}, u32[]{:S(2)}) %collective-permute-start.8) | collective-permute-done | bytes 262176 | tf_op jit(solution)/shard_map/ppermute | solution.py:10
  114.0 1.4 fusion.6
  115.4 3.6 %bitcast_subtract_fusion.1 = f32[1024,512]{1,0:T(8,128)S(1)} fusion(f32[1024,512]{1,0:T(8,128)} %copy-done.2, f32[128,512]{1,0:T(8,128)S(1)} %fusion.6, f32[3,1024,128]{2,1,0:T(8,128)} %param.7), kind=kOutput, calls=%fused_computation.1 | convolution fusion | flops 805830656 | bytes 4980736 | tf_op jit(solution)/shard_map/dot_general | solution.py:48
  119.0 0.0 copy-start.1
  119.0 2.9 %convolution_bitcast_fusion = f32[128,512]{1,0:T(8,128)S(1)} fusion(f32[1024,512]{1,0:T(8,128)S(1)} %bitcast_subtract_fusion.1, f32[3,1024,128]{2,1,0:T(8,128)} %param.8), kind=kOutput, calls=%fused_computation.3 | convolution fusion | flops 805306368 | bytes 2883584 | tf_op jit(solution)/shard_map/dot_general | solution.py:25
  121.9 0.1 collective-permute-start.9
  122.0 1.5 collective-permute-done.9
  123.5 0.1 collective-permute-start.10
  123.6 8.3 %collective-permute-done.10 = f32[128,512]{1,0:T(8,128)S(1)} collective-permute-done((f32[128,512]{1,0:T(8,128)S(1)}, f32[128,512]{1,0:T(8,128)S(1)}, u32[]{:S(2)}, u32[]{:S(2)}) %collective-permute-start.10) | collective-permute-done | bytes 262176 | tf_op jit(solution)/shard_map/ppermute | solution.py:10
  132.0 0.0 copy-done.1
  132.0 2.3 %collective-permute-start.11 = (f32[128,512]{1,0:T(8,128)S(1)}, f32[128,512]{1,0:T(8,128)S(1)}, u32[]{:S(2)}, u32[]{:S(2)}) collective-permute-start(f32[128,512]{1,0:T(8,128)S(1)} %add.101), channel_id=1, source_target_pairs={{0,16},{4,20},{8,24},{12,28},{16,0},{20,4},{24,8},{28,12},{32,48},... | collective-permute-start | bytes 786440 | tf_op jit(solution)/shard_map/ppermute | solution.py:10
  134.3 11.8 %collective-permute-done.11 = f32[128,512]{1,0:T(8,128)S(1)} collective-permute-done((f32[128,512]{1,0:T(8,128)S(1)}, f32[128,512]{1,0:T(8,128)S(1)}, u32[]{:S(2)}, u32[]{:S(2)}) %collective-permute-start.11) | collective-permute-done | bytes 262176 | tf_op jit(solution)/shard_map/ppermute | solution.py:10
  146.2 3.3 %collective-permute-start.12 = (f32[128,512]{1,0:T(8,128)S(1)}, f32[128,512]{1,0:T(8,128)S(1)}, u32[]{:S(2)}, u32[]{:S(2)}) collective-permute-start(f32[128,512]{1,0:T(8,128)S(1)} %add.102), channel_id=1, source_target_pairs={{0,32},{4,36},{8,40},{12,44},{16,48},{20,52},{24,56},{28,60},{32,0... | collective-permute-start | bytes 786440 | tf_op jit(solution)/shard_map/ppermute | solution.py:10
  149.5 13.5 %collective-permute-done.12 = f32[128,512]{1,0:T(8,128)S(1)} collective-permute-done((f32[128,512]{1,0:T(8,128)S(1)}, f32[128,512]{1,0:T(8,128)S(1)}, u32[]{:S(2)}, u32[]{:S(2)}) %collective-permute-start.12) | collective-permute-done | bytes 262176 | tf_op jit(solution)/shard_map/ppermute | solution.py:10
  163.0 1.7 collective-permute-start.13
  164.7 6.7 %collective-permute-done.13 = f32[128,512]{1,0:T(8,128)S(1)} collective-permute-done((f32[128,512]{1,0:T(8,128)S(1)}, f32[128,512]{1,0:T(8,128)S(1)}, u32[]{:S(2)}, u32[]{:S(2)}) %collective-permute-start.13) | collective-permute-done | bytes 262176 | tf_op jit(solution)/shard_map/ppermute | solution.py:10
  171.4 3.3 %collective-permute-start.14 = (f32[128,512]{1,0:T(8,128)S(1)}, f32[128,512]{1,0:T(8,128)S(1)}, u32[]{:S(2)}, u32[]{:S(2)}) collective-permute-start(f32[128,512]{1,0:T(8,128)S(1)} %add.104), channel_id=1, source_target_pairs={{0,128},{4,132},{8,136},{12,140},{16,144},{20,148},{24,152},{28,15... | collective-permute-start | bytes 786440 | tf_op jit(solution)/shard_map/ppermute | solution.py:10
  174.6 5.7 %collective-permute-done.14 = f32[128,512]{1,0:T(8,128)S(1)} collective-permute-done((f32[128,512]{1,0:T(8,128)S(1)}, f32[128,512]{1,0:T(8,128)S(1)}, u32[]{:S(2)}, u32[]{:S(2)}) %collective-permute-start.14) | collective-permute-done | bytes 262176 | tf_op jit(solution)/shard_map/ppermute | solution.py:10
  180.3 1.4 fusion.12
  181.7 4.9 %bitcast_subtract_fusion = f32[1024,512]{1,0:T(8,128)} fusion(f32[1024,512]{1,0:T(8,128)} %copy-done.1, f32[128,512]{1,0:T(8,128)S(1)} %fusion.12, f32[3,1024,128]{2,1,0:T(8,128)} %param.7), kind=kOutput, calls=%fused_computation | convolution fusion | flops 805830656 | bytes 4980736 | tf_op jit(solution)/shard_map/dot_general | solution.py:48
  (12 shorter events, 0.5 us)
Async XLA Ops:
  0.0 1.6 copy-start
  10.2 13.2 %copy-start.3 = (f32[1024,512]{1,0:T(8,128)}, f32[1024,512]{1,0:T(8,128)S(1)}, u32[]{:S(2)}) copy-start(f32[1024,512]{1,0:T(8,128)S(1)} %fusion.45) | copy-start | bytes 6291460
  13.1 1.6 collective-permute-start
  14.8 8.6 %collective-permute-start.1 = (f32[128,512]{1,0:T(8,128)S(1)}, f32[128,512]{1,0:T(8,128)S(1)}, u32[]{:S(2)}, u32[]{:S(2)}) collective-permute-start(f32[128,512]{1,0:T(8,128)S(1)} %add.87), channel_id=1, source_target_pairs={{0,8},{4,12},{8,0},{12,4},{16,24},{20,28},{24,16},{28,20},{32,40},... | collective-permute-start | bytes 786440 | tf_op jit(solution)/shard_map/ppermute | solution.py:10
  23.5 14.9 %collective-permute-start.2 = (f32[128,512]{1,0:T(8,128)S(1)}, f32[128,512]{1,0:T(8,128)S(1)}, u32[]{:S(2)}, u32[]{:S(2)}) collective-permute-start(f32[128,512]{1,0:T(8,128)S(1)} %add.88), channel_id=1, source_target_pairs={{0,16},{4,20},{8,24},{12,28},{16,0},{20,4},{24,8},{28,12},{32,48},... | collective-permute-start | bytes 786440 | tf_op jit(solution)/shard_map/ppermute | solution.py:10
  38.4 18.0 %collective-permute-start.3 = (f32[128,512]{1,0:T(8,128)S(1)}, f32[128,512]{1,0:T(8,128)S(1)}, u32[]{:S(2)}, u32[]{:S(2)}) collective-permute-start(f32[128,512]{1,0:T(8,128)S(1)} %add.89), channel_id=1, source_target_pairs={{0,32},{4,36},{8,40},{12,44},{16,48},{20,52},{24,56},{28,60},{32,0... | collective-permute-start | bytes 786440 | tf_op jit(solution)/shard_map/ppermute | solution.py:10
  61.4 13.0 %copy-start.2 = (f32[1024,512]{1,0:T(8,128)}, f32[1024,512]{1,0:T(8,128)S(1)}, u32[]{:S(2)}) copy-start(f32[1024,512]{1,0:T(8,128)S(1)} %bitcast_subtract_fusion.2) | copy-start | bytes 6291460
  64.3 1.6 collective-permute-start.4
  65.9 8.4 %collective-permute-start.5 = (f32[128,512]{1,0:T(8,128)S(1)}, f32[128,512]{1,0:T(8,128)S(1)}, u32[]{:S(2)}, u32[]{:S(2)}) collective-permute-start(f32[128,512]{1,0:T(8,128)S(1)} %add.93), channel_id=1, source_target_pairs={{0,8},{4,12},{8,0},{12,4},{16,24},{20,28},{24,16},{28,20},{32,40},... | collective-permute-start | bytes 786440 | tf_op jit(solution)/shard_map/ppermute | solution.py:10
  74.4 14.3 %collective-permute-start.6 = (f32[128,512]{1,0:T(8,128)S(1)}, f32[128,512]{1,0:T(8,128)S(1)}, u32[]{:S(2)}, u32[]{:S(2)}) collective-permute-start(f32[128,512]{1,0:T(8,128)S(1)} %add.94), channel_id=1, source_target_pairs={{0,16},{4,20},{8,24},{12,28},{16,0},{20,4},{24,8},{28,12},{32,48},... | collective-permute-start | bytes 786440 | tf_op jit(solution)/shard_map/ppermute | solution.py:10
  88.7 17.1 %collective-permute-start.7 = (f32[128,512]{1,0:T(8,128)S(1)}, f32[128,512]{1,0:T(8,128)S(1)}, u32[]{:S(2)}, u32[]{:S(2)}) collective-permute-start(f32[128,512]{1,0:T(8,128)S(1)} %add.95), channel_id=1, source_target_pairs={{0,32},{4,36},{8,40},{12,44},{16,48},{20,52},{24,56},{28,60},{32,0... | collective-permute-start | bytes 786440 | tf_op jit(solution)/shard_map/ppermute | solution.py:10
  105.9 8.1 %collective-permute-start.8 = (f32[128,512]{1,0:T(8,128)S(1)}, f32[128,512]{1,0:T(8,128)S(1)}, u32[]{:S(2)}, u32[]{:S(2)}) collective-permute-start(f32[128,512]{1,0:T(8,128)S(1)} %add.96), channel_id=1, source_target_pairs={{0,64},{4,68},{8,72},{12,76},{16,80},{20,84},{24,88},{28,92},{32,9... | collective-permute-start | bytes 786440 | tf_op jit(solution)/shard_map/ppermute | solution.py:10
  119.0 13.0 %copy-start.1 = (f32[1024,512]{1,0:T(8,128)}, f32[1024,512]{1,0:T(8,128)S(1)}, u32[]{:S(2)}) copy-start(f32[1024,512]{1,0:T(8,128)S(1)} %bitcast_subtract_fusion.1) | copy-start | bytes 6291460
  121.9 1.6 collective-permute-start.9
  123.5 8.4 %collective-permute-start.10 = (f32[128,512]{1,0:T(8,128)S(1)}, f32[128,512]{1,0:T(8,128)S(1)}, u32[]{:S(2)}, u32[]{:S(2)}) collective-permute-start(f32[128,512]{1,0:T(8,128)S(1)} %add.100), channel_id=1, source_target_pairs={{0,8},{4,12},{8,0},{12,4},{16,24},{20,28},{24,16},{28,20},{32,40},... | collective-permute-start | bytes 786440 | tf_op jit(solution)/shard_map/ppermute | solution.py:10
  132.0 14.1 %collective-permute-start.11 = (f32[128,512]{1,0:T(8,128)S(1)}, f32[128,512]{1,0:T(8,128)S(1)}, u32[]{:S(2)}, u32[]{:S(2)}) collective-permute-start(f32[128,512]{1,0:T(8,128)S(1)} %add.101), channel_id=1, source_target_pairs={{0,16},{4,20},{8,24},{12,28},{16,0},{20,4},{24,8},{28,12},{32,48},... | collective-permute-start | bytes 786440 | tf_op jit(solution)/shard_map/ppermute | solution.py:10
  146.2 16.8 %collective-permute-start.12 = (f32[128,512]{1,0:T(8,128)S(1)}, f32[128,512]{1,0:T(8,128)S(1)}, u32[]{:S(2)}, u32[]{:S(2)}) collective-permute-start(f32[128,512]{1,0:T(8,128)S(1)} %add.102), channel_id=1, source_target_pairs={{0,32},{4,36},{8,40},{12,44},{16,48},{20,52},{24,56},{28,60},{32,0... | collective-permute-start | bytes 786440 | tf_op jit(solution)/shard_map/ppermute | solution.py:10
  163.0 8.3 %collective-permute-start.13 = (f32[128,512]{1,0:T(8,128)S(1)}, f32[128,512]{1,0:T(8,128)S(1)}, u32[]{:S(2)}, u32[]{:S(2)}) collective-permute-start(f32[128,512]{1,0:T(8,128)S(1)} %add.103), channel_id=1, source_target_pairs={{0,64},{4,68},{8,72},{12,76},{16,80},{20,84},{24,88},{28,92},{32,9... | collective-permute-start | bytes 786440 | tf_op jit(solution)/shard_map/ppermute | solution.py:10
  171.4 9.0 %collective-permute-start.14 = (f32[128,512]{1,0:T(8,128)S(1)}, f32[128,512]{1,0:T(8,128)S(1)}, u32[]{:S(2)}, u32[]{:S(2)}) collective-permute-start(f32[128,512]{1,0:T(8,128)S(1)} %add.104), channel_id=1, source_target_pairs={{0,128},{4,132},{8,136},{12,140},{16,144},{20,148},{24,152},{28,15... | collective-permute-start | bytes 786440 | tf_op jit(solution)/shard_map/ppermute | solution.py:10
where the time goes:
time: 187 us
  waiting for transfers between devices  121 us (65%)
  matrix products  33.4 us (18%)
  starting transfers between devices  30 us (16%)
    ppermute x15, waiting for transfers between devices, swapped(): lax.ppermute(x, axis, [(i, i ^ 1 << apart) for i in range(lax.axis_size(a...  121 us
    ppermute x15, starting transfers between devices, swapped(): lax.ppermute(x, axis, [(i, i ^ 1 << apart) for i in range(lax.axis_size(a...  30 us
    dot_general x3, matrix products, on_device(): jnp.dot(basis_left[level_index - 1], coefficients, precision=highest, pre...  12 us
    dot_general x1, matrix products, on_device(): jnp.dot(leaf_inverse, rhs, precision=highest, preferred_element_type=jnp....  8.63 us
    dot_general x3, matrix products, on_device(): lax.dot_general(basis_right[level_index - 1], current, (((0,), (0,)), (()...  8.6 us
    dot_general x3, matrix products, on_device(): jnp.dot(core_rows, stacked, precision=highest, preferred_element_type=jnp...  4.1 us
  transfers between devices with their start and end apart: 15, of which 15 were waited for; matrix products, arithmetic and copies ran while one was open for 0% of the time, Pallas kernels for 0%

commit v1 on v0

v1 whole, which is shorter than its diff:
```python
import functools

import jax
import jax.numpy as jnp
from jax import lax
from jax.experimental import pallas as pl
from jax.experimental.pallas import tpu as pltpu
from jax.sharding import PartitionSpec as P


XS = 4
RANK = 128
LEAF = 1024
COLS = 512
QUARTER = RANK // XS
NN = (((1,), (0,)), ((), ()))
NT = (((1,), (1,)), ((), ()))
VMEM = pl.BlockSpec(memory_space=pltpu.VMEM)
SMEM = pl.BlockSpec(memory_space=pltpu.SMEM)
ANY = pl.BlockSpec(memory_space=pl.ANY)


def split(a):
    hi = a.astype(jnp.bfloat16)
    return hi, (a - hi.astype(jnp.float32)).astype(jnp.bfloat16)


def dot3(a, b, dims):
    ca, cb = dims[0][0][0], dims[0][1][0]
    lhs = jnp.concatenate([a[0], a[0], a[1]], axis=ca)
    rhs = jnp.concatenate([b[0], b[1], b[0]], axis=cb)
    return lax.dot_general(lhs, rhs, dims, preferred_element_type=jnp.float32)


def cost(flops, size):
    return pl.CostEstimate(flops=flops, bytes_accessed=size, transcendentals=0)


def params(mib):
    return pltpu.CompilerParams(vmem_limit_bytes=mib << 20)


def in_hbm(a):
    return pltpu.with_memory_space_constraint(a, pltpu.HBM)


def in_chip(*arrays):
    return tuple(pltpu.with_memory_space_constraint(a, pltpu.VMEM) for a in arrays)


def f32(*shape):
    return pltpu.VMEM(shape, jnp.float32)


def bf16(*shape):
    return pltpu.VMEM(shape, jnp.bfloat16)


def far(*shape):
    return pltpu.HBM(shape, jnp.float32)


def open_kernel(place, right, left2, left3, rhs, gram, x_hi, x_lo, acc):
    i = pl.program_id(0)

    @pl.when(i == 0)
    def _():
        acc[...] = jnp.zeros_like(acc)

    rows = pl.ds(pl.multiple_of(i * rhs.shape[0], rhs.shape[0]), rhs.shape[0])
    x_hi[rows, :], x_lo[rows, :] = split(rhs[...])
    rt = split(jnp.concatenate([right[0].T, right[1].T], axis=0))
    r1 = rt[0][:RANK], rt[1][:RANK]
    acc[:, : 2 * RANK] += dot3(split(left3[0].T), rt, NT)
    acc[:, 2 * RANK :] += dot3(split(left2[0].T), r1, NT)

    @pl.when(i == pl.num_programs(0) - 1)
    def _():
        gram[...] = acc[pl.ds(pl.multiple_of(place[0] * QUARTER, QUARTER), QUARTER), :]


def open_stage(place, right, left, rhs):
    steps = 2
    height = LEAF // steps
    return pl.pallas_call(
        open_kernel,
        grid=(steps,),
        in_specs=[
            SMEM,
            pl.BlockSpec((2, height, RANK), lambda i: (0, i, 0)),
            pl.BlockSpec((1, height, RANK), lambda i: (1, i, 0)),
            pl.BlockSpec((1, height, RANK), lambda i: (2, i, 0)),
            pl.BlockSpec((height, COLS), lambda i: (i, 0)),
        ],
        out_specs=[VMEM] * 3,
        out_shape=[f32(QUARTER, 3 * RANK), bf16(LEAF, COLS), bf16(LEAF, COLS)],
        scratch_shapes=[pltpu.VMEM((RANK, 3 * RANK), jnp.float32)],
        compiler_params=params(12),
        cost_estimate=cost(6 * LEAF * RANK * 3 * RANK, 4 << 20),
        name="open_stage",
    )(place, in_hbm(right), in_hbm(left), in_hbm(left), in_hbm(rhs))


def leaf_kernel(first, last, place, leaf, right, x_hi, x_lo, *rest):
    i = pl.program_id(0)
    y = dot3(split(leaf[...]), (x_hi[...], x_lo[...]), NN)
    rt = split(jnp.concatenate([right[0].T, right[1].T, right[2].T], axis=0))
    part = dot3(rt, split(y), NN)
    if first:
        y0, *ends = rest
    else:
        before, _, y0, *ends = rest
    acc = ends[-1]
    y0[...] = y

    @pl.when(i == 0)
    def _():
        acc[...] = part if first else before[...] + part

    @pl.when(i > 0)
    def _():
        acc[...] += part

    if not last:
        return
    keep, send = ends[:2]

    @pl.when(i == pl.num_programs(0) - 1)
    def _():
        q = acc[...]
        first_half, second_half = q[:, : COLS // 2].T, q[:, COLS // 2 :].T

        @pl.when(place[0] == 0)
        def _():
            keep[...] = first_half
            send[...] = second_half

        @pl.when(place[0] == 1)
        def _():
            keep[...] = second_half
            send[...] = first_half


def leaf_part(step, parts, place, leaf, right, halves, before=None, y0=None):
    first, last = step == 0, step == parts - 1
    steps = 2
    height = LEAF // parts // steps
    ends = [f32(COLS // 2, 3 * RANK)] * 2 if last else [f32(3 * RANK, COLS)]
    given = () if first else (*in_chip(before), in_hbm(y0))
    return pl.pallas_call(
        functools.partial(leaf_kernel, first, last),
        grid=(steps,),
        in_specs=[
            SMEM,
            pl.BlockSpec((height, LEAF), lambda i: (i + steps * step, 0)),
            pl.BlockSpec((3, height, RANK), lambda i: (0, i + steps * step, 0)),
            VMEM,
            VMEM,
        ]
        + ([] if first else [VMEM, ANY]),
        out_specs=[pl.BlockSpec((height, COLS), lambda i: (i + steps * step, 0))] + [VMEM] * len(ends),
        out_shape=[far(LEAF, COLS)] + ends,
        scratch_shapes=[pltpu.VMEM((3 * RANK, COLS), jnp.float32)] if last else [],
        input_output_aliases={} if first else {6: 0},
        compiler_params=params(16),
        cost_estimate=cost(6 * LEAF // parts * COLS * (LEAF + 3 * RANK), 2 << 20),
    )(place, in_hbm(leaf), in_hbm(right), *in_chip(*halves), *given)


def ready_kernel(place, left, core3, core2, core1, hi, lo, out3, out2, out1):
    for k in range(3):
        hi[:, k * RANK : (k + 1) * RANK], lo[:, k * RANK : (k + 1) * RANK] = split(left[k])

    @pl.when(pl.program_id(0) == 0)
    def _():
        out3[...], out2[...], out1[...] = core3[0], core2[0], core1[0]


def ready_stage(place, left, cores):
    steps = 4
    height = LEAF // steps
    node = (1, 2 * RANK, 2 * RANK)
    return pl.pallas_call(
        ready_kernel,
        grid_spec=pltpu.PrefetchScalarGridSpec(
            num_scalar_prefetch=1,
            grid=(steps,),
            in_specs=[
                pl.BlockSpec((3, height, RANK), lambda i, w: (0, i, 0)),
                pl.BlockSpec(node, lambda i, w: (w[0], 0, 0)),
                pl.BlockSpec(node, lambda i, w: (w[1], 0, 0)),
                pl.BlockSpec(node, lambda i, w: (0, 0, 0)),
            ],
            out_specs=[pl.BlockSpec((height, 3 * RANK), lambda i, w: (i, 0))] * 2
            + [pl.BlockSpec(node[1:], lambda i, w: (0, 0))] * 3,
        ),
        out_shape=[bf16(LEAF, 3 * RANK)] * 2 + [f32(*node[1:])] * 3,
        compiler_params=params(8),
        cost_estimate=cost(1 << 22, 3 << 20),
        name="ready_stage",
    )(place, in_hbm(left), in_hbm(cores), in_hbm(cores), in_hbm(cores))


def node3_kernel(place, own, oth, core, gram, c_own, rest):
    second = place[0] == 1
    a, b = own[...], oth[...]
    p_own, p_oth = a[:, 2 * RANK :], b[:, 2 * RANK :]
    p = jnp.concatenate([jnp.where(second, p_oth, p_own), jnp.where(second, p_own, p_oth)], axis=1)
    c = dot3(split(p), split(core[...]), NT)
    first_c, second_c = c[:, :RANK], c[:, RANK:]
    mine = jnp.where(second, second_c, first_c)
    other = jnp.where(second, first_c, second_c)
    c_own[...] = mine
    fix = dot3(split(jnp.concatenate([mine, other], axis=1)), split(gram[...]), NN)
    rest[...] = a[:, : 2 * RANK] + b[:, : 2 * RANK] - fix


def node2_kernel(place, own, oth, core, gram_own, gram_oth, c_own, rest):
    second = place[0] == 1
    a, b = own[...], oth[...]
    p_own, p_oth = a[:, RANK:], b[:, RANK:]
    p = jnp.concatenate([jnp.where(second, p_oth, p_own), jnp.where(second, p_own, p_oth)], axis=1)
    c = dot3(split(p), split(core[...]), NT)
    mine = jnp.where(second, c[:, RANK:], c[:, :RANK])
    other = jnp.where(second, c[:, :RANK], c[:, RANK:])
    c_own[...] = mine
    gram = jnp.concatenate([gram_own[...], gram_oth[...]], axis=0)
    fix = dot3(split(jnp.concatenate([mine, other], axis=1)), split(gram), NN)
    rest[...] = a[:, :RANK] + b[:, :RANK] - fix


def node1_kernel(place, own, oth, core, c2, c3, out):
    second = place[0] == 1
    a, b = own[...], oth[...]
    p = jnp.concatenate([jnp.where(second, b, a), jnp.where(second, a, b)], axis=1)
    c = dot3(split(p), split(core[...]), NT)
    mine = jnp.where(second, c[:, RANK:], c[:, :RANK])
    out[...] = jnp.concatenate([mine, c2[...], c3[...]], axis=1)


def in_vmem(kernel, shapes, place, *arrays):
    return pl.pallas_call(
        kernel,
        in_specs=[SMEM] + [VMEM] * len(arrays),
        out_specs=[VMEM] * len(shapes),
        out_shape=[f32(*shape) for shape in shapes],
        compiler_params=params(4),
        cost_estimate=cost(1 << 20, 1 << 18),
    )(place, *in_chip(*arrays))


def halves_kernel(place, a, b, send, keep):
    n = send.shape[0]
    own = pl.ds(pl.multiple_of(place[0] * n, n), n)
    oth = pl.ds(pl.multiple_of((1 - place[0]) * n, n), n)
    send[...] = a[oth, :] + b[oth, :]
    keep[...] = a[own, :] + b[own, :]


def halves(place, a, b):
    shape = (a.shape[0] // 2, a.shape[1])
    return in_vmem(halves_kernel, [shape, shape], place, a, b)


def add_kernel(place, a, b, out):
    out[...] = a[...] + b[...]


def add(place, a, b):
    return in_vmem(add_kernel, [a.shape], place, a, b)[0]


def beside_kernel(place, a, b, out):
    n = a.shape[1]
    out[:, :n] = a[...]
    out[:, n:] = b[...]


def ordered_kernel(place, mine, other, out):
    n = mine.shape[0]
    out[pl.ds(pl.multiple_of(place[0] * n, n), n), :] = mine[...]
    out[pl.ds(pl.multiple_of((1 - place[0]) * n, n), n), :] = other[...]


def ordered(place, mine, other):
    return in_vmem(ordered_kernel, [(2 * mine.shape[0], mine.shape[1])], place, mine, other)[0]


def grams_kernel(place, mine, other, gram3, gram2):
    n = mine.shape[0]
    for bit, part in ((place[0], mine), (1 - place[0], other)):
        start = pl.multiple_of(bit * n, n)
        gram3[pl.ds(start, n), :] = part[:, : 2 * RANK]
        gram3[pl.ds(start + RANK, n), :] = part[:, 3 * RANK : 5 * RANK]
        gram2[pl.ds(start, n), :] = part[:, 2 * RANK : 3 * RANK] + part[:, 5 * RANK :]


def correct_kernel(where, y0, l_hi, l_lo, c, *rest):
    out = rest[-1]
    n = y0.shape[0]
    rows = pl.ds(pl.multiple_of(pl.program_id(0) * n, n), n)
    out[...] = y0[...] - dot3((l_hi[rows, :], l_lo[rows, :]), split(c[...]), NT)


def correct(where, y0, left, c, into=None):
    steps = 2
    height = LEAF // steps
    given = () if into is None else (into,)
    return pl.pallas_call(
        correct_kernel,
        grid_spec=pltpu.PrefetchScalarGridSpec(
            num_scalar_prefetch=1,
            grid=(steps,),
            in_specs=[pl.BlockSpec((height, RANK), lambda i, w: (i, w[0]))] + [VMEM] * 3 + [ANY] * len(given),
            out_specs=pl.BlockSpec((height, RANK), lambda i, w: (i, w[0])),
        ),
        out_shape=far(LEAF, COLS),
        input_output_aliases={5: 0} if given else {},
        compiler_params=params(8),
        cost_estimate=cost(6 * LEAF * 3 * RANK * RANK, 1 << 20),
    )(where, in_hbm(y0), *in_chip(*left, c), *given)


def swapped(x, mask, axis="rows"):
    size = lax.axis_size(axis)
    return lax.ppermute(x, axis, [(i, i ^ mask) for i in range(size)])


def on_device(rhs, leaf_inverse, basis_left, basis_right, cores):
    position = lax.axis_index("rows").astype(jnp.int32)
    x = lax.axis_index("rhs").astype(jnp.int32)
    core, z, y = position & 1, (position >> 1) & 7, position >> 4
    sib, parity, half = z >> 2, y & 1, y >> 1
    low, high = (z & 1) ^ sib, ((z >> 1) & 1) ^ sib
    scalar = lambda v: v.reshape(1)

    gram, *rhs_halves = open_stage(scalar(x), basis_right, basis_left, rhs)
    parts = 2
    y0, *q = leaf_part(0, parts, scalar(core), leaf_inverse, basis_right, rhs_halves)
    for step in range(1, parts):
        y0, *q = leaf_part(step, parts, scalar(core), leaf_inverse, basis_right, rhs_halves, q[0], y0)
    keep, send = q
    got = swapped(send, 1)

    gram = add(scalar(x), gram, swapped(gram, 1))
    gram = add(scalar(x), gram, swapped(gram, 2))
    gram = add(scalar(x), gram, swapped(gram, 4))
    gram_sib = swapped(gram, 14)
    (sums,) = in_vmem(beside_kernel, [(QUARTER, 6 * RANK)], scalar(x), gram, gram_sib)
    sums = ordered(scalar(x & 1), sums, swapped(sums, 1, "rhs"))
    gram3, gram2 = in_vmem(
        grams_kernel,
        [(2 * RANK, 2 * RANK), (RANK, RANK)],
        scalar(x >> 1),
        sums,
        swapped(sums, 2, "rhs"),
    )
    gram2_oth = swapped(gram2, 16)

    send, keep = halves(scalar(low), keep, got)
    send, keep = halves(scalar(high), keep, swapped(send, 2))
    own = add(scalar(x), keep, swapped(send, 4))
    oth = swapped(own, 14)

    l_hi, l_lo, core3, core2, core1 = ready_stage(jnp.stack([3 + y, 1 + half]), basis_left, cores)

    chunk = (COLS // 8, RANK)
    c3, rest = in_vmem(
        node3_kernel, [chunk, (COLS // 8, 2 * RANK)], scalar(sib), own, oth, core3, gram3
    )
    rest_oth = swapped(rest, 16)
    c2, rest1 = in_vmem(
        node2_kernel, [chunk, chunk], scalar(parity), rest, rest_oth, core2, gram2, gram2_oth
    )
    rest1_oth = swapped(rest1, 32)
    (c,) = in_vmem(
        node1_kernel, [(COLS // 8, 3 * RANK)], scalar(half), rest1, rest1_oth, core1, c2, c3
    )
    c = ordered(scalar(high), c, swapped(c, 4))
    c_low = swapped(c, 2)
    c_core = swapped(c, 1)
    c_core_low = swapped(c_low, 1)

    left = l_hi, l_lo
    out = correct(scalar(2 * core + low), y0, left, c)
    out = correct(scalar(2 * (1 - core) + low), y0, left, c_core, out)
    out = correct(scalar(2 * core + 1 - low), y0, left, c_low, out)
    return correct(scalar(2 * (1 - core) + 1 - low), y0, left, c_core_low, out)


def solution(mesh):
    placed = (P("rows", "rhs"), P("rows", None), P(None, "rows", None), P(None, "rows", None), P())
    return jax.shard_map(
        on_device, mesh=mesh, in_specs=placed, out_specs=P("rows", "rhs"), check_vma=False
    )
```

time: 187 us -> 86.5 us (0.46)
  the two profiles are of different devices: /device:TPU:4 before, /device:TPU:1 now
where the time goes in v1:
time: 86.5 us; the launch traced here: 86.3 us
  starting transfers between devices  43.3 us (50%)
  Pallas kernels  29.1 us (34%)
  waiting for transfers between devices  13.6 us (16%)
    ppermute x17, starting transfers between devices, swapped(): return lax.ppermute(x, axis, [(i, i ^ mask) for i in range(size)])  43.3 us
    ppermute x17, waiting for transfers between devices, swapped(): return lax.ppermute(x, axis, [(i, i ^ mask) for i in range(size)])  13.6 us
    pallas_call x2, Pallas kernels, leaf_part(): pl.pallas_call(functools.partial(leaf_kernel, first, last), grid=(steps,)...  10.8 us
    pallas_call x4, Pallas kernels, correct(): pl.pallas_call(correct_kernel, grid_spec=pltpu.PrefetchScalarGridSpec(num...  10.5 us
    pallas_call x1, Pallas kernels, open_stage(): pl.pallas_call(open_kernel, grid=(steps,), in_specs=[SMEM, pl.BlockSpec((...  3.32 us
    pallas_call x1, Pallas kernels, ready_stage(): pl.pallas_call(ready_kernel, grid_spec=pltpu.PrefetchScalarGridSpec(num_s...  3.17 us
  transfers between devices with their start and end apart: 17, of which 8 were waited for; matrix products, arithmetic and copies ran while one was open for 0% of the time, Pallas kernels for 13%

profile of v1, /device:TPU:1, one launch (start us, length us, event | category | flops | bytes accessed | tf_op | source)
XLA Modules:
  0.0 86.3 jit_solution(17973746836973350340)
XLA Ops:
  0.0 3.3 %open_stage.1 = (f32[32,384]{1,0:T(8,128)S(1)}, bf16[1024,512]{1,0:T(8,128)(2,1)S(1)}, bf16[1024,512]{1,0:T(8,128)(2,1)S(1)}) custom-call(s32[1]{0:T(128)} %bitcast.2.place, f32[3,1024,128]{2,1,0:T(8,128)} %right.5, f32[3,1024,128]{2,1,0:T(8,128)} %left.1, f32[3,1024,128]{2,1,0:T(8,128)} %left.1, f32[1024,512]{1,0:T(8,128)} %rhs.1), custom_call_target="tpu_custom_call" | custom-call | flops 301989888 | bytes 4194304 | tf_op jit(solution)/shard_map/open_stage/pallas_call | solution.py:85
  3.3 5.2 %shard_map.55 = (f32[1024,512]{1,0:T(8,128)}, f32[384,512]{1,0:T(8,128)S(1)}) custom-call(s32[1]{0:T(128)} %bitcast.1.place, f32[1024,1024]{1,0:T(8,128)} %leaf.3, f32[3,1024,128]{2,1,0:T(8,128)} %right.5, bf16[1024,512]{1,0:T(8,128)(2,1)S(1)} %get-tuple-element.28.x_hi, bf16[1024,512]{1,0:T(8,128)(2,1)S(1)} %get-tuple-element.29.x_lo), custom_call_target="tpu_custom_call" | custom-call | flops 2214592512 | bytes 2097152 | tf_op jit(solution)/shard_map/pallas_call | solution.py:150
  8.6 5.6 %shard_map.56 = (f32[1024,512]{1,0:T(8,128)}, f32[256,384]{1,0:T(8,128)S(1)}, f32[256,384]{1,0:T(8,128)S(1)}) custom-call(s32[1]{0:T(128)} %bitcast.1.place, f32[1024,1024]{1,0:T(8,128)} %leaf.3, f32[3,1024,128]{2,1,0:T(8,128)} %right.5, bf16[1024,512]{1,0:T(8,128)(2,1)S(1)} %get-tuple-element.28.x_hi, ...), custom_call_target="tpu_custom_call", output_to_operand_aliasing={{0}: (6, {})} | custom-call | flops 2214592512 | bytes 2097152 | tf_op jit(solution)/shard_map/pallas_call | solution.py:150
  14.1 3.2 %collective-permute-start = (f32[256,384]{1,0:T(8,128)S(1)}, f32[256,384]{1,0:T(8,128)S(1)}, u32[]{:S(2)}, u32[]{:S(2)}) collective-permute-start(f32[256,384]{1,0:T(8,128)S(1)} %get-tuple-element.36), channel_id=1, source_target_pairs={{0,4},{4,0},{8,12},{12,8},{16,20},{20,16},{24,28},{28,24},{32,36},... | collective-permute-start | bytes 1179656 | tf_op jit(solution)/shard_map/ppermute | solution.py:326
  17.3 0.0 collective-permute-start.4
  17.3 1.4 %collective-permute-done.4.b = f32[32,384]{1,0:T(8,128)S(1)} collective-permute-done((f32[32,384]{1,0:T(8,128)S(1)}, f32[32,384]{1,0:T(8,128)S(1)}, u32[]{:S(2)}, u32[]{:S(2)}) %collective-permute-start.4) | collective-permute-done | bytes 49184 | tf_op jit(solution)/shard_map/ppermute | solution.py:326
  18.7 0.0 collective-permute-start.5
  18.8 0.0 collective-permute-done.b
  18.8 1.5 %collective-permute-start.1 = (f32[128,384]{1,0:T(8,128)S(1)}, f32[128,384]{1,0:T(8,128)S(1)}, u32[]{:S(2)}, u32[]{:S(2)}) collective-permute-start(f32[128,384]{1,0:T(8,128)S(1)} %get-tuple-element.38), channel_id=1, source_target_pairs={{0,8},{4,12},{8,0},{12,4},{16,24},{20,28},{24,16},{28,20},{32,40},... | collective-permute-start | bytes 589832 | tf_op jit(solution)/shard_map/ppermute | solution.py:326
  20.4 1.3 %collective-permute-done.5.b = f32[32,384]{1,0:T(8,128)S(1)} collective-permute-done((f32[32,384]{1,0:T(8,128)S(1)}, f32[32,384]{1,0:T(8,128)S(1)}, u32[]{:S(2)}, u32[]{:S(2)}) %collective-permute-start.5) | collective-permute-done | bytes 49184 | tf_op jit(solution)/shard_map/ppermute | solution.py:326
  21.7 1.5 %collective-permute-start.6 = (f32[32,384]{1,0:T(8,128)S(1)}, f32[32,384]{1,0:T(8,128)S(1)}, u32[]{:S(2)}, u32[]{:S(2)}) collective-permute-start(f32[32,384]{1,0:T(8,128)S(1)} %shard_map.61.a), channel_id=1, source_target_pairs={{0,16},{4,20},{8,24},{12,28},{16,0},{20,4},{24,8},{28,12},{32,48},... | collective-permute-start | bytes 147464 | tf_op jit(solution)/shard_map/ppermute | solution.py:326
  23.2 2.5 %collective-permute-done.6.b = f32[32,384]{1,0:T(8,128)S(1)} collective-permute-done((f32[32,384]{1,0:T(8,128)S(1)}, f32[32,384]{1,0:T(8,128)S(1)}, u32[]{:S(2)}, u32[]{:S(2)}) %collective-permute-start.6) | collective-permute-done | bytes 49184 | tf_op jit(solution)/shard_map/ppermute | solution.py:326
  25.7 4.2 %collective-permute-start.7 = (f32[32,384]{1,0:T(8,128)S(1)}, f32[32,384]{1,0:T(8,128)S(1)}, u32[]{:S(2)}, u32[]{:S(2)}) collective-permute-start(f32[32,384]{1,0:T(8,128)S(1)} %shard_map.62.a), channel_id=1, source_target_pairs={{0,56},{4,60},{8,48},{12,52},{16,40},{20,44},{24,32},{28,36},{32,2... | collective-permute-start | bytes 147464 | tf_op jit(solution)/shard_map/ppermute | solution.py:326
  29.9 1.5 %collective-permute-done.7.b = f32[32,384]{1,0:T(8,128)S(1)} collective-permute-done((f32[32,384]{1,0:T(8,128)S(1)}, f32[32,384]{1,0:T(8,128)S(1)}, u32[]{:S(2)}, u32[]{:S(2)}) %collective-permute-start.7) | collective-permute-done | bytes 49184 | tf_op jit(solution)/shard_map/ppermute | solution.py:326
  31.4 1.3 %collective-permute-start.8 = (f32[32,768]{1,0:T(8,128)S(1)}, f32[32,768]{1,0:T(8,128)S(1)}, u32[]{:S(2)}, u32[]{:S(2)}) collective-permute-start(f32[32,768]{1,0:T(8,128)S(1)} %shard_map.63.mine), channel_id=1, source_target_pairs={{0,1},{1,0},{2,3},{3,2},{4,5},{5,4},{6,7},{7,6},{8,9},{9,8},{10,11... | collective-permute-start | bytes 294920 | tf_op jit(solution)/shard_map/ppermute | solution.py:326
  32.7 0.0 collective-permute-done.1.b
  32.7 3.9 %collective-permute-start.2 = (f32[64,384]{1,0:T(8,128)S(1)}, f32[64,384]{1,0:T(8,128)S(1)}, u32[]{:S(2)}, u32[]{:S(2)}) collective-permute-start(f32[64,384]{1,0:T(8,128)S(1)} %get-tuple-element.40), channel_id=1, source_target_pairs={{0,16},{4,20},{8,24},{12,28},{16,0},{20,4},{24,8},{28,12},{32,48},... | collective-permute-start | bytes 294920 | tf_op jit(solution)/shard_map/ppermute | solution.py:326
  36.6 0.0 collective-permute-done.8.other
  36.6 2.5 %collective-permute-start.9 = (f32[64,768]{1,0:T(8,128)S(1)}, f32[64,768]{1,0:T(8,128)S(1)}, u32[]{:S(2)}, u32[]{:S(2)}) collective-permute-start(f32[64,768]{1,0:T(8,128)S(1)} %shard_map.64.mine), channel_id=1, source_target_pairs={{0,2},{1,3},{2,0},{3,1},{4,6},{5,7},{6,4},{7,5},{8,10},{9,11},{10,... | collective-permute-start | bytes 589832 | tf_op jit(solution)/shard_map/ppermute | solution.py:326
  39.1 0.0 collective-permute-done.2.b
  39.2 3.7 %collective-permute-start.3 = (f32[64,384]{1,0:T(8,128)S(1)}, f32[64,384]{1,0:T(8,128)S(1)}, u32[]{:S(2)}, u32[]{:S(2)}) collective-permute-start(f32[64,384]{1,0:T(8,128)S(1)} %shard_map.59.own), channel_id=1, source_target_pairs={{0,56},{4,60},{8,48},{12,52},{16,40},{20,44},{24,32},{28,36},{32,2... | collective-permute-start | bytes 294920 | tf_op jit(solution)/shard_map/ppermute | solution.py:326
  42.8 0.1 pad_add_fusion.place
  42.9 3.2 %ready_stage.1 = (bf16[1024,384]{1,0:T(8,128)(2,1)S(1)}, bf16[1024,384]{1,0:T(8,128)(2,1)S(1)}, f32[256,256]{1,0:T(8,128)S(1)}, f32[256,256]{1,0:T(8,128)S(1)}, f32[256,256]{1,0:T(8,128)S(1)}) custom-call(s32[2]{0:T(128)S(1)} %pad_add_fusion.place, f32[3,1024,128]{2,1,0:T(8,128)} %left.1, f32[7,256,256]{2,1,0:T(8,128)} %core1.1, f32[7,256,256]{2,1,0:T(8,128)} %core1.1, ...), custom_call_target="tpu_custom_call" | custom-call | flops 4194304 | bytes 3145728 | tf_op jit(solution)/shard_map/ready_stage/pallas_call | solution.py:183
  46.1 0.0 collective-permute-done.9.other
  46.1 1.4 %collective-permute-start.11 = (f32[128,128]{1,0:T(8,128)S(1)}, f32[128,128]{1,0:T(8,128)S(1)}, u32[]{:S(2)}, u32[]{:S(2)}) collective-permute-start(f32[128,128]{1,0:T(8,128)S(1)} %get-tuple-element.46.gram_own), channel_id=1, source_target_pairs={{0,64},{4,68},{8,72},{12,76},{16,80},{20,84},{24,88},{28,92},{32,9... | collective-permute-start | bytes 196616 | tf_op jit(solution)/shard_map/ppermute | solution.py:326
  47.5 0.0 collective-permute-done.3.oth
  47.5 0.4 shard_map.66
  47.9 0.3 collective-permute-start.10
  48.2 1.1 %collective-permute-done.11.gram_oth = f32[128,128]{1,0:T(8,128)S(1)} collective-permute-done((f32[128,128]{1,0:T(8,128)S(1)}, f32[128,128]{1,0:T(8,128)S(1)}, u32[]{:S(2)}, u32[]{:S(2)}) %collective-permute-start.11) | collective-permute-done | bytes 65568 | tf_op jit(solution)/shard_map/ppermute | solution.py:326
  49.3 2.1 %collective-permute-done.10.oth = f32[64,256]{1,0:T(8,128)S(1)} collective-permute-done((f32[64,256]{1,0:T(8,128)S(1)}, f32[64,256]{1,0:T(8,128)S(1)}, u32[]{:S(2)}, u32[]{:S(2)}) %collective-permute-start.10) | collective-permute-done | bytes 65568 | tf_op jit(solution)/shard_map/ppermute | solution.py:326
  51.4 0.4 shard_map.67
  51.9 2.7 %collective-permute-start.12 = (f32[64,128]{1,0:T(8,128)S(1)}, f32[64,128]{1,0:T(8,128)S(1)}, u32[]{:S(2)}, u32[]{:S(2)}) collective-permute-start(f32[64,128]{1,0:T(8,128)S(1)} %get-tuple-element.47.own), channel_id=1, source_target_pairs={{0,128},{4,132},{8,136},{12,140},{16,144},{20,148},{24,152},{28,15... | collective-permute-start | bytes 98312 | tf_op jit(solution)/shard_map/ppermute | solution.py:326
  54.6 1.7 %collective-permute-done.12.oth = f32[64,128]{1,0:T(8,128)S(1)} collective-permute-done((f32[64,128]{1,0:T(8,128)S(1)}, f32[64,128]{1,0:T(8,128)S(1)}, u32[]{:S(2)}, u32[]{:S(2)}) %collective-permute-start.12) | collective-permute-done | bytes 32800 | tf_op jit(solution)/shard_map/ppermute | solution.py:326
  56.2 0.3 shard_map.68.mine
  56.5 3.4 %collective-permute-start.13 = (f32[64,384]{1,0:T(8,128)S(1)}, f32[64,384]{1,0:T(8,128)S(1)}, u32[]{:S(2)}, u32[]{:S(2)}) collective-permute-start(f32[64,384]{1,0:T(8,128)S(1)} %shard_map.68.mine), channel_id=1, source_target_pairs={{0,16},{4,20},{8,24},{12,28},{16,0},{20,4},{24,8},{28,12},{32,48},... | collective-permute-start | bytes 294920 | tf_op jit(solution)/shard_map/ppermute | solution.py:326
  59.9 2.0 %collective-permute-done.13.other = f32[64,384]{1,0:T(8,128)S(1)} collective-permute-done((f32[64,384]{1,0:T(8,128)S(1)}, f32[64,384]{1,0:T(8,128)S(1)}, u32[]{:S(2)}, u32[]{:S(2)}) %collective-permute-start.13) | collective-permute-done | bytes 98336 | tf_op jit(solution)/shard_map/ppermute | solution.py:326
  61.9 2.0 %collective-permute-start.14 = (f32[128,384]{1,0:T(8,128)S(1)}, f32[128,384]{1,0:T(8,128)S(1)}, u32[]{:S(2)}, u32[]{:S(2)}) collective-permute-start(f32[128,384]{1,0:T(8,128)S(1)} %shard_map.69.c), channel_id=1, source_target_pairs={{0,8},{4,12},{8,0},{12,4},{16,24},{20,28},{24,16},{28,20},{32,40},... | collective-permute-start | bytes 589832 | tf_op jit(solution)/shard_map/ppermute | solution.py:326
  63.9 8.2 %collective-permute-start.16 = (f32[128,384]{1,0:T(8,128)S(1)}, f32[128,384]{1,0:T(8,128)S(1)}, u32[]{:S(2)}, u32[]{:S(2)}) collective-permute-start(f32[128,384]{1,0:T(8,128)S(1)} %shard_map.69.c), channel_id=1, source_target_pairs={{0,4},{4,0},{8,12},{12,8},{16,20},{20,16},{24,28},{28,24},{32,36},... | collective-permute-start | bytes 589832 | tf_op jit(solution)/shard_map/ppermute | solution.py:326
  72.1 0.0 collective-permute-done.14.c
  72.1 3.6 %collective-permute-start.15 = (f32[128,384]{1,0:T(8,128)S(1)}, f32[128,384]{1,0:T(8,128)S(1)}, u32[]{:S(2)}, u32[]{:S(2)}) collective-permute-start(f32[128,384]{1,0:T(8,128)S(1)} %collective-permute-done.14.c), channel_id=1, source_target_pairs={{0,4},{4,0},{8,12},{12,8},{16,20},{20,16},{24,28},{28,24},{32,36},... | collective-permute-start | bytes 589832 | tf_op jit(solution)/shard_map/ppermute | solution.py:326
  75.8 2.6 %shard_map.70.rest_0_ = f32[1024,512]{1,0:T(8,128)} custom-call(s32[1]{0:T(128)} %bitcast.14.where, f32[1024,512]{1,0:T(8,128)} %get-tuple-element.32.y0, bf16[1024,384]{1,0:T(8,128)(2,1)S(1)} %get-tuple-element.33.l_hi, bf16[1024,384]{1,0:T(8,128)(2,1)S(1)} %get-tuple-element.34.l_lo, f32[128,384]{1,0:T(8,128)S(1)} %shard_map.69.c), custom_call_target="tpu_custom_call" | custom-call | flops 301989888 | bytes 1048576 | tf_op jit(solution)/shard_map/pallas_call | solution.py:309
  78.4 0.0 collective-permute-done.16.c
  78.4 2.6 %shard_map.71.rest_0_ = f32[1024,512]{1,0:T(8,128)} custom-call(s32[1]{0:T(128)} %bitcast.13.where, f32[1024,512]{1,0:T(8,128)} %get-tuple-element.32.y0, bf16[1024,384]{1,0:T(8,128)(2,1)S(1)} %get-tuple-element.33.l_hi, bf16[1024,384]{1,0:T(8,128)(2,1)S(1)} %get-tuple-element.34.l_lo, ...), custom_call_target="tpu_custom_call", output_to_operand_aliasing={{}: (5, {})} | custom-call | flops 301989888 | bytes 1048576 | tf_op jit(solution)/shard_map/pallas_call | solution.py:309
  81.0 2.6 %shard_map.72.rest_0_ = f32[1024,512]{1,0:T(8,128)} custom-call(s32[1]{0:T(128)} %bitcast.12.where, f32[1024,512]{1,0:T(8,128)} %get-tuple-element.32.y0, bf16[1024,384]{1,0:T(8,128)(2,1)S(1)} %get-tuple-element.33.l_hi, bf16[1024,384]{1,0:T(8,128)(2,1)S(1)} %get-tuple-element.34.l_lo, ...), custom_call_target="tpu_custom_call", output_to_operand_aliasing={{}: (5, {})} | custom-call | flops 301989888 | bytes 1048576 | tf_op jit(solution)/shard_map/pallas_call | solution.py:309
  83.7 0.0 collective-permute-done.15.c
  83.7 2.6 %shard_map.73 = f32[1024,512]{1,0:T(8,128)} custom-call(s32[1]{0:T(128)} %bitcast.where, f32[1024,512]{1,0:T(8,128)} %get-tuple-element.32.y0, bf16[1024,384]{1,0:T(8,128)(2,1)S(1)} %get-tuple-element.33.l_hi, bf16[1024,384]{1,0:T(8,128)(2,1)S(1)} %get-tuple-element.34.l_lo, ...), custom_call_target="tpu_custom_call", output_to_operand_aliasing={{}: (5, {})} | custom-call | flops 301989888 | bytes 1048576 | tf_op jit(solution)/shard_map/pallas_call | solution.py:309
  (10 shorter events, 0.2 us)
Async XLA Ops:
  14.1 4.6 %collective-permute-start = (f32[256,384]{1,0:T(8,128)S(1)}, f32[256,384]{1,0:T(8,128)S(1)}, u32[]{:S(2)}, u32[]{:S(2)}) collective-permute-start(f32[256,384]{1,0:T(8,128)S(1)} %get-tuple-element.36), channel_id=1, source_target_pairs={{0,4},{4,0},{8,12},{12,8},{16,20},{20,16},{24,28},{28,24},{32,36},... | collective-permute-start | bytes 1179656 | tf_op jit(solution)/shard_map/ppermute | solution.py:326
  17.3 1.4 %collective-permute-start.4 = (f32[32,384]{1,0:T(8,128)S(1)}, f32[32,384]{1,0:T(8,128)S(1)}, u32[]{:S(2)}, u32[]{:S(2)}) collective-permute-start(f32[32,384]{1,0:T(8,128)S(1)} %get-tuple-element.42.a), channel_id=1, source_target_pairs={{0,4},{4,0},{8,12},{12,8},{16,20},{20,16},{24,28},{28,24},{32,36},... | collective-permute-start | bytes 147464 | tf_op jit(solution)/shard_map/ppermute | solution.py:326
  18.7 3.0 %collective-permute-start.5 = (f32[32,384]{1,0:T(8,128)S(1)}, f32[32,384]{1,0:T(8,128)S(1)}, u32[]{:S(2)}, u32[]{:S(2)}) collective-permute-start(f32[32,384]{1,0:T(8,128)S(1)} %shard_map.60.a), channel_id=1, source_target_pairs={{0,8},{4,12},{8,0},{12,4},{16,24},{20,28},{24,16},{28,20},{32,40},... | collective-permute-start | bytes 147464 | tf_op jit(solution)/shard_map/ppermute | solution.py:326
  18.8 13.8 %collective-permute-start.1 = (f32[128,384]{1,0:T(8,128)S(1)}, f32[128,384]{1,0:T(8,128)S(1)}, u32[]{:S(2)}, u32[]{:S(2)}) collective-permute-start(f32[128,384]{1,0:T(8,128)S(1)} %get-tuple-element.38), channel_id=1, source_target_pairs={{0,8},{4,12},{8,0},{12,4},{16,24},{20,28},{24,16},{28,20},{32,40},... | collective-permute-start | bytes 589832 | tf_op jit(solution)/shard_map/ppermute | solution.py:326
  21.7 4.0 %collective-permute-start.6 = (f32[32,384]{1,0:T(8,128)S(1)}, f32[32,384]{1,0:T(8,128)S(1)}, u32[]{:S(2)}, u32[]{:S(2)}) collective-permute-start(f32[32,384]{1,0:T(8,128)S(1)} %shard_map.61.a), channel_id=1, source_target_pairs={{0,16},{4,20},{8,24},{12,28},{16,0},{20,4},{24,8},{28,12},{32,48},... | collective-permute-start | bytes 147464 | tf_op jit(solution)/shard_map/ppermute | solution.py:326
  25.7 5.6 %collective-permute-start.7 = (f32[32,384]{1,0:T(8,128)S(1)}, f32[32,384]{1,0:T(8,128)S(1)}, u32[]{:S(2)}, u32[]{:S(2)}) collective-permute-start(f32[32,384]{1,0:T(8,128)S(1)} %shard_map.62.a), channel_id=1, source_target_pairs={{0,56},{4,60},{8,48},{12,52},{16,40},{20,44},{24,32},{28,36},{32,2... | collective-permute-start | bytes 147464 | tf_op jit(solution)/shard_map/ppermute | solution.py:326
  31.4 5.2 %collective-permute-start.8 = (f32[32,768]{1,0:T(8,128)S(1)}, f32[32,768]{1,0:T(8,128)S(1)}, u32[]{:S(2)}, u32[]{:S(2)}) collective-permute-start(f32[32,768]{1,0:T(8,128)S(1)} %shard_map.63.mine), channel_id=1, source_target_pairs={{0,1},{1,0},{2,3},{3,2},{4,5},{5,4},{6,7},{7,6},{8,9},{9,8},{10,11... | collective-permute-start | bytes 294920 | tf_op jit(solution)/shard_map/ppermute | solution.py:326
  32.7 6.4 %collective-permute-start.2 = (f32[64,384]{1,0:T(8,128)S(1)}, f32[64,384]{1,0:T(8,128)S(1)}, u32[]{:S(2)}, u32[]{:S(2)}) collective-permute-start(f32[64,384]{1,0:T(8,128)S(1)} %get-tuple-element.40), channel_id=1, source_target_pairs={{0,16},{4,20},{8,24},{12,28},{16,0},{20,4},{24,8},{28,12},{32,48},... | collective-permute-start | bytes 294920 | tf_op jit(solution)/shard_map/ppermute | solution.py:326
  36.6 9.5 %collective-permute-start.9 = (f32[64,768]{1,0:T(8,128)S(1)}, f32[64,768]{1,0:T(8,128)S(1)}, u32[]{:S(2)}, u32[]{:S(2)}) collective-permute-start(f32[64,768]{1,0:T(8,128)S(1)} %shard_map.64.mine), channel_id=1, source_target_pairs={{0,2},{1,3},{2,0},{3,1},{4,6},{5,7},{6,4},{7,5},{8,10},{9,11},{10,... | collective-permute-start | bytes 589832 | tf_op jit(solution)/shard_map/ppermute | solution.py:326
  39.2 8.3 %collective-permute-start.3 = (f32[64,384]{1,0:T(8,128)S(1)}, f32[64,384]{1,0:T(8,128)S(1)}, u32[]{:S(2)}, u32[]{:S(2)}) collective-permute-start(f32[64,384]{1,0:T(8,128)S(1)} %shard_map.59.own), channel_id=1, source_target_pairs={{0,56},{4,60},{8,48},{12,52},{16,40},{20,44},{24,32},{28,36},{32,2... | collective-permute-start | bytes 294920 | tf_op jit(solution)/shard_map/ppermute | solution.py:326
  46.1 3.2 %collective-permute-start.11 = (f32[128,128]{1,0:T(8,128)S(1)}, f32[128,128]{1,0:T(8,128)S(1)}, u32[]{:S(2)}, u32[]{:S(2)}) collective-permute-start(f32[128,128]{1,0:T(8,128)S(1)} %get-tuple-element.46.gram_own), channel_id=1, source_target_pairs={{0,64},{4,68},{8,72},{12,76},{16,80},{20,84},{24,88},{28,92},{32,9... | collective-permute-start | bytes 196616 | tf_op jit(solution)/shard_map/ppermute | solution.py:326
  47.9 3.5 %collective-permute-start.10 = (f32[64,256]{1,0:T(8,128)S(1)}, f32[64,256]{1,0:T(8,128)S(1)}, u32[]{:S(2)}, u32[]{:S(2)}) collective-permute-start(f32[64,256]{1,0:T(8,128)S(1)} %get-tuple-element.44.own), channel_id=1, source_target_pairs={{0,64},{4,68},{8,72},{12,76},{16,80},{20,84},{24,88},{28,92},{32,9... | collective-permute-start | bytes 196616 | tf_op jit(solution)/shard_map/ppermute | solution.py:326
  51.9 4.4 %collective-permute-start.12 = (f32[64,128]{1,0:T(8,128)S(1)}, f32[64,128]{1,0:T(8,128)S(1)}, u32[]{:S(2)}, u32[]{:S(2)}) collective-permute-start(f32[64,128]{1,0:T(8,128)S(1)} %get-tuple-element.47.own), channel_id=1, source_target_pairs={{0,128},{4,132},{8,136},{12,140},{16,144},{20,148},{24,152},{28,15... | collective-permute-start | bytes 98312 | tf_op jit(solution)/shard_map/ppermute | solution.py:326
  56.5 5.4 %collective-permute-start.13 = (f32[64,384]{1,0:T(8,128)S(1)}, f32[64,384]{1,0:T(8,128)S(1)}, u32[]{:S(2)}, u32[]{:S(2)}) collective-permute-start(f32[64,384]{1,0:T(8,128)S(1)} %shard_map.68.mine), channel_id=1, source_target_pairs={{0,16},{4,20},{8,24},{12,28},{16,0},{20,4},{24,8},{28,12},{32,48},... | collective-permute-start | bytes 294920 | tf_op jit(solution)/shard_map/ppermute | solution.py:326
  61.9 10.2 %collective-permute-start.14 = (f32[128,384]{1,0:T(8,128)S(1)}, f32[128,384]{1,0:T(8,128)S(1)}, u32[]{:S(2)}, u32[]{:S(2)}) collective-permute-start(f32[128,384]{1,0:T(8,128)S(1)} %shard_map.69.c), channel_id=1, source_target_pairs={{0,8},{4,12},{8,0},{12,4},{16,24},{20,28},{24,16},{28,20},{32,40},... | collective-permute-start | bytes 589832 | tf_op jit(solution)/shard_map/ppermute | solution.py:326
  63.9 14.5 %collective-permute-start.16 = (f32[128,384]{1,0:T(8,128)S(1)}, f32[128,384]{1,0:T(8,128)S(1)}, u32[]{:S(2)}, u32[]{:S(2)}) collective-permute-start(f32[128,384]{1,0:T(8,128)S(1)} %shard_map.69.c), channel_id=1, source_target_pairs={{0,4},{4,0},{8,12},{12,8},{16,20},{20,16},{24,28},{28,24},{32,36},... | collective-permute-start | bytes 589832 | tf_op jit(solution)/shard_map/ppermute | solution.py:326
  72.1 11.5 %collective-permute-start.15 = (f32[128,384]{1,0:T(8,128)S(1)}, f32[128,384]{1,0:T(8,128)S(1)}, u32[]{:S(2)}, u32[]{:S(2)}) collective-permute-start(f32[128,384]{1,0:T(8,128)S(1)} %collective-permute-done.14.c), channel_id=1, source_target_pairs={{0,4},{4,0},{8,12},{12,8},{16,20},{20,16},{24,28},{28,24},{32,36},... | collective-permute-start | bytes 589832 | tf_op jit(solution)/shard_map/ppermute | solution.py:326

commit v2 on v1

--- a/solution.py
+++ b/solution.py
@@ -1,5 +1,3 @@
-import functools
-
 import jax
 import jax.numpy as jnp
 from jax import lax
@@ -13,11 +11,14 @@
 LEAF = 1024
 COLS = 512
 QUARTER = RANK // XS
+EIGHTH = QUARTER // 2
+BLOCKS = 128, 128, 256, 256, 256
 NN = (((1,), (0,)), ((), ()))
 NT = (((1,), (1,)), ((), ()))
 VMEM = pl.BlockSpec(memory_space=pltpu.VMEM)
 SMEM = pl.BlockSpec(memory_space=pltpu.SMEM)
 ANY = pl.BlockSpec(memory_space=pl.ANY)
+HBM = pl.BlockSpec(memory_space=pltpu.HBM)
 
 
 def split(a):
@@ -60,11 +61,13 @@
     return pltpu.HBM(shape, jnp.float32)
 
 
-def open_kernel(place, right, left2, left3, rhs, gram, x_hi, x_lo, acc):
+def open_kernel(place, right, left2, left3, rhs, leaf, keep, send, x_hi, x_lo, ahead, acc, sem):
     i = pl.program_id(0)
+    copy = pltpu.make_async_copy(leaf.at[: ahead.shape[0], :], ahead, sem)
 
     @pl.when(i == 0)
     def _():
+        copy.start()
         acc[...] = jnp.zeros_like(acc)
 
     rows = pl.ds(pl.multiple_of(i * rhs.shape[0], rhs.shape[0]), rhs.shape[0])
@@ -76,10 +79,13 @@
 
     @pl.when(i == pl.num_programs(0) - 1)
     def _():
-        gram[...] = acc[pl.ds(pl.multiple_of(place[0] * QUARTER, QUARTER), QUARTER), :]
-
-
-def open_stage(place, right, left, rhs):
+        start = place[0] * QUARTER
+        keep[...] = acc[pl.ds(pl.multiple_of(start + place[1] * EIGHTH, EIGHTH), EIGHTH), :]
+        send[...] = acc[pl.ds(pl.multiple_of(start + (1 - place[1]) * EIGHTH, EIGHTH), EIGHTH), :]
+        copy.wait()
+
+
+def open_stage(place, right, left, rhs, leaf):
     steps = 2
     height = LEAF // steps
     return pl.pallas_call(
@@ -91,80 +97,72 @@
             pl.BlockSpec((1, height, RANK), lambda i: (1, i, 0)),
             pl.BlockSpec((1, height, RANK), lambda i: (2, i, 0)),
             pl.BlockSpec((height, COLS), lambda i: (i, 0)),
+            HBM,
         ],
-        out_specs=[VMEM] * 3,
-        out_shape=[f32(QUARTER, 3 * RANK), bf16(LEAF, COLS), bf16(LEAF, COLS)],
-        scratch_shapes=[pltpu.VMEM((RANK, 3 * RANK), jnp.float32)],
+        out_specs=[VMEM] * 5,
+        out_shape=[f32(EIGHTH, 3 * RANK)] * 2 + [bf16(LEAF, COLS), bf16(LEAF, COLS), f32(BLOCKS[0], LEAF)],
+        scratch_shapes=[pltpu.VMEM((RANK, 3 * RANK), jnp.float32), pltpu.SemaphoreType.DMA],
         compiler_params=params(12),
         cost_estimate=cost(6 * LEAF * RANK * 3 * RANK, 4 << 20),
         name="open_stage",
-    )(place, in_hbm(right), in_hbm(left), in_hbm(left), in_hbm(rhs))
-
-
-def leaf_kernel(first, last, place, leaf, right, x_hi, x_lo, *rest):
-    i = pl.program_id(0)
-    y = dot3(split(leaf[...]), (x_hi[...], x_lo[...]), NN)
-    rt = split(jnp.concatenate([right[0].T, right[1].T, right[2].T], axis=0))
-    part = dot3(rt, split(y), NN)
-    if first:
-        y0, *ends = rest
-    else:
-        before, _, y0, *ends = rest
-    acc = ends[-1]
-    y0[...] = y
-
-    @pl.when(i == 0)
-    def _():
-        acc[...] = part if first else before[...] + part
-
-    @pl.when(i > 0)
-    def _():
-        acc[...] += part
-
-    if not last:
-        return
-    keep, send = ends[:2]
-
-    @pl.when(i == pl.num_programs(0) - 1)
-    def _():
-        q = acc[...]
-        first_half, second_half = q[:, : COLS // 2].T, q[:, COLS // 2 :].T
-
-        @pl.when(place[0] == 0)
-        def _():
-            keep[...] = first_half
-            send[...] = second_half
-
-        @pl.when(place[0] == 1)
-        def _():
-            keep[...] = second_half
-            send[...] = first_half
-
-
-def leaf_part(step, parts, place, leaf, right, halves, before=None, y0=None):
-    first, last = step == 0, step == parts - 1
-    steps = 2
-    height = LEAF // parts // steps
-    ends = [f32(COLS // 2, 3 * RANK)] * 2 if last else [f32(3 * RANK, COLS)]
-    given = () if first else (*in_chip(before), in_hbm(y0))
-    return pl.pallas_call(
-        functools.partial(leaf_kernel, first, last),
-        grid=(steps,),
-        in_specs=[
-            SMEM,
-            pl.BlockSpec((height, LEAF), lambda i: (i + steps * step, 0)),
-            pl.BlockSpec((3, height, RANK), lambda i: (0, i + steps * step, 0)),
-            VMEM,
-            VMEM,
-        ]
-        + ([] if first else [VMEM, ANY]),
-        out_specs=[pl.BlockSpec((height, COLS), lambda i: (i + steps * step, 0))] + [VMEM] * len(ends),
-        out_shape=[far(LEAF, COLS)] + ends,
-        scratch_shapes=[pltpu.VMEM((3 * RANK, COLS), jnp.float32)] if last else [],
-        input_output_aliases={} if first else {6: 0},
-        compiler_params=params(16),
-        cost_estimate=cost(6 * LEAF // parts * COLS * (LEAF + 3 * RANK), 2 << 20),
-    )(place, in_hbm(leaf), in_hbm(right), *in_chip(*halves), *given)
+    )(place, in_hbm(right), in_hbm(left), in_hbm(left), in_hbm(rhs), in_hbm(leaf))
+
+
+def leaf_kernel(place, leaf, right, x_hi, x_lo, ahead, y0, keep, send, blocks, bases, y, acc, sems):
+    count = len(BLOCKS)
+    rows = [slice(sum(BLOCKS[:k]), sum(BLOCKS[: k + 1])) for k in range(count)]
+    loads = [pltpu.make_async_copy(leaf.at[r, :], blocks.at[r, :], sems.at[k]) for k, r in enumerate(rows)]
+    bases_load = pltpu.make_async_copy(right, bases, sems.at[0])
+    stores = [pltpu.make_async_copy(y.at[r, :], y0.at[r, :], sems.at[count + k]) for k, r in enumerate(rows)]
+    loads[1].start()
+    bases_load.start()
+    for load in loads[2:]:
+        load.start()
+    for k, here in enumerate(rows):
+        if k:
+            loads[k].wait()
+        block = blocks[here, :] if k else ahead[...]
+        part = dot3(split(block), (x_hi[...], x_lo[...]), NN)
+        y[here, :] = part
+        stores[k].start()
+        if k == 0:
+            bases_load.wait()
+        rt = split(jnp.concatenate([bases[i, here, :].T for i in range(3)], axis=0))
+        q = dot3(rt, split(part), NN)
+        acc[...] = acc[...] + q if k else q
+    first_half, second_half = acc[:, : COLS // 2].T, acc[:, COLS // 2 :].T
+
+    @pl.when(place[0] == 0)
+    def _():
+        keep[...] = first_half
+        send[...] = second_half
+
+    @pl.when(place[0] == 1)
+    def _():
+        keep[...] = second_half
+        send[...] = first_half
+
+    for store in stores:
+        store.wait()
+
+
+def leaf_stage(place, leaf, right, *arrays):
+    return pl.pallas_call(
+        leaf_kernel,
+        in_specs=[SMEM, HBM, HBM, VMEM, VMEM, VMEM],
+        out_specs=[HBM, VMEM, VMEM],
+        out_shape=[far(LEAF, COLS)] + [f32(COLS // 2, 3 * RANK)] * 2,
+        scratch_shapes=[
+            pltpu.VMEM((LEAF, LEAF), jnp.float32),
+            pltpu.VMEM((3, LEAF, RANK), jnp.float32),
+            pltpu.VMEM((LEAF, COLS), jnp.float32),
+            pltpu.VMEM((3 * RANK, COLS), jnp.float32),
+            pltpu.SemaphoreType.DMA((2 * len(BLOCKS),)),
+        ],
+        compiler_params=params(24),
+        cost_estimate=cost(6 * LEAF * COLS * (LEAF + 3 * RANK), 8 << 20),
+        name="leaf_stage",
+    )(place, in_hbm(leaf), in_hbm(right), *in_chip(*arrays))
 
 
 def ready_kernel(place, left, core3, core2, core1, hi, lo, out3, out2, out1):
@@ -271,9 +269,16 @@
 
 
 def beside_kernel(place, a, b, out):
-    n = a.shape[1]
-    out[:, :n] = a[...]
-    out[:, n:] = b[...]
+    n = 2 * RANK
+    out[:, :n] = a[:, :n]
+    out[:, n : 2 * n] = b[:, :n]
+    out[:, 2 * n :] = a[:, n:] + b[:, n:]
+
+
+def collect_kernel(place, *refs):
+    out = refs[-1]
+    for m, part in enumerate(refs[:-1]):
+        out[pl.ds(pl.multiple_of((place[0] ^ m) * EIGHTH, EIGHTH), EIGHTH), :] = part[...]
 
 
 def ordered_kernel(place, mine, other, out):
@@ -287,38 +292,85 @@
 
 
 def grams_kernel(place, mine, other, gram3, gram2):
-    n = mine.shape[0]
+    n = 2 * RANK
     for bit, part in ((place[0], mine), (1 - place[0], other)):
-        start = pl.multiple_of(bit * n, n)
-        gram3[pl.ds(start, n), :] = part[:, : 2 * RANK]
-        gram3[pl.ds(start + RANK, n), :] = part[:, 3 * RANK : 5 * RANK]
-        gram2[pl.ds(start, n), :] = part[:, 2 * RANK : 3 * RANK] + part[:, 5 * RANK :]
-
-
-def correct_kernel(where, y0, l_hi, l_lo, c, *rest):
-    out = rest[-1]
-    n = y0.shape[0]
-    rows = pl.ds(pl.multiple_of(pl.program_id(0) * n, n), n)
-    out[...] = y0[...] - dot3((l_hi[rows, :], l_lo[rows, :]), split(c[...]), NT)
-
-
-def correct(where, y0, left, c, into=None):
-    steps = 2
-    height = LEAF // steps
-    given = () if into is None else (into,)
-    return pl.pallas_call(
-        correct_kernel,
+        for k in range(XS):
+            here = slice(k * EIGHTH, (k + 1) * EIGHTH)
+            start = pl.multiple_of(k * QUARTER + bit * EIGHTH, EIGHTH)
+            gram3[pl.ds(start, EIGHTH), :] = part[here, :n]
+            gram3[pl.ds(start + RANK, EIGHTH), :] = part[here, n : 2 * n]
+            gram2[pl.ds(start, EIGHTH), :] = part[here, 2 * n :]
+
+
+def early_kernel(where, y0, l_hi, l_lo, c, c_core, columns, out, ahead_a, ahead_b, sems):
+    i = pl.program_id(0)
+    copies = [
+        pltpu.make_async_copy(y0.at[:, pl.ds(pl.multiple_of(where[2 + k] * RANK, RANK), RANK)], ahead, sems.at[k])
+        for k, ahead in enumerate((ahead_a, ahead_b))
+    ]
+
+    @pl.when(i == 0)
+    def _():
+        for copy in copies:
+            copy.start()
+
+    half = out.shape[0]
+    rows = pl.ds(pl.multiple_of(i % 2 * half, half), half)
+    left = l_hi[rows, :], l_lo[rows, :]
+
+    @pl.when(i < 2)
+    def _():
+        out[...] = columns[...] - dot3(left, split(c[...]), NT)
+
+    @pl.when(i >= 2)
+    def _():
+        out[...] = columns[...] - dot3(left, split(c_core[...]), NT)
+
+    @pl.when(i == pl.num_programs(0) - 1)
+    def _():
+        for copy in copies:
+            copy.wait()
+
+
+def late_kernel(where, l_hi, l_lo, c, columns, into, out):
+    half = out.shape[0]
+    rows = pl.ds(pl.multiple_of(pl.program_id(0) * half, half), half)
+    out[...] = columns[rows, :] - dot3((l_hi[rows, :], l_lo[rows, :]), split(c[...]), NT)
+
+
+def early_corrections(where, y0, left, c, c_core):
+    block = pl.BlockSpec((LEAF // 2, RANK), lambda i, w: (i % 2, w[i // 2]))
+    return pl.pallas_call(
+        early_kernel,
         grid_spec=pltpu.PrefetchScalarGridSpec(
             num_scalar_prefetch=1,
-            grid=(steps,),
-            in_specs=[pl.BlockSpec((height, RANK), lambda i, w: (i, w[0]))] + [VMEM] * 3 + [ANY] * len(given),
-            out_specs=pl.BlockSpec((height, RANK), lambda i, w: (i, w[0])),
+            grid=(4,),
+            in_specs=[HBM] + [VMEM] * 4 + [block],
+            out_specs=[block, VMEM, VMEM],
+            scratch_shapes=[pltpu.SemaphoreType.DMA((2,))],
+        ),
+        out_shape=[far(LEAF, COLS)] + [f32(LEAF, RANK)] * 2,
+        compiler_params=params(8),
+        cost_estimate=cost(12 * LEAF * 3 * RANK * RANK, 3 << 20),
+        name="early",
+    )(where, in_hbm(y0), *in_chip(*left, c, c_core), in_hbm(y0))
+
+
+def late_correction(where, left, c, columns, into):
+    block = pl.BlockSpec((LEAF // 2, RANK), lambda i, w: (i, w[0]))
+    return pl.pallas_call(
+        late_kernel,
+        grid_spec=pltpu.PrefetchScalarGridSpec(
+            num_scalar_prefetch=1,
+            grid=(2,),
+            in_specs=[VMEM] * 4 + [ANY],
+            out_specs=block,
         ),
         out_shape=far(LEAF, COLS),
-        input_output_aliases={5: 0} if given else {},
+        input_output_aliases={5: 0},
         compiler_params=params(8),
         cost_estimate=cost(6 * LEAF * 3 * RANK * RANK, 1 << 20),
-    )(where, in_hbm(y0), *in_chip(*left, c), *given)
+    )(where, *in_chip(*left, c, columns), into)
 
 
 def swapped(x, mask, axis="rows"):
@@ -334,27 +386,18 @@
     low, high = (z & 1) ^ sib, ((z >> 1) & 1) ^ sib
     scalar = lambda v: v.reshape(1)
 
-    gram, *rhs_halves = open_stage(scalar(x), basis_right, basis_left, rhs)
-    parts = 2
-    y0, *q = leaf_part(0, parts, scalar(core), leaf_inverse, basis_right, rhs_halves)
-    for step in range(1, parts):
-        y0, *q = leaf_part(step, parts, scalar(core), leaf_inverse, basis_right, rhs_halves, q[0], y0)
-    keep, send = q
+    gram, gram_send, *arrays = open_stage(jnp.stack([x, core]), basis_right, basis_left, rhs, leaf_inverse)
+    y0, keep, send = leaf_stage(scalar(core), leaf_inverse, basis_right, *arrays)
     got = swapped(send, 1)
 
-    gram = add(scalar(x), gram, swapped(gram, 1))
+    gram = add(scalar(x), gram, swapped(gram_send, 1))
     gram = add(scalar(x), gram, swapped(gram, 2))
     gram = add(scalar(x), gram, swapped(gram, 4))
-    gram_sib = swapped(gram, 14)
-    (sums,) = in_vmem(beside_kernel, [(QUARTER, 6 * RANK)], scalar(x), gram, gram_sib)
-    sums = ordered(scalar(x & 1), sums, swapped(sums, 1, "rhs"))
-    gram3, gram2 = in_vmem(
-        grams_kernel,
-        [(2 * RANK, 2 * RANK), (RANK, RANK)],
-        scalar(x >> 1),
-        sums,
-        swapped(sums, 2, "rhs"),
-    )
+    wide = (EIGHTH, 5 * RANK)
+    (sums,) = in_vmem(beside_kernel, [wide], scalar(x), gram, swapped(gram, 14))
+    sums = [sums] + [swapped(sums, m, "rhs") for m in range(1, XS)]
+    (sums,) = in_vmem(collect_kernel, [(XS * wide[0], wide[1])], scalar(x), *sums)
+    gram3, gram2 = in_vmem(grams_kernel, [(2 * RANK, 2 * RANK), (RANK, RANK)], scalar(core), sums, swapped(sums, 1))
     gram2_oth = swapped(gram2, 16)
 
     send, keep = halves(scalar(low), keep, got)
@@ -365,31 +408,23 @@
     l_hi, l_lo, core3, core2, core1 = ready_stage(jnp.stack([3 + y, 1 + half]), basis_left, cores)
 
     chunk = (COLS // 8, RANK)
-    c3, rest = in_vmem(
-        node3_kernel, [chunk, (COLS // 8, 2 * RANK)], scalar(sib), own, oth, core3, gram3
-    )
+    c3, rest = in_vmem(node3_kernel, [chunk, (COLS // 8, 2 * RANK)], scalar(sib), own, oth, core3, gram3)
     rest_oth = swapped(rest, 16)
-    c2, rest1 = in_vmem(
-        node2_kernel, [chunk, chunk], scalar(parity), rest, rest_oth, core2, gram2, gram2_oth
-    )
+    c2, rest1 = in_vmem(node2_kernel, [chunk, chunk], scalar(parity), rest, rest_oth, core2, gram2, gram2_oth)
     rest1_oth = swapped(rest1, 32)
-    (c,) = in_vmem(
-        node1_kernel, [(COLS // 8, 3 * RANK)], scalar(half), rest1, rest1_oth, core1, c2, c3
-    )
+    (c,) = in_vmem(node1_kernel, [(COLS // 8, 3 * RANK)], scalar(half), rest1, rest1_oth, core1, c2, c3)
     c = ordered(scalar(high), c, swapped(c, 4))
     c_low = swapped(c, 2)
     c_core = swapped(c, 1)
     c_core_low = swapped(c_low, 1)
 
     left = l_hi, l_lo
-    out = correct(scalar(2 * core + low), y0, left, c)
-    out = correct(scalar(2 * (1 - core) + low), y0, left, c_core, out)
-    out = correct(scalar(2 * core + 1 - low), y0, left, c_low, out)
-    return correct(scalar(2 * (1 - core) + 1 - low), y0, left, c_core_low, out)
+    order = jnp.stack([2 * core + low, 2 * (1 - core) + low, 2 * core + 1 - low, 2 * (1 - core) + 1 - low])
+    out, ahead_a, ahead_b = early_corrections(order, y0, left, c, c_core)
+    out = late_correction(order[2:3], left, c_low, ahead_a, out)
+    return late_correction(order[3:4], left, c_core_low, ahead_b, out)
 
 
 def solution(mesh):
     placed = (P("rows", "rhs"), P("rows", None), P(None, "rows", None), P(None, "rows", None), P())
-    return jax.shard_map(
-        on_device, mesh=mesh, in_specs=placed, out_specs=P("rows", "rhs"), check_vma=False
-    )
+    return jax.shard_map(on_device, mesh=mesh, in_specs=placed, out_specs=P("rows", "rhs"), check_vma=False)

time: 86.5 us -> 84.3 us (0.975)
  Pallas kernels: 29.1 us -> 23.6 us
  waiting for transfers between devices: 13.6 us -> 17.4 us
    pallas_call x6 -> x4, Pallas kernels: 21.3 us -> 15.8 us  [the longest x1 7.32 us: leaf_stage(): pl.pallas_call(leaf_kernel, in_specs=[SMEM, HBM, HBM, VMEM, VMEM, VMEM],...]
    ppermute x17 -> x19, waiting for transfers between devices: 13.6 us -> 17.4 us  [swapped(): return lax.ppermute(x, axis, [(i, i ^ mask) for i in range(size)])]
    ppermute x17 -> x19, starting transfers between devices: 43.3 us -> 42.9 us  [swapped(): return lax.ppermute(x, axis, [(i, i ^ mask) for i in range(size)])]
  transfers between devices with their start and end apart: 17 -> 19, of which waited for: 8 -> 11; matrix products, arithmetic and copies ran while one was open for 0% -> 0% of each run, Pallas kernels for 13% -> 12%
where the time goes in v2:
time: 84.3 us; the launch traced here: 84.2 us
  starting transfers between devices  42.9 us (51%)
  Pallas kernels  23.6 us (28%)
  waiting for transfers between devices  17.4 us (21%)
    ppermute x19, starting transfers between devices, swapped(): return lax.ppermute(x, axis, [(i, i ^ mask) for i in range(size)])  42.9 us
    ppermute x19, waiting for transfers between devices, swapped(): return lax.ppermute(x, axis, [(i, i ^ mask) for i in range(size)])  17.4 us
    pallas_call x1, Pallas kernels, leaf_stage(): pl.pallas_call(leaf_kernel, in_specs=[SMEM, HBM, HBM, VMEM, VMEM, VMEM],...  7.32 us
    pallas_call x1, Pallas kernels, early_corrections(): pl.pallas_call(early_kernel, grid_spec=pltpu.PrefetchScalarGridSpec(num_s...  5.09 us
    pallas_call x2, Pallas kernels, late_correction(): pl.pallas_call(late_kernel, grid_spec=pltpu.PrefetchScalarGridSpec(num_sc...  3.35 us
    pallas_call x1, Pallas kernels, open_stage(): pl.pallas_call(open_kernel, grid=(steps,), in_specs=[SMEM, pl.BlockSpec((...  3.35 us
    pallas_call x1, Pallas kernels, ready_stage(): pl.pallas_call(ready_kernel, grid_spec=pltpu.PrefetchScalarGridSpec(num_s...  3.17 us
  transfers between devices with their start and end apart: 19, of which 11 were waited for; matrix products, arithmetic and copies ran while one was open for 0% of the time, Pallas kernels for 12%

profile of v2, /device:TPU:1, one launch (start us, length us, event | category | flops | bytes accessed | tf_op | source)
XLA Modules:
  0.0 84.2 jit_solution(10528049923775773847)
XLA Ops:
  0.0 0.1 pad_add_fusion.1.place
  0.1 3.3 %open_stage.1 = (f32[16,384]{1,0:T(8,128)S(1)}, f32[16,384]{1,0:T(8,128)S(1)}, bf16[1024,512]{1,0:T(8,128)(2,1)S(1)}, bf16[1024,512]{1,0:T(8,128)(2,1)S(1)}, f32[128,1024]{1,0:T(8,128)S(1)}) custom-call(s32[2]{0:T(128)S(1)} %pad_add_fusion.1.place, f32[3,1024,128]{2,1,0:T(8,128)} %right.3, f32[3,1024,128]{2,1,0:T(8,128)} %left3.1, f32[3,1024,128]{2,1,0:T(8,128)} %left3.1, ...), custom_call_target="tpu_custom_call" | custom-call | flops 301989888 | bytes 4194304 | tf_op jit(solution)/shard_map/open_stage/pallas_call | solution.py:91
  3.4 7.3 %leaf_stage.1 = (f32[1024,512]{1,0:T(8,128)}, f32[256,384]{1,0:T(8,128)S(1)}, f32[256,384]{1,0:T(8,128)S(1)}) custom-call(s32[1]{0:T(128)} %bitcast.9.place, f32[1024,1024]{1,0:T(8,128)} %leaf.3, f32[3,1024,128]{2,1,0:T(8,128)} %right.3, bf16[1024,512]{1,0:T(8,128)(2,1)S(1)} %get-tuple-element.33.x_hi, bf16[1024,512]{1,0:T(8,128)(2,1)S(1)} %get-tuple-element.34.x_lo, ...), custom_call_target="tpu_custom_call" | custom-call | flops 4429185024 | bytes 8388608 | tf_op jit(solution)/shard_map/leaf_stage/pallas_call | solution.py:150
  10.8 3.3 %collective-permute-start = (f32[256,384]{1,0:T(8,128)S(1)}, f32[256,384]{1,0:T(8,128)S(1)}, u32[]{:S(2)}, u32[]{:S(2)}) collective-permute-start(f32[256,384]{1,0:T(8,128)S(1)} %get-tuple-element.37), channel_id=1, source_target_pairs={{0,4},{4,0},{8,12},{12,8},{16,20},{20,16},{24,28},{28,24},{32,36},... | collective-permute-start | bytes 1179656 | tf_op jit(solution)/shard_map/ppermute | solution.py:378
  14.0 1.3 %collective-permute-done.b = f32[256,384]{1,0:T(8,128)S(1)} collective-permute-done((f32[256,384]{1,0:T(8,128)S(1)}, f32[256,384]{1,0:T(8,128)S(1)}, u32[]{:S(2)}, u32[]{:S(2)}) %collective-permute-start) | collective-permute-done | bytes 393248 | tf_op jit(solution)/shard_map/ppermute | solution.py:378
  15.4 0.1 collective-permute-start.1
  15.5 0.6 collective-permute-start.4
  16.1 0.8 %collective-permute-done.4.b = f32[16,384]{1,0:T(8,128)S(1)} collective-permute-done((f32[16,384]{1,0:T(8,128)S(1)}, f32[16,384]{1,0:T(8,128)S(1)}, u32[]{:S(2)}, u32[]{:S(2)}) %collective-permute-start.4) | collective-permute-done | bytes 24608 | tf_op jit(solution)/shard_map/ppermute | solution.py:378
  17.0 1.5 %collective-permute-start.5 = (f32[16,384]{1,0:T(8,128)S(1)}, f32[16,384]{1,0:T(8,128)S(1)}, u32[]{:S(2)}, u32[]{:S(2)}) collective-permute-start(f32[16,384]{1,0:T(8,128)S(1)} %shard_map.58.a), channel_id=1, source_target_pairs={{0,8},{4,12},{8,0},{12,4},{16,24},{20,28},{24,16},{28,20},{32,40},... | collective-permute-start | bytes 73736 | tf_op jit(solution)/shard_map/ppermute | solution.py:378
  18.5 3.6 %collective-permute-done.5.b = f32[16,384]{1,0:T(8,128)S(1)} collective-permute-done((f32[16,384]{1,0:T(8,128)S(1)}, f32[16,384]{1,0:T(8,128)S(1)}, u32[]{:S(2)}, u32[]{:S(2)}) %collective-permute-start.5) | collective-permute-done | bytes 24608 | tf_op jit(solution)/shard_map/ppermute | solution.py:378
  22.2 1.6 %collective-permute-start.6 = (f32[16,384]{1,0:T(8,128)S(1)}, f32[16,384]{1,0:T(8,128)S(1)}, u32[]{:S(2)}, u32[]{:S(2)}) collective-permute-start(f32[16,384]{1,0:T(8,128)S(1)} %shard_map.59.a), channel_id=1, source_target_pairs={{0,16},{4,20},{8,24},{12,28},{16,0},{20,4},{24,8},{28,12},{32,48},... | collective-permute-start | bytes 73736 | tf_op jit(solution)/shard_map/ppermute | solution.py:378
  23.8 1.9 %collective-permute-done.6.b = f32[16,384]{1,0:T(8,128)S(1)} collective-permute-done((f32[16,384]{1,0:T(8,128)S(1)}, f32[16,384]{1,0:T(8,128)S(1)}, u32[]{:S(2)}, u32[]{:S(2)}) %collective-permute-start.6) | collective-permute-done | bytes 24608 | tf_op jit(solution)/shard_map/ppermute | solution.py:378
  25.7 3.9 %collective-permute-start.7 = (f32[16,384]{1,0:T(8,128)S(1)}, f32[16,384]{1,0:T(8,128)S(1)}, u32[]{:S(2)}, u32[]{:S(2)}) collective-permute-start(f32[16,384]{1,0:T(8,128)S(1)} %shard_map.60.a), channel_id=1, source_target_pairs={{0,56},{4,60},{8,48},{12,52},{16,40},{20,44},{24,32},{28,36},{32,2... | collective-permute-start | bytes 73736 | tf_op jit(solution)/shard_map/ppermute | solution.py:378
  29.6 0.0 collective-permute-done.1.b
  29.6 2.1 %collective-permute-start.2 = (f32[64,384]{1,0:T(8,128)S(1)}, f32[64,384]{1,0:T(8,128)S(1)}, u32[]{:S(2)}, u32[]{:S(2)}) collective-permute-start(f32[64,384]{1,0:T(8,128)S(1)} %get-tuple-element.41), channel_id=1, source_target_pairs={{0,16},{4,20},{8,24},{12,28},{16,0},{20,4},{24,8},{28,12},{32,48},... | collective-permute-start | bytes 294920 | tf_op jit(solution)/shard_map/ppermute | solution.py:378
  31.8 0.0 collective-permute-done.7.b
  31.8 2.6 %collective-permute-start.10 = (f32[16,640]{1,0:T(8,128)S(1)}, f32[16,640]{1,0:T(8,128)S(1)}, u32[]{:S(2)}, u32[]{:S(2)}) collective-permute-start(f32[16,640]{1,0:T(8,128)S(1)} %shard_map.61.refs_0_), channel_id=1, source_target_pairs={{0,3},{1,2},{2,1},{3,0},{4,7},{5,6},{6,5},{7,4},{8,11},{9,10},{10,... | collective-permute-start | bytes 122888 | tf_op jit(solution)/shard_map/ppermute | solution.py:378
  34.4 0.0 collective-permute-start.8
  34.4 1.4 %collective-permute-start.9 = (f32[16,640]{1,0:T(8,128)S(1)}, f32[16,640]{1,0:T(8,128)S(1)}, u32[]{:S(2)}, u32[]{:S(2)}) collective-permute-start(f32[16,640]{1,0:T(8,128)S(1)} %shard_map.61.refs_0_), channel_id=1, source_target_pairs={{0,2},{1,3},{2,0},{3,1},{4,6},{5,7},{6,4},{7,5},{8,10},{9,11},{10,... | collective-permute-start | bytes 122888 | tf_op jit(solution)/shard_map/ppermute | solution.py:378
  35.7 0.2 collective-permute-done.10.refs_3_
  35.9 1.6 %collective-permute-done.8.refs_1_ = f32[16,640]{1,0:T(8,128)S(1)} collective-permute-done((f32[16,640]{1,0:T(8,128)S(1)}, f32[16,640]{1,0:T(8,128)S(1)}, u32[]{:S(2)}, u32[]{:S(2)}) %collective-permute-start.8) | collective-permute-done | bytes 40992 | tf_op jit(solution)/shard_map/ppermute | solution.py:378
  37.5 1.2 %collective-permute-done.9.refs_2_ = f32[16,640]{1,0:T(8,128)S(1)} collective-permute-done((f32[16,640]{1,0:T(8,128)S(1)}, f32[16,640]{1,0:T(8,128)S(1)}, u32[]{:S(2)}, u32[]{:S(2)}) %collective-permute-start.9) | collective-permute-done | bytes 40992 | tf_op jit(solution)/shard_map/ppermute | solution.py:378
  38.7 4.7 %collective-permute-start.11 = (f32[64,640]{1,0:T(8,128)S(1)}, f32[64,640]{1,0:T(8,128)S(1)}, u32[]{:S(2)}, u32[]{:S(2)}) collective-permute-start(f32[64,640]{1,0:T(8,128)S(1)} %shard_map.62.mine), channel_id=1, source_target_pairs={{0,4},{4,0},{8,12},{12,8},{16,20},{20,16},{24,28},{28,24},{32,36},... | collective-permute-start | bytes 491528 | tf_op jit(solution)/shard_map/ppermute | solution.py:378
  43.4 0.0 collective-permute-done.2.b
  43.4 2.3 %collective-permute-start.3 = (f32[64,384]{1,0:T(8,128)S(1)}, f32[64,384]{1,0:T(8,128)S(1)}, u32[]{:S(2)}, u32[]{:S(2)}) collective-permute-start(f32[64,384]{1,0:T(8,128)S(1)} %shard_map.57.own), channel_id=1, source_target_pairs={{0,56},{4,60},{8,48},{12,52},{16,40},{20,44},{24,32},{28,36},{32,2... | collective-permute-start | bytes 294920 | tf_op jit(solution)/shard_map/ppermute | solution.py:378
  45.7 0.1 pad_add_fusion.place
  45.8 3.2 %ready_stage.1 = (bf16[1024,384]{1,0:T(8,128)(2,1)S(1)}, bf16[1024,384]{1,0:T(8,128)(2,1)S(1)}, f32[256,256]{1,0:T(8,128)S(1)}, f32[256,256]{1,0:T(8,128)S(1)}, f32[256,256]{1,0:T(8,128)S(1)}) custom-call(s32[2]{0:T(128)S(1)} %pad_add_fusion.place, f32[3,1024,128]{2,1,0:T(8,128)} %left3.1, f32[7,256,256]{2,1,0:T(8,128)} %core1.1, f32[7,256,256]{2,1,0:T(8,128)} %core1.1, ...), custom_call_target="tpu_custom_call" | custom-call | flops 4194304 | bytes 3145728 | tf_op jit(solution)/shard_map/ready_stage/pallas_call | solution.py:181
  49.0 0.0 collective-permute-done.11.other
  49.0 1.6 %collective-permute-start.13 = (f32[128,128]{1,0:T(8,128)S(1)}, f32[128,128]{1,0:T(8,128)S(1)}, u32[]{:S(2)}, u32[]{:S(2)}) collective-permute-start(f32[128,128]{1,0:T(8,128)S(1)} %get-tuple-element.48.gram_own), channel_id=1, source_target_pairs={{0,64},{4,68},{8,72},{12,76},{16,80},{20,84},{24,88},{28,92},{32,9... | collective-permute-start | bytes 196616 | tf_op jit(solution)/shard_map/ppermute | solution.py:378
  50.6 0.4 shard_map.64
  51.0 0.3 collective-permute-start.12
  51.3 1.1 %collective-permute-done.13.gram_oth = f32[128,128]{1,0:T(8,128)S(1)} collective-permute-done((f32[128,128]{1,0:T(8,128)S(1)}, f32[128,128]{1,0:T(8,128)S(1)}, u32[]{:S(2)}, u32[]{:S(2)}) %collective-permute-start.13) | collective-permute-done | bytes 65568 | tf_op jit(solution)/shard_map/ppermute | solution.py:378
  52.4 1.8 %collective-permute-done.12.oth = f32[64,256]{1,0:T(8,128)S(1)} collective-permute-done((f32[64,256]{1,0:T(8,128)S(1)}, f32[64,256]{1,0:T(8,128)S(1)}, u32[]{:S(2)}, u32[]{:S(2)}) %collective-permute-start.12) | collective-permute-done | bytes 65568 | tf_op jit(solution)/shard_map/ppermute | solution.py:378
  54.2 0.4 shard_map.65
  54.7 2.7 %collective-permute-start.14 = (f32[64,128]{1,0:T(8,128)S(1)}, f32[64,128]{1,0:T(8,128)S(1)}, u32[]{:S(2)}, u32[]{:S(2)}) collective-permute-start(f32[64,128]{1,0:T(8,128)S(1)} %get-tuple-element.49.own), channel_id=1, source_target_pairs={{0,128},{4,132},{8,136},{12,140},{16,144},{20,148},{24,152},{28,15... | collective-permute-start | bytes 98312 | tf_op jit(solution)/shard_map/ppermute | solution.py:378
  57.4 1.6 %collective-permute-done.14.oth = f32[64,128]{1,0:T(8,128)S(1)} collective-permute-done((f32[64,128]{1,0:T(8,128)S(1)}, f32[64,128]{1,0:T(8,128)S(1)}, u32[]{:S(2)}, u32[]{:S(2)}) %collective-permute-start.14) | collective-permute-done | bytes 32800 | tf_op jit(solution)/shard_map/ppermute | solution.py:378
  59.0 0.3 shard_map.66.mine
  59.3 4.0 %collective-permute-start.15 = (f32[64,384]{1,0:T(8,128)S(1)}, f32[64,384]{1,0:T(8,128)S(1)}, u32[]{:S(2)}, u32[]{:S(2)}) collective-permute-start(f32[64,384]{1,0:T(8,128)S(1)} %shard_map.66.mine), channel_id=1, source_target_pairs={{0,16},{4,20},{8,24},{12,28},{16,0},{20,4},{24,8},{28,12},{32,48},... | collective-permute-start | bytes 294920 | tf_op jit(solution)/shard_map/ppermute | solution.py:378
  63.3 2.0 %collective-permute-done.15.other = f32[64,384]{1,0:T(8,128)S(1)} collective-permute-done((f32[64,384]{1,0:T(8,128)S(1)}, f32[64,384]{1,0:T(8,128)S(1)}, u32[]{:S(2)}, u32[]{:S(2)}) %collective-permute-start.15) | collective-permute-done | bytes 98336 | tf_op jit(solution)/shard_map/ppermute | solution.py:378
  65.3 2.0 %collective-permute-start.16 = (f32[128,384]{1,0:T(8,128)S(1)}, f32[128,384]{1,0:T(8,128)S(1)}, u32[]{:S(2)}, u32[]{:S(2)}) collective-permute-start(f32[128,384]{1,0:T(8,128)S(1)} %shard_map.67.c), channel_id=1, source_target_pairs={{0,8},{4,12},{8,0},{12,4},{16,24},{20,28},{24,16},{28,20},{32,40},... | collective-permute-start | bytes 589832 | tf_op jit(solution)/shard_map/ppermute | solution.py:378
  67.3 4.7 %collective-permute-start.18 = (f32[128,384]{1,0:T(8,128)S(1)}, f32[128,384]{1,0:T(8,128)S(1)}, u32[]{:S(2)}, u32[]{:S(2)}) collective-permute-start(f32[128,384]{1,0:T(8,128)S(1)} %shard_map.67.c), channel_id=1, source_target_pairs={{0,4},{4,0},{8,12},{12,8},{16,20},{20,16},{24,28},{28,24},{32,36},... | collective-permute-start | bytes 589832 | tf_op jit(solution)/shard_map/ppermute | solution.py:378
  72.0 0.0 collective-permute-done.16.c
  72.0 3.6 %collective-permute-start.17 = (f32[128,384]{1,0:T(8,128)S(1)}, f32[128,384]{1,0:T(8,128)S(1)}, u32[]{:S(2)}, u32[]{:S(2)}) collective-permute-start(f32[128,384]{1,0:T(8,128)S(1)} %collective-permute-done.16.c), channel_id=1, source_target_pairs={{0,4},{4,0},{8,12},{12,8},{16,20},{20,16},{24,28},{28,24},{32,36},... | collective-permute-start | bytes 589832 | tf_op jit(solution)/shard_map/ppermute | solution.py:378
  75.6 0.1 pad_add_fusion.2.where
  75.7 5.1 %early.1 = (f32[1024,512]{1,0:T(8,128)}, f32[1024,128]{1,0:T(8,128)S(1)}, f32[1024,128]{1,0:T(8,128)S(1)}) custom-call(s32[4]{0:T(128)S(1)} %pad_add_fusion.2.where, f32[1024,512]{1,0:T(8,128)} %get-tuple-element.53.y0.columns, bf16[1024,384]{1,0:T(8,128)(2,1)S(1)} %get-tuple-element.31.l_hi, bf16[1024,384]{1,0:T(8,128)(2,1)S(1)} %get-tuple-element.32.l_lo, ...), custom_call_target="tpu_custom_call" | custom-call | flops 603979776 | bytes 3145728 | tf_op jit(solution)/shard_map/early/pallas_call | solution.py:343
  80.8 1.7 %shard_map.68.into = f32[1024,512]{1,0:T(8,128)} custom-call(s32[1]{0:T(128)} %bitcast.12.where, bf16[1024,384]{1,0:T(8,128)(2,1)S(1)} %get-tuple-element.31.l_hi, bf16[1024,384]{1,0:T(8,128)(2,1)S(1)} %get-tuple-element.32.l_lo, f32[128,384]{1,0:T(8,128)S(1)} %collective-permute-done.16.c, ...), custom_call_target="tpu_custom_call", output_to_operand_aliasing={{}: (5, {})} | custom-call | flops 301989888 | bytes 1048576 | tf_op jit(solution)/shard_map/pallas_call | solution.py:361
  82.5 0.0 collective-permute-done.17.c
  82.5 1.7 %shard_map.69 = f32[1024,512]{1,0:T(8,128)} custom-call(s32[1]{0:T(128)} %bitcast.where, bf16[1024,384]{1,0:T(8,128)(2,1)S(1)} %get-tuple-element.31.l_hi, bf16[1024,384]{1,0:T(8,128)(2,1)S(1)} %get-tuple-element.32.l_lo, f32[128,384]{1,0:T(8,128)S(1)} %collective-permute-done.17.c, ...), custom_call_target="tpu_custom_call", output_to_operand_aliasing={{}: (5, {})} | custom-call | flops 301989888 | bytes 1048576 | tf_op jit(solution)/shard_map/pallas_call | solution.py:361
  (12 shorter events, 0.2 us)
Async XLA Ops:
  10.8 4.6 %collective-permute-start = (f32[256,384]{1,0:T(8,128)S(1)}, f32[256,384]{1,0:T(8,128)S(1)}, u32[]{:S(2)}, u32[]{:S(2)}) collective-permute-start(f32[256,384]{1,0:T(8,128)S(1)} %get-tuple-element.37), channel_id=1, source_target_pairs={{0,4},{4,0},{8,12},{12,8},{16,20},{20,16},{24,28},{28,24},{32,36},... | collective-permute-start | bytes 1179656 | tf_op jit(solution)/shard_map/ppermute | solution.py:378
  15.4 14.2 %collective-permute-start.1 = (f32[128,384]{1,0:T(8,128)S(1)}, f32[128,384]{1,0:T(8,128)S(1)}, u32[]{:S(2)}, u32[]{:S(2)}) collective-permute-start(f32[128,384]{1,0:T(8,128)S(1)} %get-tuple-element.39), channel_id=1, source_target_pairs={{0,8},{4,12},{8,0},{12,4},{16,24},{20,28},{24,16},{28,20},{32,40},... | collective-permute-start | bytes 589832 | tf_op jit(solution)/shard_map/ppermute | solution.py:378
  15.5 1.4 %collective-permute-start.4 = (f32[16,384]{1,0:T(8,128)S(1)}, f32[16,384]{1,0:T(8,128)S(1)}, u32[]{:S(2)}, u32[]{:S(2)}) collective-permute-start(f32[16,384]{1,0:T(8,128)S(1)} %get-tuple-element.44), channel_id=1, source_target_pairs={{0,4},{4,0},{8,12},{12,8},{16,20},{20,16},{24,28},{28,24},{32,36},... | collective-permute-start | bytes 73736 | tf_op jit(solution)/shard_map/ppermute | solution.py:378
  17.0 5.2 %collective-permute-start.5 = (f32[16,384]{1,0:T(8,128)S(1)}, f32[16,384]{1,0:T(8,128)S(1)}, u32[]{:S(2)}, u32[]{:S(2)}) collective-permute-start(f32[16,384]{1,0:T(8,128)S(1)} %shard_map.58.a), channel_id=1, source_target_pairs={{0,8},{4,12},{8,0},{12,4},{16,24},{20,28},{24,16},{28,20},{32,40},... | collective-permute-start | bytes 73736 | tf_op jit(solution)/shard_map/ppermute | solution.py:378
  22.2 3.6 %collective-permute-start.6 = (f32[16,384]{1,0:T(8,128)S(1)}, f32[16,384]{1,0:T(8,128)S(1)}, u32[]{:S(2)}, u32[]{:S(2)}) collective-permute-start(f32[16,384]{1,0:T(8,128)S(1)} %shard_map.59.a), channel_id=1, source_target_pairs={{0,16},{4,20},{8,24},{12,28},{16,0},{20,4},{24,8},{28,12},{32,48},... | collective-permute-start | bytes 73736 | tf_op jit(solution)/shard_map/ppermute | solution.py:378
  25.7 6.0 %collective-permute-start.7 = (f32[16,384]{1,0:T(8,128)S(1)}, f32[16,384]{1,0:T(8,128)S(1)}, u32[]{:S(2)}, u32[]{:S(2)}) collective-permute-start(f32[16,384]{1,0:T(8,128)S(1)} %shard_map.60.a), channel_id=1, source_target_pairs={{0,56},{4,60},{8,48},{12,52},{16,40},{20,44},{24,32},{28,36},{32,2... | collective-permute-start | bytes 73736 | tf_op jit(solution)/shard_map/ppermute | solution.py:378
  29.6 13.8 %collective-permute-start.2 = (f32[64,384]{1,0:T(8,128)S(1)}, f32[64,384]{1,0:T(8,128)S(1)}, u32[]{:S(2)}, u32[]{:S(2)}) collective-permute-start(f32[64,384]{1,0:T(8,128)S(1)} %get-tuple-element.41), channel_id=1, source_target_pairs={{0,16},{4,20},{8,24},{12,28},{16,0},{20,4},{24,8},{28,12},{32,48},... | collective-permute-start | bytes 294920 | tf_op jit(solution)/shard_map/ppermute | solution.py:378
  31.8 4.2 %collective-permute-start.10 = (f32[16,640]{1,0:T(8,128)S(1)}, f32[16,640]{1,0:T(8,128)S(1)}, u32[]{:S(2)}, u32[]{:S(2)}) collective-permute-start(f32[16,640]{1,0:T(8,128)S(1)} %shard_map.61.refs_0_), channel_id=1, source_target_pairs={{0,3},{1,2},{2,1},{3,0},{4,7},{5,6},{6,5},{7,4},{8,11},{9,10},{10,... | collective-permute-start | bytes 122888 | tf_op jit(solution)/shard_map/ppermute | solution.py:378
  34.4 3.1 %collective-permute-start.8 = (f32[16,640]{1,0:T(8,128)S(1)}, f32[16,640]{1,0:T(8,128)S(1)}, u32[]{:S(2)}, u32[]{:S(2)}) collective-permute-start(f32[16,640]{1,0:T(8,128)S(1)} %shard_map.61.refs_0_), channel_id=1, source_target_pairs={{0,1},{1,0},{2,3},{3,2},{4,5},{5,4},{6,7},{7,6},{8,9},{9,8},{10,11... | collective-permute-start | bytes 122888 | tf_op jit(solution)/shard_map/ppermute | solution.py:378
  34.4 4.4 %collective-permute-start.9 = (f32[16,640]{1,0:T(8,128)S(1)}, f32[16,640]{1,0:T(8,128)S(1)}, u32[]{:S(2)}, u32[]{:S(2)}) collective-permute-start(f32[16,640]{1,0:T(8,128)S(1)} %shard_map.61.refs_0_), channel_id=1, source_target_pairs={{0,2},{1,3},{2,0},{3,1},{4,6},{5,7},{6,4},{7,5},{8,10},{9,11},{10,... | collective-permute-start | bytes 122888 | tf_op jit(solution)/shard_map/ppermute | solution.py:378
  38.7 10.2 %collective-permute-start.11 = (f32[64,640]{1,0:T(8,128)S(1)}, f32[64,640]{1,0:T(8,128)S(1)}, u32[]{:S(2)}, u32[]{:S(2)}) collective-permute-start(f32[64,640]{1,0:T(8,128)S(1)} %shard_map.62.mine), channel_id=1, source_target_pairs={{0,4},{4,0},{8,12},{12,8},{16,20},{20,16},{24,28},{28,24},{32,36},... | collective-permute-start | bytes 491528 | tf_op jit(solution)/shard_map/ppermute | solution.py:378
  43.4 7.2 %collective-permute-start.3 = (f32[64,384]{1,0:T(8,128)S(1)}, f32[64,384]{1,0:T(8,128)S(1)}, u32[]{:S(2)}, u32[]{:S(2)}) collective-permute-start(f32[64,384]{1,0:T(8,128)S(1)} %shard_map.57.own), channel_id=1, source_target_pairs={{0,56},{4,60},{8,48},{12,52},{16,40},{20,44},{24,32},{28,36},{32,2... | collective-permute-start | bytes 294920 | tf_op jit(solution)/shard_map/ppermute | solution.py:378
  49.0 3.4 %collective-permute-start.13 = (f32[128,128]{1,0:T(8,128)S(1)}, f32[128,128]{1,0:T(8,128)S(1)}, u32[]{:S(2)}, u32[]{:S(2)}) collective-permute-start(f32[128,128]{1,0:T(8,128)S(1)} %get-tuple-element.48.gram_own), channel_id=1, source_target_pairs={{0,64},{4,68},{8,72},{12,76},{16,80},{20,84},{24,88},{28,92},{32,9... | collective-permute-start | bytes 196616 | tf_op jit(solution)/shard_map/ppermute | solution.py:378
  51.0 3.2 %collective-permute-start.12 = (f32[64,256]{1,0:T(8,128)S(1)}, f32[64,256]{1,0:T(8,128)S(1)}, u32[]{:S(2)}, u32[]{:S(2)}) collective-permute-start(f32[64,256]{1,0:T(8,128)S(1)} %get-tuple-element.46.own), channel_id=1, source_target_pairs={{0,64},{4,68},{8,72},{12,76},{16,80},{20,84},{24,88},{28,92},{32,9... | collective-permute-start | bytes 196616 | tf_op jit(solution)/shard_map/ppermute | solution.py:378
  54.7 4.4 %collective-permute-start.14 = (f32[64,128]{1,0:T(8,128)S(1)}, f32[64,128]{1,0:T(8,128)S(1)}, u32[]{:S(2)}, u32[]{:S(2)}) collective-permute-start(f32[64,128]{1,0:T(8,128)S(1)} %get-tuple-element.49.own), channel_id=1, source_target_pairs={{0,128},{4,132},{8,136},{12,140},{16,144},{20,148},{24,152},{28,15... | collective-permute-start | bytes 98312 | tf_op jit(solution)/shard_map/ppermute | solution.py:378
  59.3 6.0 %collective-permute-start.15 = (f32[64,384]{1,0:T(8,128)S(1)}, f32[64,384]{1,0:T(8,128)S(1)}, u32[]{:S(2)}, u32[]{:S(2)}) collective-permute-start(f32[64,384]{1,0:T(8,128)S(1)} %shard_map.66.mine), channel_id=1, source_target_pairs={{0,16},{4,20},{8,24},{12,28},{16,0},{20,4},{24,8},{28,12},{32,48},... | collective-permute-start | bytes 294920 | tf_op jit(solution)/shard_map/ppermute | solution.py:378
  65.3 6.7 %collective-permute-start.16 = (f32[128,384]{1,0:T(8,128)S(1)}, f32[128,384]{1,0:T(8,128)S(1)}, u32[]{:S(2)}, u32[]{:S(2)}) collective-permute-start(f32[128,384]{1,0:T(8,128)S(1)} %shard_map.67.c), channel_id=1, source_target_pairs={{0,8},{4,12},{8,0},{12,4},{16,24},{20,28},{24,16},{28,20},{32,40},... | collective-permute-start | bytes 589832 | tf_op jit(solution)/shard_map/ppermute | solution.py:378
  67.3 8.4 %collective-permute-start.18 = (f32[128,384]{1,0:T(8,128)S(1)}, f32[128,384]{1,0:T(8,128)S(1)}, u32[]{:S(2)}, u32[]{:S(2)}) collective-permute-start(f32[128,384]{1,0:T(8,128)S(1)} %shard_map.67.c), channel_id=1, source_target_pairs={{0,4},{4,0},{8,12},{12,8},{16,20},{20,16},{24,28},{28,24},{32,36},... | collective-permute-start | bytes 589832 | tf_op jit(solution)/shard_map/ppermute | solution.py:378
  72.0 10.5 %collective-permute-start.17 = (f32[128,384]{1,0:T(8,128)S(1)}, f32[128,384]{1,0:T(8,128)S(1)}, u32[]{:S(2)}, u32[]{:S(2)}) collective-permute-start(f32[128,384]{1,0:T(8,128)S(1)} %collective-permute-done.16.c), channel_id=1, source_target_pairs={{0,4},{4,0},{8,12},{12,8},{16,20},{20,16},{24,28},{28,24},{32,36},... | collective-permute-start | bytes 589832 | tf_op jit(solution)/shard_map/ppermute | solution.py:378

commit v3 on v2

--- a/solution.py
+++ b/solution.py
@@ -12,7 +12,8 @@
 COLS = 512
 QUARTER = RANK // XS
 EIGHTH = QUARTER // 2
-BLOCKS = 128, 128, 256, 256, 256
+BLOCKS = 64, 192, 256, 256, 256
+BATCH = 256
 NN = (((1,), (0,)), ((), ()))
 NT = (((1,), (1,)), ((), ()))
 VMEM = pl.BlockSpec(memory_space=pltpu.VMEM)
@@ -61,7 +62,7 @@
     return pltpu.HBM(shape, jnp.float32)
 
 
-def open_kernel(place, right, left2, left3, rhs, leaf, keep, send, x_hi, x_lo, ahead, acc, sem):
+def open_kernel(place, right, left2, left3, rhs, leaf, gram, x_hi, x_lo, ahead, acc, sem):
     i = pl.program_id(0)
     copy = pltpu.make_async_copy(leaf.at[: ahead.shape[0], :], ahead, sem)
 
@@ -79,9 +80,7 @@
 
     @pl.when(i == pl.num_programs(0) - 1)
     def _():
-        start = place[0] * QUARTER
-        keep[...] = acc[pl.ds(pl.multiple_of(start + place[1] * EIGHTH, EIGHTH), EIGHTH), :]
-        send[...] = acc[pl.ds(pl.multiple_of(start + (1 - place[1]) * EIGHTH, EIGHTH), EIGHTH), :]
+        gram[...] = acc[pl.ds(pl.multiple_of(place[0] * QUARTER, QUARTER), QUARTER), :]
         copy.wait()
 
 
@@ -99,8 +98,8 @@
             pl.BlockSpec((height, COLS), lambda i: (i, 0)),
             HBM,
         ],
-        out_specs=[VMEM] * 5,
-        out_shape=[f32(EIGHTH, 3 * RANK)] * 2 + [bf16(LEAF, COLS), bf16(LEAF, COLS), f32(BLOCKS[0], LEAF)],
+        out_specs=[VMEM] * 4,
+        out_shape=[f32(QUARTER, 3 * RANK), bf16(LEAF, COLS), bf16(LEAF, COLS), f32(BLOCKS[0], LEAF)],
         scratch_shapes=[pltpu.VMEM((RANK, 3 * RANK), jnp.float32), pltpu.SemaphoreType.DMA],
         compiler_params=params(12),
         cost_estimate=cost(6 * LEAF * RANK * 3 * RANK, 4 << 20),
@@ -118,18 +117,22 @@
     bases_load.start()
     for load in loads[2:]:
         load.start()
+    projected = 0
     for k, here in enumerate(rows):
         if k:
             loads[k].wait()
         block = blocks[here, :] if k else ahead[...]
-        part = dot3(split(block), (x_hi[...], x_lo[...]), NN)
-        y[here, :] = part
+        y[here, :] = dot3(split(block), (x_hi[...], x_lo[...]), NN)
         stores[k].start()
-        if k == 0:
+        if k == 1:
             bases_load.wait()
-        rt = split(jnp.concatenate([bases[i, here, :].T for i in range(3)], axis=0))
-        q = dot3(rt, split(part), NN)
-        acc[...] = acc[...] + q if k else q
+        ready = here.stop if k == count - 1 else here.start // BATCH * BATCH
+        while projected < ready:
+            done = slice(projected, projected + BATCH)
+            projected += BATCH
+            rt = split(jnp.concatenate([bases[i, done, :].T for i in range(3)], axis=0))
+            q = dot3(rt, split(y[done, :]), NN)
+            acc[...] = acc[...] + q if done.start else q
     first_half, second_half = acc[:, : COLS // 2].T, acc[:, COLS // 2 :].T
 
     @pl.when(place[0] == 0)
@@ -165,38 +168,48 @@
     )(place, in_hbm(leaf), in_hbm(right), *in_chip(*arrays))
 
 
-def ready_kernel(place, left, core3, core2, core1, hi, lo, out3, out2, out1):
+def left_kernel(left, hi, lo):
     for k in range(3):
         hi[:, k * RANK : (k + 1) * RANK], lo[:, k * RANK : (k + 1) * RANK] = split(left[k])
 
-    @pl.when(pl.program_id(0) == 0)
-    def _():
-        out3[...], out2[...], out1[...] = core3[0], core2[0], core1[0]
-
-
-def ready_stage(place, left, cores):
+
+def left_halves(left):
     steps = 4
     height = LEAF // steps
-    node = (1, 2 * RANK, 2 * RANK)
-    return pl.pallas_call(
-        ready_kernel,
-        grid_spec=pltpu.PrefetchScalarGridSpec(
-            num_scalar_prefetch=1,
-            grid=(steps,),
-            in_specs=[
-                pl.BlockSpec((3, height, RANK), lambda i, w: (0, i, 0)),
-                pl.BlockSpec(node, lambda i, w: (w[0], 0, 0)),
-                pl.BlockSpec(node, lambda i, w: (w[1], 0, 0)),
-                pl.BlockSpec(node, lambda i, w: (0, 0, 0)),
-            ],
-            out_specs=[pl.BlockSpec((height, 3 * RANK), lambda i, w: (i, 0))] * 2
-            + [pl.BlockSpec(node[1:], lambda i, w: (0, 0))] * 3,
-        ),
-        out_shape=[bf16(LEAF, 3 * RANK)] * 2 + [f32(*node[1:])] * 3,
+    return pl.pallas_call(
+        left_kernel,
+        grid=(steps,),
+        in_specs=[pl.BlockSpec((3, height, RANK), lambda i: (0, i, 0))],
+        out_specs=[pl.BlockSpec((height, 3 * RANK), lambda i: (i, 0))] * 2,
+        out_shape=[bf16(LEAF, 3 * RANK)] * 2,
         compiler_params=params(8),
         cost_estimate=cost(1 << 22, 3 << 20),
-        name="ready_stage",
-    )(place, in_hbm(left), in_hbm(cores), in_hbm(cores), in_hbm(cores))
+        name="left_halves",
+    )(in_hbm(left))
+
+
+def pick_kernel(place, cores, out3, out2, out1, sems):
+    copies = [
+        pltpu.make_async_copy(cores.at[where], out, sems.at[k])
+        for k, (where, out) in enumerate(((place[0], out3), (place[1], out2), (0, out1)))
+    ]
+    for copy in copies:
+        copy.start()
+    for copy in copies:
+        copy.wait()
+
+
+def pick_cores(place, cores):
+    return pl.pallas_call(
+        pick_kernel,
+        in_specs=[SMEM, HBM],
+        out_specs=[VMEM] * 3,
+        out_shape=[f32(*cores.shape[1:])] * 3,
+        scratch_shapes=[pltpu.SemaphoreType.DMA((3,))],
+        compiler_params=params(4),
+        cost_estimate=cost(1 << 20, 1 << 20),
+        name="pick_cores",
+    )(place, in_hbm(cores))
 
 
 def node3_kernel(place, own, oth, core, gram, c_own, rest):
@@ -302,34 +315,22 @@
             gram2[pl.ds(start, EIGHTH), :] = part[here, 2 * n :]
 
 
-def early_kernel(where, y0, l_hi, l_lo, c, c_core, columns, out, ahead_a, ahead_b, sems):
-    i = pl.program_id(0)
-    copies = [
-        pltpu.make_async_copy(y0.at[:, pl.ds(pl.multiple_of(where[2 + k] * RANK, RANK), RANK)], ahead, sems.at[k])
-        for k, ahead in enumerate((ahead_a, ahead_b))
-    ]
-
-    @pl.when(i == 0)
-    def _():
-        for copy in copies:
-            copy.start()
-
-    half = out.shape[0]
-    rows = pl.ds(pl.multiple_of(i % 2 * half, half), half)
-    left = l_hi[rows, :], l_lo[rows, :]
-
-    @pl.when(i < 2)
-    def _():
-        out[...] = columns[...] - dot3(left, split(c[...]), NT)
-
-    @pl.when(i >= 2)
-    def _():
-        out[...] = columns[...] - dot3(left, split(c_core[...]), NT)
-
-    @pl.when(i == pl.num_programs(0) - 1)
-    def _():
-        for copy in copies:
-            copy.wait()
+def early_kernel(where, y0, l_hi, l_lo, c, c_core, out, ahead_a, ahead_b, given, made, sems):
+    def columns(ref, k):
+        return ref.at[:, pl.ds(pl.multiple_of(where[k] * RANK, RANK), RANK)]
+
+    targets = given.at[0], given.at[1], ahead_a, ahead_b
+    loads = [pltpu.make_async_copy(columns(y0, k), target, sems.at[k]) for k, target in enumerate(targets)]
+    stores = [pltpu.make_async_copy(made.at[k], columns(out, k), sems.at[4 + k]) for k in range(2)]
+    for load in loads:
+        load.start()
+    for k, chunk in enumerate((c, c_core)):
+        fix = dot3((l_hi[...], l_lo[...]), split(chunk[...]), NT)
+        loads[k].wait()
+        made[k] = given[k] - fix
+        stores[k].start()
+    for copy in loads[2:] + stores:
+        copy.wait()
 
 
 def late_kernel(where, l_hi, l_lo, c, columns, into, out):
@@ -339,21 +340,16 @@
 
 
 def early_corrections(where, y0, left, c, c_core):
-    block = pl.BlockSpec((LEAF // 2, RANK), lambda i, w: (i % 2, w[i // 2]))
     return pl.pallas_call(
         early_kernel,
-        grid_spec=pltpu.PrefetchScalarGridSpec(
-            num_scalar_prefetch=1,
-            grid=(4,),
-            in_specs=[HBM] + [VMEM] * 4 + [block],
-            out_specs=[block, VMEM, VMEM],
-            scratch_shapes=[pltpu.SemaphoreType.DMA((2,))],
-        ),
+        in_specs=[SMEM, HBM] + [VMEM] * 4,
+        out_specs=[HBM, VMEM, VMEM],
         out_shape=[far(LEAF, COLS)] + [f32(LEAF, RANK)] * 2,
-        compiler_params=params(8),
+        scratch_shapes=[pltpu.VMEM((2, LEAF, RANK), jnp.float32)] * 2 + [pltpu.SemaphoreType.DMA((6,))],
+        compiler_params=params(12),
         cost_estimate=cost(12 * LEAF * 3 * RANK * RANK, 3 << 20),
         name="early",
-    )(where, in_hbm(y0), *in_chip(*left, c, c_core), in_hbm(y0))
+    )(where, in_hbm(y0), *in_chip(*left, c, c_core))
 
 
 def late_correction(where, left, c, columns, into):
@@ -386,12 +382,12 @@
     low, high = (z & 1) ^ sib, ((z >> 1) & 1) ^ sib
     scalar = lambda v: v.reshape(1)
 
-    gram, gram_send, *arrays = open_stage(jnp.stack([x, core]), basis_right, basis_left, rhs, leaf_inverse)
+    gram, *arrays = open_stage(scalar(x), basis_right, basis_left, rhs, leaf_inverse)
     y0, keep, send = leaf_stage(scalar(core), leaf_inverse, basis_right, *arrays)
     got = swapped(send, 1)
 
-    gram = add(scalar(x), gram, swapped(gram_send, 1))
-    gram = add(scalar(x), gram, swapped(gram, 2))
+    send_gram, gram = halves(scalar(core), gram, swapped(gram, 2))
+    gram = add(scalar(x), gram, swapped(send_gram, 1))
     gram = add(scalar(x), gram, swapped(gram, 4))
     wide = (EIGHTH, 5 * RANK)
     (sums,) = in_vmem(beside_kernel, [wide], scalar(x), gram, swapped(gram, 14))
@@ -405,7 +401,7 @@
     own = add(scalar(x), keep, swapped(send, 4))
     oth = swapped(own, 14)
 
-    l_hi, l_lo, core3, core2, core1 = ready_stage(jnp.stack([3 + y, 1 + half]), basis_left, cores)
+    core3, core2, core1 = pick_cores(jnp.stack([3 + y, 1 + half]), cores)
 
     chunk = (COLS // 8, RANK)
     c3, rest = in_vmem(node3_kernel, [chunk, (COLS // 8, 2 * RANK)], scalar(sib), own, oth, core3, gram3)
@@ -418,7 +414,7 @@
     c_core = swapped(c, 1)
     c_core_low = swapped(c_low, 1)
 
-    left = l_hi, l_lo
+    left = left_halves(basis_left)
     order = jnp.stack([2 * core + low, 2 * (1 - core) + low, 2 * core + 1 - low, 2 * (1 - core) + 1 - low])
     out, ahead_a, ahead_b = early_corrections(order, y0, left, c, c_core)
     out = late_correction(order[2:3], left, c_low, ahead_a, out)

time: 84.3 us -> 82.7 us (0.981)
  Pallas kernels: 23.6 us -> 22.3 us
  starting transfers between devices: 42.9 us -> 41.7 us
  waiting for transfers between devices: 17.4 us -> 18.4 us
    ppermute x19, starting transfers between devices: 42.9 us -> 41.7 us  [swapped(): return lax.ppermute(x, axis, [(i, i ^ mask) for i in range(size)])]
    pallas_call x1, Pallas kernels: 7.32 us -> 6.31 us  [leaf_stage(): pl.pallas_call(leaf_kernel, in_specs=[SMEM, HBM, HBM, VMEM, VMEM, VMEM],...]
    ppermute x19, waiting for transfers between devices: 17.4 us -> 18.4 us  [swapped(): return lax.ppermute(x, axis, [(i, i ^ mask) for i in range(size)])]
    pallas_call x2 -> x3, Pallas kernels: 8.26 us -> 7.97 us  [the longest x1 4 us: early_corrections(): pl.pallas_call(early_kernel, in_specs=[SMEM, HBM] + [VMEM] * 4, out_specs...]
  transfers between devices with their start and end apart: 19 -> 19, of which waited for: 11 -> 10; matrix products, arithmetic and copies ran while one was open for 0% -> 0% of each run, Pallas kernels for 12% -> 12%
where the time goes in v3:
time: 82.7 us; the launch traced here: 82.6 us
  starting transfers between devices  41.7 us (50%)
  Pallas kernels  22.3 us (27%)
  waiting for transfers between devices  18.4 us (22%)
    ppermute x19, starting transfers between devices, swapped(): return lax.ppermute(x, axis, [(i, i ^ mask) for i in range(size)])  41.7 us
    ppermute x19, waiting for transfers between devices, swapped(): return lax.ppermute(x, axis, [(i, i ^ mask) for i in range(size)])  18.4 us
    pallas_call x1, Pallas kernels, leaf_stage(): pl.pallas_call(leaf_kernel, in_specs=[SMEM, HBM, HBM, VMEM, VMEM, VMEM],...  6.31 us
    pallas_call x1, Pallas kernels, early_corrections(): pl.pallas_call(early_kernel, in_specs=[SMEM, HBM] + [VMEM] * 4, out_specs...  4 us
    pallas_call x2, Pallas kernels, late_correction(): pl.pallas_call(late_kernel, grid_spec=pltpu.PrefetchScalarGridSpec(num_sc...  3.36 us
    pallas_call x1, Pallas kernels, open_stage(): pl.pallas_call(open_kernel, grid=(steps,), in_specs=[SMEM, pl.BlockSpec((...  3.33 us
    pallas_call x1, Pallas kernels, left_halves(): pl.pallas_call(left_kernel, grid=(steps,), in_specs=[pl.BlockSpec((3, hei...  2.3 us
    pallas_call x1, Pallas kernels, pick_cores(): pl.pallas_call(pick_kernel, in_specs=[SMEM, HBM], out_specs=[VMEM] * 3, o...  1.68 us
  transfers between devices with their start and end apart: 19, of which 10 were waited for; matrix products, arithmetic and copies ran while one was open for 0% of the time, Pallas kernels for 12%

profile of v3, /device:TPU:1, one launch (start us, length us, event | category | flops | bytes accessed | tf_op | source)
XLA Modules:
  0.0 82.6 jit_solution(7498834753976164505)
XLA Ops:
  0.0 3.3 %open_stage.1 = (f32[32,384]{1,0:T(8,128)S(1)}, bf16[1024,512]{1,0:T(8,128)(2,1)S(1)}, bf16[1024,512]{1,0:T(8,128)(2,1)S(1)}, f32[64,1024]{1,0:T(8,128)S(1)}) custom-call(s32[1]{0:T(128)} %bitcast.5.place, f32[3,1024,128]{2,1,0:T(8,128)} %right.3, f32[3,1024,128]{2,1,0:T(8,128)} %left3.1, f32[3,1024,128]{2,1,0:T(8,128)} %left3.1, f32[1024,512]{1,0:T(8,128)} %rhs.1, ...), custom_call_target="tpu_custom_call" | custom-call | flops 301989888 | bytes 4194304 | tf_op jit(solution)/shard_map/open_stage/pallas_call | solution.py:90
  3.3 6.3 %leaf_stage.1 = (f32[1024,512]{1,0:T(8,128)}, f32[256,384]{1,0:T(8,128)S(1)}, f32[256,384]{1,0:T(8,128)S(1)}) custom-call(s32[1]{0:T(128)} %bitcast.7.place, f32[1024,1024]{1,0:T(8,128)} %leaf.3, f32[3,1024,128]{2,1,0:T(8,128)} %right.3, bf16[1024,512]{1,0:T(8,128)(2,1)S(1)} %get-tuple-element.34.x_hi, bf16[1024,512]{1,0:T(8,128)(2,1)S(1)} %get-tuple-element.35.x_lo, ...), custom_call_target="tpu_custom_call" | custom-call | flops 4429185024 | bytes 8388608 | tf_op jit(solution)/shard_map/leaf_stage/pallas_call | solution.py:153
  9.7 3.3 %collective-permute-start = (f32[256,384]{1,0:T(8,128)S(1)}, f32[256,384]{1,0:T(8,128)S(1)}, u32[]{:S(2)}, u32[]{:S(2)}) collective-permute-start(f32[256,384]{1,0:T(8,128)S(1)} %get-tuple-element.38), channel_id=1, source_target_pairs={{0,4},{4,0},{8,12},{12,8},{16,20},{20,16},{24,28},{28,24},{32,36},... | collective-permute-start | bytes 1179656 | tf_op jit(solution)/shard_map/ppermute | solution.py:374
  12.9 1.3 %collective-permute-done.b = f32[256,384]{1,0:T(8,128)S(1)} collective-permute-done((f32[256,384]{1,0:T(8,128)S(1)}, f32[256,384]{1,0:T(8,128)S(1)}, u32[]{:S(2)}, u32[]{:S(2)}) %collective-permute-start) | collective-permute-done | bytes 393248 | tf_op jit(solution)/shard_map/ppermute | solution.py:374
  14.3 0.1 collective-permute-start.1
  14.4 1.5 %collective-permute-start.4 = (f32[32,384]{1,0:T(8,128)S(1)}, f32[32,384]{1,0:T(8,128)S(1)}, u32[]{:S(2)}, u32[]{:S(2)}) collective-permute-start(f32[32,384]{1,0:T(8,128)S(1)} %get-tuple-element.44.a), channel_id=1, source_target_pairs={{0,8},{4,12},{8,0},{12,4},{16,24},{20,28},{24,16},{28,20},{32,40},... | collective-permute-start | bytes 147464 | tf_op jit(solution)/shard_map/ppermute | solution.py:374
  15.9 5.7 %collective-permute-done.4.b = f32[32,384]{1,0:T(8,128)S(1)} collective-permute-done((f32[32,384]{1,0:T(8,128)S(1)}, f32[32,384]{1,0:T(8,128)S(1)}, u32[]{:S(2)}, u32[]{:S(2)}) %collective-permute-start.4) | collective-permute-done | bytes 49184 | tf_op jit(solution)/shard_map/ppermute | solution.py:374
  21.6 1.3 %collective-permute-start.5 = (f32[16,384]{1,0:T(8,128)S(1)}, f32[16,384]{1,0:T(8,128)S(1)}, u32[]{:S(2)}, u32[]{:S(2)}) collective-permute-start(f32[16,384]{1,0:T(8,128)S(1)} %get-tuple-element.46), channel_id=1, source_target_pairs={{0,4},{4,0},{8,12},{12,8},{16,20},{20,16},{24,28},{28,24},{32,36},... | collective-permute-start | bytes 73736 | tf_op jit(solution)/shard_map/ppermute | solution.py:374
  22.9 0.8 %collective-permute-done.5.b = f32[16,384]{1,0:T(8,128)S(1)} collective-permute-done((f32[16,384]{1,0:T(8,128)S(1)}, f32[16,384]{1,0:T(8,128)S(1)}, u32[]{:S(2)}, u32[]{:S(2)}) %collective-permute-start.5) | collective-permute-done | bytes 24608 | tf_op jit(solution)/shard_map/ppermute | solution.py:374
  23.7 1.5 %collective-permute-start.6 = (f32[16,384]{1,0:T(8,128)S(1)}, f32[16,384]{1,0:T(8,128)S(1)}, u32[]{:S(2)}, u32[]{:S(2)}) collective-permute-start(f32[16,384]{1,0:T(8,128)S(1)} %shard_map.59.a), channel_id=1, source_target_pairs={{0,16},{4,20},{8,24},{12,28},{16,0},{20,4},{24,8},{28,12},{32,48},... | collective-permute-start | bytes 73736 | tf_op jit(solution)/shard_map/ppermute | solution.py:374
  25.2 2.1 %collective-permute-done.6.b = f32[16,384]{1,0:T(8,128)S(1)} collective-permute-done((f32[16,384]{1,0:T(8,128)S(1)}, f32[16,384]{1,0:T(8,128)S(1)}, u32[]{:S(2)}, u32[]{:S(2)}) %collective-permute-start.6) | collective-permute-done | bytes 24608 | tf_op jit(solution)/shard_map/ppermute | solution.py:374
  27.3 3.9 %collective-permute-start.7 = (f32[16,384]{1,0:T(8,128)S(1)}, f32[16,384]{1,0:T(8,128)S(1)}, u32[]{:S(2)}, u32[]{:S(2)}) collective-permute-start(f32[16,384]{1,0:T(8,128)S(1)} %shard_map.60.a), channel_id=1, source_target_pairs={{0,56},{4,60},{8,48},{12,52},{16,40},{20,44},{24,32},{28,36},{32,2... | collective-permute-start | bytes 73736 | tf_op jit(solution)/shard_map/ppermute | solution.py:374
  31.2 0.0 collective-permute-done.1.b
  31.2 2.2 %collective-permute-start.2 = (f32[64,384]{1,0:T(8,128)S(1)}, f32[64,384]{1,0:T(8,128)S(1)}, u32[]{:S(2)}, u32[]{:S(2)}) collective-permute-start(f32[64,384]{1,0:T(8,128)S(1)} %get-tuple-element.42), channel_id=1, source_target_pairs={{0,16},{4,20},{8,24},{12,28},{16,0},{20,4},{24,8},{28,12},{32,48},... | collective-permute-start | bytes 294920 | tf_op jit(solution)/shard_map/ppermute | solution.py:374
  33.4 0.0 collective-permute-done.7.b
  33.4 2.6 %collective-permute-start.10 = (f32[16,640]{1,0:T(8,128)S(1)}, f32[16,640]{1,0:T(8,128)S(1)}, u32[]{:S(2)}, u32[]{:S(2)}) collective-permute-start(f32[16,640]{1,0:T(8,128)S(1)} %shard_map.61.refs_0_), channel_id=1, source_target_pairs={{0,3},{1,2},{2,1},{3,0},{4,7},{5,6},{6,5},{7,4},{8,11},{9,10},{10,... | collective-permute-start | bytes 122888 | tf_op jit(solution)/shard_map/ppermute | solution.py:374
  35.9 1.4 %collective-permute-start.9 = (f32[16,640]{1,0:T(8,128)S(1)}, f32[16,640]{1,0:T(8,128)S(1)}, u32[]{:S(2)}, u32[]{:S(2)}) collective-permute-start(f32[16,640]{1,0:T(8,128)S(1)} %shard_map.61.refs_0_), channel_id=1, source_target_pairs={{0,2},{1,3},{2,0},{3,1},{4,6},{5,7},{6,4},{7,5},{8,10},{9,11},{10,... | collective-permute-start | bytes 122888 | tf_op jit(solution)/shard_map/ppermute | solution.py:374
  37.3 0.3 collective-permute-done.10.refs_3_
  37.7 1.4 %collective-permute-done.8.refs_1_ = f32[16,640]{1,0:T(8,128)S(1)} collective-permute-done((f32[16,640]{1,0:T(8,128)S(1)}, f32[16,640]{1,0:T(8,128)S(1)}, u32[]{:S(2)}, u32[]{:S(2)}) %collective-permute-start.8) | collective-permute-done | bytes 40992 | tf_op jit(solution)/shard_map/ppermute | solution.py:374
  39.1 1.3 %collective-permute-done.9.refs_2_ = f32[16,640]{1,0:T(8,128)S(1)} collective-permute-done((f32[16,640]{1,0:T(8,128)S(1)}, f32[16,640]{1,0:T(8,128)S(1)}, u32[]{:S(2)}, u32[]{:S(2)}) %collective-permute-start.9) | collective-permute-done | bytes 40992 | tf_op jit(solution)/shard_map/ppermute | solution.py:374
  40.4 3.7 %collective-permute-start.11 = (f32[64,640]{1,0:T(8,128)S(1)}, f32[64,640]{1,0:T(8,128)S(1)}, u32[]{:S(2)}, u32[]{:S(2)}) collective-permute-start(f32[64,640]{1,0:T(8,128)S(1)} %shard_map.62.mine), channel_id=1, source_target_pairs={{0,4},{4,0},{8,12},{12,8},{16,20},{20,16},{24,28},{28,24},{32,36},... | collective-permute-start | bytes 491528 | tf_op jit(solution)/shard_map/ppermute | solution.py:374
  44.1 0.0 collective-permute-done.2.b
  44.1 2.3 %collective-permute-start.3 = (f32[64,384]{1,0:T(8,128)S(1)}, f32[64,384]{1,0:T(8,128)S(1)}, u32[]{:S(2)}, u32[]{:S(2)}) collective-permute-start(f32[64,384]{1,0:T(8,128)S(1)} %shard_map.57.own), channel_id=1, source_target_pairs={{0,56},{4,60},{8,48},{12,52},{16,40},{20,44},{24,32},{28,36},{32,2... | collective-permute-start | bytes 294920 | tf_op jit(solution)/shard_map/ppermute | solution.py:374
  46.4 0.1 pad_add_fusion.place
  46.5 1.7 %pick_cores.1 = (f32[256,256]{1,0:T(8,128)S(1)}, f32[256,256]{1,0:T(8,128)S(1)}, f32[256,256]{1,0:T(8,128)S(1)}) custom-call(s32[2]{0:T(128)S(1)} %pad_add_fusion.place, f32[7,256,256]{2,1,0:T(8,128)} %cores.1), custom_call_target="tpu_custom_call" | custom-call | flops 1048576 | bytes 1048576 | tf_op jit(solution)/shard_map/pick_cores/pallas_call | solution.py:203
  48.2 0.0 collective-permute-done.11.other
  48.2 1.6 %collective-permute-start.13 = (f32[128,128]{1,0:T(8,128)S(1)}, f32[128,128]{1,0:T(8,128)S(1)}, u32[]{:S(2)}, u32[]{:S(2)}) collective-permute-start(f32[128,128]{1,0:T(8,128)S(1)} %get-tuple-element.50.gram_own), channel_id=1, source_target_pairs={{0,64},{4,68},{8,72},{12,76},{16,80},{20,84},{24,88},{28,92},{32,9... | collective-permute-start | bytes 196616 | tf_op jit(solution)/shard_map/ppermute | solution.py:374
  49.8 0.0 collective-permute-done.3.oth
  49.8 0.4 shard_map.64
  50.2 1.3 %collective-permute-start.12 = (f32[64,256]{1,0:T(8,128)S(1)}, f32[64,256]{1,0:T(8,128)S(1)}, u32[]{:S(2)}, u32[]{:S(2)}) collective-permute-start(f32[64,256]{1,0:T(8,128)S(1)} %get-tuple-element.48.own), channel_id=1, source_target_pairs={{0,64},{4,68},{8,72},{12,76},{16,80},{20,84},{24,88},{28,92},{32,9... | collective-permute-start | bytes 196616 | tf_op jit(solution)/shard_map/ppermute | solution.py:374
  51.6 0.0 collective-permute-done.13.gram_oth
  51.6 1.8 %collective-permute-done.12.oth = f32[64,256]{1,0:T(8,128)S(1)} collective-permute-done((f32[64,256]{1,0:T(8,128)S(1)}, f32[64,256]{1,0:T(8,128)S(1)}, u32[]{:S(2)}, u32[]{:S(2)}) %collective-permute-start.12) | collective-permute-done | bytes 65568 | tf_op jit(solution)/shard_map/ppermute | solution.py:374
  53.5 0.4 shard_map.65
  53.9 3.0 %collective-permute-start.14 = (f32[64,128]{1,0:T(8,128)S(1)}, f32[64,128]{1,0:T(8,128)S(1)}, u32[]{:S(2)}, u32[]{:S(2)}) collective-permute-start(f32[64,128]{1,0:T(8,128)S(1)} %get-tuple-element.51.own), channel_id=1, source_target_pairs={{0,128},{4,132},{8,136},{12,140},{16,144},{20,148},{24,152},{28,15... | collective-permute-start | bytes 98312 | tf_op jit(solution)/shard_map/ppermute | solution.py:374
  56.8 1.4 %collective-permute-done.14.oth = f32[64,128]{1,0:T(8,128)S(1)} collective-permute-done((f32[64,128]{1,0:T(8,128)S(1)}, f32[64,128]{1,0:T(8,128)S(1)}, u32[]{:S(2)}, u32[]{:S(2)}) %collective-permute-start.14) | collective-permute-done | bytes 32800 | tf_op jit(solution)/shard_map/ppermute | solution.py:374
  58.2 0.3 shard_map.66.mine
  58.5 4.0 %collective-permute-start.15 = (f32[64,384]{1,0:T(8,128)S(1)}, f32[64,384]{1,0:T(8,128)S(1)}, u32[]{:S(2)}, u32[]{:S(2)}) collective-permute-start(f32[64,384]{1,0:T(8,128)S(1)} %shard_map.66.mine), channel_id=1, source_target_pairs={{0,16},{4,20},{8,24},{12,28},{16,0},{20,4},{24,8},{28,12},{32,48},... | collective-permute-start | bytes 294920 | tf_op jit(solution)/shard_map/ppermute | solution.py:374
  62.5 2.0 %collective-permute-done.15.other = f32[64,384]{1,0:T(8,128)S(1)} collective-permute-done((f32[64,384]{1,0:T(8,128)S(1)}, f32[64,384]{1,0:T(8,128)S(1)}, u32[]{:S(2)}, u32[]{:S(2)}) %collective-permute-start.15) | collective-permute-done | bytes 98336 | tf_op jit(solution)/shard_map/ppermute | solution.py:374
  64.5 2.0 %collective-permute-start.16 = (f32[128,384]{1,0:T(8,128)S(1)}, f32[128,384]{1,0:T(8,128)S(1)}, u32[]{:S(2)}, u32[]{:S(2)}) collective-permute-start(f32[128,384]{1,0:T(8,128)S(1)} %shard_map.67.c), channel_id=1, source_target_pairs={{0,8},{4,12},{8,0},{12,4},{16,24},{20,28},{24,16},{28,20},{32,40},... | collective-permute-start | bytes 589832 | tf_op jit(solution)/shard_map/ppermute | solution.py:374
  66.5 5.0 %collective-permute-start.18 = (f32[128,384]{1,0:T(8,128)S(1)}, f32[128,384]{1,0:T(8,128)S(1)}, u32[]{:S(2)}, u32[]{:S(2)}) collective-permute-start(f32[128,384]{1,0:T(8,128)S(1)} %shard_map.67.c), channel_id=1, source_target_pairs={{0,4},{4,0},{8,12},{12,8},{16,20},{20,16},{24,28},{28,24},{32,36},... | collective-permute-start | bytes 589832 | tf_op jit(solution)/shard_map/ppermute | solution.py:374
  71.5 2.3 %left_halves.1 = (bf16[1024,384]{1,0:T(8,128)(2,1)S(1)}, bf16[1024,384]{1,0:T(8,128)(2,1)S(1)}) custom-call(f32[3,1024,128]{2,1,0:T(8,128)} %left3.1), custom_call_target="tpu_custom_call" | custom-call | flops 4194304 | bytes 3145728 | tf_op jit(solution)/shard_map/left_halves/pallas_call | solution.py:179
  73.8 0.0 collective-permute-done.16.c
  73.8 1.3 %collective-permute-start.17 = (f32[128,384]{1,0:T(8,128)S(1)}, f32[128,384]{1,0:T(8,128)S(1)}, u32[]{:S(2)}, u32[]{:S(2)}) collective-permute-start(f32[128,384]{1,0:T(8,128)S(1)} %collective-permute-done.16.c), channel_id=1, source_target_pairs={{0,4},{4,0},{8,12},{12,8},{16,20},{20,16},{24,28},{28,24},{32,36},... | collective-permute-start | bytes 589832 | tf_op jit(solution)/shard_map/ppermute | solution.py:374
  75.1 0.1 pad_add_fusion.1.where
  75.2 0.0 collective-permute-done.18.c_core
  75.2 4.0 %early.1 = (f32[1024,512]{1,0:T(8,128)}, f32[1024,128]{1,0:T(8,128)S(1)}, f32[1024,128]{1,0:T(8,128)S(1)}) custom-call(s32[4]{0:T(128)S(1)} %pad_add_fusion.1.where, f32[1024,512]{1,0:T(8,128)} %get-tuple-element.55.y0, bf16[1024,384]{1,0:T(8,128)(2,1)S(1)} %get-tuple-element.32.l_hi, bf16[1024,384]{1,0:T(8,128)(2,1)S(1)} %get-tuple-element.33.l_lo, ...), custom_call_target="tpu_custom_call" | custom-call | flops 603979776 | bytes 3145728 | tf_op jit(solution)/shard_map/early/pallas_call | solution.py:343
  79.2 1.7 %shard_map.68.into = f32[1024,512]{1,0:T(8,128)} custom-call(s32[1]{0:T(128)} %bitcast.12.where, bf16[1024,384]{1,0:T(8,128)(2,1)S(1)} %get-tuple-element.32.l_hi, bf16[1024,384]{1,0:T(8,128)(2,1)S(1)} %get-tuple-element.33.l_lo, f32[128,384]{1,0:T(8,128)S(1)} %collective-permute-done.16.c, ...), custom_call_target="tpu_custom_call", output_to_operand_aliasing={{}: (5, {})} | custom-call | flops 301989888 | bytes 1048576 | tf_op jit(solution)/shard_map/pallas_call | solution.py:357
  80.9 1.7 %shard_map.69 = f32[1024,512]{1,0:T(8,128)} custom-call(s32[1]{0:T(128)} %bitcast.where, bf16[1024,384]{1,0:T(8,128)(2,1)S(1)} %get-tuple-element.32.l_hi, bf16[1024,384]{1,0:T(8,128)(2,1)S(1)} %get-tuple-element.33.l_lo, f32[128,384]{1,0:T(8,128)S(1)} %collective-permute-done.17.c, ...), custom_call_target="tpu_custom_call", output_to_operand_aliasing={{}: (5, {})} | custom-call | flops 301989888 | bytes 1048576 | tf_op jit(solution)/shard_map/pallas_call | solution.py:357
  (12 shorter events, 0.2 us)
Async XLA Ops:
  9.7 4.6 %collective-permute-start = (f32[256,384]{1,0:T(8,128)S(1)}, f32[256,384]{1,0:T(8,128)S(1)}, u32[]{:S(2)}, u32[]{:S(2)}) collective-permute-start(f32[256,384]{1,0:T(8,128)S(1)} %get-tuple-element.38), channel_id=1, source_target_pairs={{0,4},{4,0},{8,12},{12,8},{16,20},{20,16},{24,28},{28,24},{32,36},... | collective-permute-start | bytes 1179656 | tf_op jit(solution)/shard_map/ppermute | solution.py:374
  14.3 16.9 %collective-permute-start.1 = (f32[128,384]{1,0:T(8,128)S(1)}, f32[128,384]{1,0:T(8,128)S(1)}, u32[]{:S(2)}, u32[]{:S(2)}) collective-permute-start(f32[128,384]{1,0:T(8,128)S(1)} %get-tuple-element.40), channel_id=1, source_target_pairs={{0,8},{4,12},{8,0},{12,4},{16,24},{20,28},{24,16},{28,20},{32,40},... | collective-permute-start | bytes 589832 | tf_op jit(solution)/shard_map/ppermute | solution.py:374
  14.4 7.1 %collective-permute-start.4 = (f32[32,384]{1,0:T(8,128)S(1)}, f32[32,384]{1,0:T(8,128)S(1)}, u32[]{:S(2)}, u32[]{:S(2)}) collective-permute-start(f32[32,384]{1,0:T(8,128)S(1)} %get-tuple-element.44.a), channel_id=1, source_target_pairs={{0,8},{4,12},{8,0},{12,4},{16,24},{20,28},{24,16},{28,20},{32,40},... | collective-permute-start | bytes 147464 | tf_op jit(solution)/shard_map/ppermute | solution.py:374
  21.6 2.2 %collective-permute-start.5 = (f32[16,384]{1,0:T(8,128)S(1)}, f32[16,384]{1,0:T(8,128)S(1)}, u32[]{:S(2)}, u32[]{:S(2)}) collective-permute-start(f32[16,384]{1,0:T(8,128)S(1)} %get-tuple-element.46), channel_id=1, source_target_pairs={{0,4},{4,0},{8,12},{12,8},{16,20},{20,16},{24,28},{28,24},{32,36},... | collective-permute-start | bytes 73736 | tf_op jit(solution)/shard_map/ppermute | solution.py:374
  23.7 3.6 %collective-permute-start.6 = (f32[16,384]{1,0:T(8,128)S(1)}, f32[16,384]{1,0:T(8,128)S(1)}, u32[]{:S(2)}, u32[]{:S(2)}) collective-permute-start(f32[16,384]{1,0:T(8,128)S(1)} %shard_map.59.a), channel_id=1, source_target_pairs={{0,16},{4,20},{8,24},{12,28},{16,0},{20,4},{24,8},{28,12},{32,48},... | collective-permute-start | bytes 73736 | tf_op jit(solution)/shard_map/ppermute | solution.py:374
  27.3 6.1 %collective-permute-start.7 = (f32[16,384]{1,0:T(8,128)S(1)}, f32[16,384]{1,0:T(8,128)S(1)}, u32[]{:S(2)}, u32[]{:S(2)}) collective-permute-start(f32[16,384]{1,0:T(8,128)S(1)} %shard_map.60.a), channel_id=1, source_target_pairs={{0,56},{4,60},{8,48},{12,52},{16,40},{20,44},{24,32},{28,36},{32,2... | collective-permute-start | bytes 73736 | tf_op jit(solution)/shard_map/ppermute | solution.py:374
  31.2 12.9 %collective-permute-start.2 = (f32[64,384]{1,0:T(8,128)S(1)}, f32[64,384]{1,0:T(8,128)S(1)}, u32[]{:S(2)}, u32[]{:S(2)}) collective-permute-start(f32[64,384]{1,0:T(8,128)S(1)} %get-tuple-element.42), channel_id=1, source_target_pairs={{0,16},{4,20},{8,24},{12,28},{16,0},{20,4},{24,8},{28,12},{32,48},... | collective-permute-start | bytes 294920 | tf_op jit(solution)/shard_map/ppermute | solution.py:374
  33.4 4.3 %collective-permute-start.10 = (f32[16,640]{1,0:T(8,128)S(1)}, f32[16,640]{1,0:T(8,128)S(1)}, u32[]{:S(2)}, u32[]{:S(2)}) collective-permute-start(f32[16,640]{1,0:T(8,128)S(1)} %shard_map.61.refs_0_), channel_id=1, source_target_pairs={{0,3},{1,2},{2,1},{3,0},{4,7},{5,6},{6,5},{7,4},{8,11},{9,10},{10,... | collective-permute-start | bytes 122888 | tf_op jit(solution)/shard_map/ppermute | solution.py:374
  35.9 3.1 %collective-permute-start.8 = (f32[16,640]{1,0:T(8,128)S(1)}, f32[16,640]{1,0:T(8,128)S(1)}, u32[]{:S(2)}, u32[]{:S(2)}) collective-permute-start(f32[16,640]{1,0:T(8,128)S(1)} %shard_map.61.refs_0_), channel_id=1, source_target_pairs={{0,1},{1,0},{2,3},{3,2},{4,5},{5,4},{6,7},{7,6},{8,9},{9,8},{10,11... | collective-permute-start | bytes 122888 | tf_op jit(solution)/shard_map/ppermute | solution.py:374
  35.9 4.5 %collective-permute-start.9 = (f32[16,640]{1,0:T(8,128)S(1)}, f32[16,640]{1,0:T(8,128)S(1)}, u32[]{:S(2)}, u32[]{:S(2)}) collective-permute-start(f32[16,640]{1,0:T(8,128)S(1)} %shard_map.61.refs_0_), channel_id=1, source_target_pairs={{0,2},{1,3},{2,0},{3,1},{4,6},{5,7},{6,4},{7,5},{8,10},{9,11},{10,... | collective-permute-start | bytes 122888 | tf_op jit(solution)/shard_map/ppermute | solution.py:374
  40.4 7.8 %collective-permute-start.11 = (f32[64,640]{1,0:T(8,128)S(1)}, f32[64,640]{1,0:T(8,128)S(1)}, u32[]{:S(2)}, u32[]{:S(2)}) collective-permute-start(f32[64,640]{1,0:T(8,128)S(1)} %shard_map.62.mine), channel_id=1, source_target_pairs={{0,4},{4,0},{8,12},{12,8},{16,20},{20,16},{24,28},{28,24},{32,36},... | collective-permute-start | bytes 491528 | tf_op jit(solution)/shard_map/ppermute | solution.py:374
  44.1 5.7 %collective-permute-start.3 = (f32[64,384]{1,0:T(8,128)S(1)}, f32[64,384]{1,0:T(8,128)S(1)}, u32[]{:S(2)}, u32[]{:S(2)}) collective-permute-start(f32[64,384]{1,0:T(8,128)S(1)} %shard_map.57.own), channel_id=1, source_target_pairs={{0,56},{4,60},{8,48},{12,52},{16,40},{20,44},{24,32},{28,36},{32,2... | collective-permute-start | bytes 294920 | tf_op jit(solution)/shard_map/ppermute | solution.py:374
  48.2 3.4 %collective-permute-start.13 = (f32[128,128]{1,0:T(8,128)S(1)}, f32[128,128]{1,0:T(8,128)S(1)}, u32[]{:S(2)}, u32[]{:S(2)}) collective-permute-start(f32[128,128]{1,0:T(8,128)S(1)} %get-tuple-element.50.gram_own), channel_id=1, source_target_pairs={{0,64},{4,68},{8,72},{12,76},{16,80},{20,84},{24,88},{28,92},{32,9... | collective-permute-start | bytes 196616 | tf_op jit(solution)/shard_map/ppermute | solution.py:374
  50.2 3.2 %collective-permute-start.12 = (f32[64,256]{1,0:T(8,128)S(1)}, f32[64,256]{1,0:T(8,128)S(1)}, u32[]{:S(2)}, u32[]{:S(2)}) collective-permute-start(f32[64,256]{1,0:T(8,128)S(1)} %get-tuple-element.48.own), channel_id=1, source_target_pairs={{0,64},{4,68},{8,72},{12,76},{16,80},{20,84},{24,88},{28,92},{32,9... | collective-permute-start | bytes 196616 | tf_op jit(solution)/shard_map/ppermute | solution.py:374
  53.9 4.4 %collective-permute-start.14 = (f32[64,128]{1,0:T(8,128)S(1)}, f32[64,128]{1,0:T(8,128)S(1)}, u32[]{:S(2)}, u32[]{:S(2)}) collective-permute-start(f32[64,128]{1,0:T(8,128)S(1)} %get-tuple-element.51.own), channel_id=1, source_target_pairs={{0,128},{4,132},{8,136},{12,140},{16,144},{20,148},{24,152},{28,15... | collective-permute-start | bytes 98312 | tf_op jit(solution)/shard_map/ppermute | solution.py:374
  58.5 6.0 %collective-permute-start.15 = (f32[64,384]{1,0:T(8,128)S(1)}, f32[64,384]{1,0:T(8,128)S(1)}, u32[]{:S(2)}, u32[]{:S(2)}) collective-permute-start(f32[64,384]{1,0:T(8,128)S(1)} %shard_map.66.mine), channel_id=1, source_target_pairs={{0,16},{4,20},{8,24},{12,28},{16,0},{20,4},{24,8},{28,12},{32,48},... | collective-permute-start | bytes 294920 | tf_op jit(solution)/shard_map/ppermute | solution.py:374
  64.5 9.3 %collective-permute-start.16 = (f32[128,384]{1,0:T(8,128)S(1)}, f32[128,384]{1,0:T(8,128)S(1)}, u32[]{:S(2)}, u32[]{:S(2)}) collective-permute-start(f32[128,384]{1,0:T(8,128)S(1)} %shard_map.67.c), channel_id=1, source_target_pairs={{0,8},{4,12},{8,0},{12,4},{16,24},{20,28},{24,16},{28,20},{32,40},... | collective-permute-start | bytes 589832 | tf_op jit(solution)/shard_map/ppermute | solution.py:374
  66.5 8.7 %collective-permute-start.18 = (f32[128,384]{1,0:T(8,128)S(1)}, f32[128,384]{1,0:T(8,128)S(1)}, u32[]{:S(2)}, u32[]{:S(2)}) collective-permute-start(f32[128,384]{1,0:T(8,128)S(1)} %shard_map.67.c), channel_id=1, source_target_pairs={{0,4},{4,0},{8,12},{12,8},{16,20},{20,16},{24,28},{28,24},{32,36},... | collective-permute-start | bytes 589832 | tf_op jit(solution)/shard_map/ppermute | solution.py:374
  73.8 7.1 %collective-permute-start.17 = (f32[128,384]{1,0:T(8,128)S(1)}, f32[128,384]{1,0:T(8,128)S(1)}, u32[]{:S(2)}, u32[]{:S(2)}) collective-permute-start(f32[128,384]{1,0:T(8,128)S(1)} %collective-permute-done.16.c), channel_id=1, source_target_pairs={{0,4},{4,0},{8,12},{12,8},{16,20},{20,16},{24,28},{28,24},{32,36},... | collective-permute-start | bytes 589832 | tf_op jit(solution)/shard_map/ppermute | solution.py:374

commit v4 on v3

--- a/solution.py
+++ b/solution.py
@@ -321,14 +321,24 @@
 
     targets = given.at[0], given.at[1], ahead_a, ahead_b
     loads = [pltpu.make_async_copy(columns(y0, k), target, sems.at[k]) for k, target in enumerate(targets)]
-    stores = [pltpu.make_async_copy(made.at[k], columns(out, k), sems.at[4 + k]) for k in range(2)]
     for load in loads:
         load.start()
-    for k, chunk in enumerate((c, c_core)):
-        fix = dot3((l_hi[...], l_lo[...]), split(chunk[...]), NT)
-        loads[k].wait()
-        made[k] = given[k] - fix
-        stores[k].start()
+    both = split(jnp.concatenate([c[...], c_core[...]], axis=0))
+    half = LEAF // 2
+    stores = []
+    for h in range(2):
+        rows = slice(h * half, (h + 1) * half)
+        fix = dot3((l_hi[rows, :], l_lo[rows, :]), both, NT)
+        for k in range(2):
+            if h == 0:
+                loads[k].wait()
+            made[k, rows, :] = given[k, rows, :] - fix[:, k * RANK : (k + 1) * RANK]
+            start = pl.multiple_of(where[k] * RANK, RANK)
+            store = pltpu.make_async_copy(
+                made.at[k, rows, :], out.at[rows, pl.ds(start, RANK)], sems.at[4 + 2 * h + k]
+            )
+            store.start()
+            stores.append(store)
     for copy in loads[2:] + stores:
         copy.wait()
 
@@ -345,7 +355,7 @@
         in_specs=[SMEM, HBM] + [VMEM] * 4,
         out_specs=[HBM, VMEM, VMEM],
         out_shape=[far(LEAF, COLS)] + [f32(LEAF, RANK)] * 2,
-        scratch_shapes=[pltpu.VMEM((2, LEAF, RANK), jnp.float32)] * 2 + [pltpu.SemaphoreType.DMA((6,))],
+        scratch_shapes=[pltpu.VMEM((2, LEAF, RANK), jnp.float32)] * 2 + [pltpu.SemaphoreType.DMA((8,))],
         compiler_params=params(12),
         cost_estimate=cost(12 * LEAF * 3 * RANK * RANK, 3 << 20),
         name="early",

time: 82.7 us -> 82.5 us (level)
  no operation moved by 1% of the time
where the time goes in v4:
time: 82.5 us; the launch traced here: 82.3 us
  starting transfers between devices  41.7 us (51%)
  Pallas kernels  22 us (27%)
  waiting for transfers between devices  18.4 us (22%)
    ppermute x19, starting transfers between devices, swapped(): return lax.ppermute(x, axis, [(i, i ^ mask) for i in range(size)])  41.7 us
    ppermute x19, waiting for transfers between devices, swapped(): return lax.ppermute(x, axis, [(i, i ^ mask) for i in range(size)])  18.4 us
    pallas_call x1, Pallas kernels, leaf_stage(): pl.pallas_call(leaf_kernel, in_specs=[SMEM, HBM, HBM, VMEM, VMEM, VMEM],...  6.31 us
    pallas_call x1, Pallas kernels, early_corrections(): pl.pallas_call(early_kernel, in_specs=[SMEM, HBM] + [VMEM] * 4, out_specs...  3.73 us
    pallas_call x2, Pallas kernels, late_correction(): pl.pallas_call(late_kernel, grid_spec=pltpu.PrefetchScalarGridSpec(num_sc...  3.36 us
    pallas_call x1, Pallas kernels, open_stage(): pl.pallas_call(open_kernel, grid=(steps,), in_specs=[SMEM, pl.BlockSpec((...  3.33 us
    pallas_call x1, Pallas kernels, left_halves(): pl.pallas_call(left_kernel, grid=(steps,), in_specs=[pl.BlockSpec((3, hei...  2.3 us
    pallas_call x1, Pallas kernels, pick_cores(): pl.pallas_call(pick_kernel, in_specs=[SMEM, HBM], out_specs=[VMEM] * 3, o...  1.68 us
  transfers between devices with their start and end apart: 19, of which 10 were waited for; matrix products, arithmetic and copies ran while one was open for 0% of the time, Pallas kernels for 12%

profile of v4, /device:TPU:1, one launch (start us, length us, event | category | flops | bytes accessed | tf_op | source)
XLA Modules:
  0.0 82.3 jit_solution(4995239736065039840)
XLA Ops:
  0.0 3.3 %open_stage.1 = (f32[32,384]{1,0:T(8,128)S(1)}, bf16[1024,512]{1,0:T(8,128)(2,1)S(1)}, bf16[1024,512]{1,0:T(8,128)(2,1)S(1)}, f32[64,1024]{1,0:T(8,128)S(1)}) custom-call(s32[1]{0:T(128)} %bitcast.5.place, f32[3,1024,128]{2,1,0:T(8,128)} %right.3, f32[3,1024,128]{2,1,0:T(8,128)} %left3.1, f32[3,1024,128]{2,1,0:T(8,128)} %left3.1, f32[1024,512]{1,0:T(8,128)} %rhs.1, ...), custom_call_target="tpu_custom_call" | custom-call | flops 301989888 | bytes 4194304 | tf_op jit(solution)/shard_map/open_stage/pallas_call | solution.py:90
  3.3 6.3 %leaf_stage.1 = (f32[1024,512]{1,0:T(8,128)}, f32[256,384]{1,0:T(8,128)S(1)}, f32[256,384]{1,0:T(8,128)S(1)}) custom-call(s32[1]{0:T(128)} %bitcast.7.place, f32[1024,1024]{1,0:T(8,128)} %leaf.3, f32[3,1024,128]{2,1,0:T(8,128)} %right.3, bf16[1024,512]{1,0:T(8,128)(2,1)S(1)} %get-tuple-element.34.x_hi, bf16[1024,512]{1,0:T(8,128)(2,1)S(1)} %get-tuple-element.35.x_lo, ...), custom_call_target="tpu_custom_call" | custom-call | flops 4429185024 | bytes 8388608 | tf_op jit(solution)/shard_map/leaf_stage/pallas_call | solution.py:153
  9.7 3.3 %collective-permute-start = (f32[256,384]{1,0:T(8,128)S(1)}, f32[256,384]{1,0:T(8,128)S(1)}, u32[]{:S(2)}, u32[]{:S(2)}) collective-permute-start(f32[256,384]{1,0:T(8,128)S(1)} %get-tuple-element.38), channel_id=1, source_target_pairs={{0,4},{4,0},{8,12},{12,8},{16,20},{20,16},{24,28},{28,24},{32,36},... | collective-permute-start | bytes 1179656 | tf_op jit(solution)/shard_map/ppermute | solution.py:384
  12.9 1.3 %collective-permute-done.b = f32[256,384]{1,0:T(8,128)S(1)} collective-permute-done((f32[256,384]{1,0:T(8,128)S(1)}, f32[256,384]{1,0:T(8,128)S(1)}, u32[]{:S(2)}, u32[]{:S(2)}) %collective-permute-start) | collective-permute-done | bytes 393248 | tf_op jit(solution)/shard_map/ppermute | solution.py:384
  14.3 0.1 collective-permute-start.1
  14.4 1.5 %collective-permute-start.4 = (f32[32,384]{1,0:T(8,128)S(1)}, f32[32,384]{1,0:T(8,128)S(1)}, u32[]{:S(2)}, u32[]{:S(2)}) collective-permute-start(f32[32,384]{1,0:T(8,128)S(1)} %get-tuple-element.44.a), channel_id=1, source_target_pairs={{0,8},{4,12},{8,0},{12,4},{16,24},{20,28},{24,16},{28,20},{32,40},... | collective-permute-start | bytes 147464 | tf_op jit(solution)/shard_map/ppermute | solution.py:384
  15.9 5.7 %collective-permute-done.4.b = f32[32,384]{1,0:T(8,128)S(1)} collective-permute-done((f32[32,384]{1,0:T(8,128)S(1)}, f32[32,384]{1,0:T(8,128)S(1)}, u32[]{:S(2)}, u32[]{:S(2)}) %collective-permute-start.4) | collective-permute-done | bytes 49184 | tf_op jit(solution)/shard_map/ppermute | solution.py:384
  21.6 1.3 %collective-permute-start.5 = (f32[16,384]{1,0:T(8,128)S(1)}, f32[16,384]{1,0:T(8,128)S(1)}, u32[]{:S(2)}, u32[]{:S(2)}) collective-permute-start(f32[16,384]{1,0:T(8,128)S(1)} %get-tuple-element.46), channel_id=1, source_target_pairs={{0,4},{4,0},{8,12},{12,8},{16,20},{20,16},{24,28},{28,24},{32,36},... | collective-permute-start | bytes 73736 | tf_op jit(solution)/shard_map/ppermute | solution.py:384
  22.9 0.8 %collective-permute-done.5.b = f32[16,384]{1,0:T(8,128)S(1)} collective-permute-done((f32[16,384]{1,0:T(8,128)S(1)}, f32[16,384]{1,0:T(8,128)S(1)}, u32[]{:S(2)}, u32[]{:S(2)}) %collective-permute-start.5) | collective-permute-done | bytes 24608 | tf_op jit(solution)/shard_map/ppermute | solution.py:384
  23.7 1.5 %collective-permute-start.6 = (f32[16,384]{1,0:T(8,128)S(1)}, f32[16,384]{1,0:T(8,128)S(1)}, u32[]{:S(2)}, u32[]{:S(2)}) collective-permute-start(f32[16,384]{1,0:T(8,128)S(1)} %shard_map.59.a), channel_id=1, source_target_pairs={{0,16},{4,20},{8,24},{12,28},{16,0},{20,4},{24,8},{28,12},{32,48},... | collective-permute-start | bytes 73736 | tf_op jit(solution)/shard_map/ppermute | solution.py:384
  25.2 2.1 %collective-permute-done.6.b = f32[16,384]{1,0:T(8,128)S(1)} collective-permute-done((f32[16,384]{1,0:T(8,128)S(1)}, f32[16,384]{1,0:T(8,128)S(1)}, u32[]{:S(2)}, u32[]{:S(2)}) %collective-permute-start.6) | collective-permute-done | bytes 24608 | tf_op jit(solution)/shard_map/ppermute | solution.py:384
  27.3 3.9 %collective-permute-start.7 = (f32[16,384]{1,0:T(8,128)S(1)}, f32[16,384]{1,0:T(8,128)S(1)}, u32[]{:S(2)}, u32[]{:S(2)}) collective-permute-start(f32[16,384]{1,0:T(8,128)S(1)} %shard_map.60.a), channel_id=1, source_target_pairs={{0,56},{4,60},{8,48},{12,52},{16,40},{20,44},{24,32},{28,36},{32,2... | collective-permute-start | bytes 73736 | tf_op jit(solution)/shard_map/ppermute | solution.py:384
  31.2 0.0 collective-permute-done.1.b
  31.2 2.2 %collective-permute-start.2 = (f32[64,384]{1,0:T(8,128)S(1)}, f32[64,384]{1,0:T(8,128)S(1)}, u32[]{:S(2)}, u32[]{:S(2)}) collective-permute-start(f32[64,384]{1,0:T(8,128)S(1)} %get-tuple-element.42), channel_id=1, source_target_pairs={{0,16},{4,20},{8,24},{12,28},{16,0},{20,4},{24,8},{28,12},{32,48},... | collective-permute-start | bytes 294920 | tf_op jit(solution)/shard_map/ppermute | solution.py:384
  33.4 0.0 collective-permute-done.7.b
  33.4 2.6 %collective-permute-start.10 = (f32[16,640]{1,0:T(8,128)S(1)}, f32[16,640]{1,0:T(8,128)S(1)}, u32[]{:S(2)}, u32[]{:S(2)}) collective-permute-start(f32[16,640]{1,0:T(8,128)S(1)} %shard_map.61.refs_0_), channel_id=1, source_target_pairs={{0,3},{1,2},{2,1},{3,0},{4,7},{5,6},{6,5},{7,4},{8,11},{9,10},{10,... | collective-permute-start | bytes 122888 | tf_op jit(solution)/shard_map/ppermute | solution.py:384
  35.9 1.4 %collective-permute-start.9 = (f32[16,640]{1,0:T(8,128)S(1)}, f32[16,640]{1,0:T(8,128)S(1)}, u32[]{:S(2)}, u32[]{:S(2)}) collective-permute-start(f32[16,640]{1,0:T(8,128)S(1)} %shard_map.61.refs_0_), channel_id=1, source_target_pairs={{0,2},{1,3},{2,0},{3,1},{4,6},{5,7},{6,4},{7,5},{8,10},{9,11},{10,... | collective-permute-start | bytes 122888 | tf_op jit(solution)/shard_map/ppermute | solution.py:384
  37.3 0.3 collective-permute-done.10.refs_3_
  37.7 1.4 %collective-permute-done.8.refs_1_ = f32[16,640]{1,0:T(8,128)S(1)} collective-permute-done((f32[16,640]{1,0:T(8,128)S(1)}, f32[16,640]{1,0:T(8,128)S(1)}, u32[]{:S(2)}, u32[]{:S(2)}) %collective-permute-start.8) | collective-permute-done | bytes 40992 | tf_op jit(solution)/shard_map/ppermute | solution.py:384
  39.1 1.3 %collective-permute-done.9.refs_2_ = f32[16,640]{1,0:T(8,128)S(1)} collective-permute-done((f32[16,640]{1,0:T(8,128)S(1)}, f32[16,640]{1,0:T(8,128)S(1)}, u32[]{:S(2)}, u32[]{:S(2)}) %collective-permute-start.9) | collective-permute-done | bytes 40992 | tf_op jit(solution)/shard_map/ppermute | solution.py:384
  40.4 3.7 %collective-permute-start.11 = (f32[64,640]{1,0:T(8,128)S(1)}, f32[64,640]{1,0:T(8,128)S(1)}, u32[]{:S(2)}, u32[]{:S(2)}) collective-permute-start(f32[64,640]{1,0:T(8,128)S(1)} %shard_map.62.mine), channel_id=1, source_target_pairs={{0,4},{4,0},{8,12},{12,8},{16,20},{20,16},{24,28},{28,24},{32,36},... | collective-permute-start | bytes 491528 | tf_op jit(solution)/shard_map/ppermute | solution.py:384
  44.1 0.0 collective-permute-done.2.b
  44.1 2.3 %collective-permute-start.3 = (f32[64,384]{1,0:T(8,128)S(1)}, f32[64,384]{1,0:T(8,128)S(1)}, u32[]{:S(2)}, u32[]{:S(2)}) collective-permute-start(f32[64,384]{1,0:T(8,128)S(1)} %shard_map.57.own), channel_id=1, source_target_pairs={{0,56},{4,60},{8,48},{12,52},{16,40},{20,44},{24,32},{28,36},{32,2... | collective-permute-start | bytes 294920 | tf_op jit(solution)/shard_map/ppermute | solution.py:384
  46.4 0.1 pad_add_fusion.place
  46.5 1.7 %pick_cores.1 = (f32[256,256]{1,0:T(8,128)S(1)}, f32[256,256]{1,0:T(8,128)S(1)}, f32[256,256]{1,0:T(8,128)S(1)}) custom-call(s32[2]{0:T(128)S(1)} %pad_add_fusion.place, f32[7,256,256]{2,1,0:T(8,128)} %cores.1), custom_call_target="tpu_custom_call" | custom-call | flops 1048576 | bytes 1048576 | tf_op jit(solution)/shard_map/pick_cores/pallas_call | solution.py:203
  48.2 0.0 collective-permute-done.11.other
  48.2 1.6 %collective-permute-start.13 = (f32[128,128]{1,0:T(8,128)S(1)}, f32[128,128]{1,0:T(8,128)S(1)}, u32[]{:S(2)}, u32[]{:S(2)}) collective-permute-start(f32[128,128]{1,0:T(8,128)S(1)} %get-tuple-element.50.gram_own), channel_id=1, source_target_pairs={{0,64},{4,68},{8,72},{12,76},{16,80},{20,84},{24,88},{28,92},{32,9... | collective-permute-start | bytes 196616 | tf_op jit(solution)/shard_map/ppermute | solution.py:384
  49.8 0.0 collective-permute-done.3.oth
  49.8 0.4 shard_map.64
  50.2 1.3 %collective-permute-start.12 = (f32[64,256]{1,0:T(8,128)S(1)}, f32[64,256]{1,0:T(8,128)S(1)}, u32[]{:S(2)}, u32[]{:S(2)}) collective-permute-start(f32[64,256]{1,0:T(8,128)S(1)} %get-tuple-element.48.own), channel_id=1, source_target_pairs={{0,64},{4,68},{8,72},{12,76},{16,80},{20,84},{24,88},{28,92},{32,9... | collective-permute-start | bytes 196616 | tf_op jit(solution)/shard_map/ppermute | solution.py:384
  51.6 0.0 collective-permute-done.13.gram_oth
  51.6 1.8 %collective-permute-done.12.oth = f32[64,256]{1,0:T(8,128)S(1)} collective-permute-done((f32[64,256]{1,0:T(8,128)S(1)}, f32[64,256]{1,0:T(8,128)S(1)}, u32[]{:S(2)}, u32[]{:S(2)}) %collective-permute-start.12) | collective-permute-done | bytes 65568 | tf_op jit(solution)/shard_map/ppermute | solution.py:384
  53.5 0.4 shard_map.65
  53.9 3.0 %collective-permute-start.14 = (f32[64,128]{1,0:T(8,128)S(1)}, f32[64,128]{1,0:T(8,128)S(1)}, u32[]{:S(2)}, u32[]{:S(2)}) collective-permute-start(f32[64,128]{1,0:T(8,128)S(1)} %get-tuple-element.51.own), channel_id=1, source_target_pairs={{0,128},{4,132},{8,136},{12,140},{16,144},{20,148},{24,152},{28,15... | collective-permute-start | bytes 98312 | tf_op jit(solution)/shard_map/ppermute | solution.py:384
  56.8 1.4 %collective-permute-done.14.oth = f32[64,128]{1,0:T(8,128)S(1)} collective-permute-done((f32[64,128]{1,0:T(8,128)S(1)}, f32[64,128]{1,0:T(8,128)S(1)}, u32[]{:S(2)}, u32[]{:S(2)}) %collective-permute-start.14) | collective-permute-done | bytes 32800 | tf_op jit(solution)/shard_map/ppermute | solution.py:384
  58.2 0.3 shard_map.66.mine
  58.5 4.0 %collective-permute-start.15 = (f32[64,384]{1,0:T(8,128)S(1)}, f32[64,384]{1,0:T(8,128)S(1)}, u32[]{:S(2)}, u32[]{:S(2)}) collective-permute-start(f32[64,384]{1,0:T(8,128)S(1)} %shard_map.66.mine), channel_id=1, source_target_pairs={{0,16},{4,20},{8,24},{12,28},{16,0},{20,4},{24,8},{28,12},{32,48},... | collective-permute-start | bytes 294920 | tf_op jit(solution)/shard_map/ppermute | solution.py:384
  62.5 2.0 %collective-permute-done.15.other = f32[64,384]{1,0:T(8,128)S(1)} collective-permute-done((f32[64,384]{1,0:T(8,128)S(1)}, f32[64,384]{1,0:T(8,128)S(1)}, u32[]{:S(2)}, u32[]{:S(2)}) %collective-permute-start.15) | collective-permute-done | bytes 98336 | tf_op jit(solution)/shard_map/ppermute | solution.py:384
  64.5 2.0 %collective-permute-start.16 = (f32[128,384]{1,0:T(8,128)S(1)}, f32[128,384]{1,0:T(8,128)S(1)}, u32[]{:S(2)}, u32[]{:S(2)}) collective-permute-start(f32[128,384]{1,0:T(8,128)S(1)} %shard_map.67.c), channel_id=1, source_target_pairs={{0,8},{4,12},{8,0},{12,4},{16,24},{20,28},{24,16},{28,20},{32,40},... | collective-permute-start | bytes 589832 | tf_op jit(solution)/shard_map/ppermute | solution.py:384
  66.5 5.0 %collective-permute-start.18 = (f32[128,384]{1,0:T(8,128)S(1)}, f32[128,384]{1,0:T(8,128)S(1)}, u32[]{:S(2)}, u32[]{:S(2)}) collective-permute-start(f32[128,384]{1,0:T(8,128)S(1)} %shard_map.67.c), channel_id=1, source_target_pairs={{0,4},{4,0},{8,12},{12,8},{16,20},{20,16},{24,28},{28,24},{32,36},... | collective-permute-start | bytes 589832 | tf_op jit(solution)/shard_map/ppermute | solution.py:384
  71.5 2.3 %left_halves.1 = (bf16[1024,384]{1,0:T(8,128)(2,1)S(1)}, bf16[1024,384]{1,0:T(8,128)(2,1)S(1)}) custom-call(f32[3,1024,128]{2,1,0:T(8,128)} %left3.1), custom_call_target="tpu_custom_call" | custom-call | flops 4194304 | bytes 3145728 | tf_op jit(solution)/shard_map/left_halves/pallas_call | solution.py:179
  73.8 0.0 collective-permute-done.16.c
  73.8 1.3 %collective-permute-start.17 = (f32[128,384]{1,0:T(8,128)S(1)}, f32[128,384]{1,0:T(8,128)S(1)}, u32[]{:S(2)}, u32[]{:S(2)}) collective-permute-start(f32[128,384]{1,0:T(8,128)S(1)} %collective-permute-done.16.c), channel_id=1, source_target_pairs={{0,4},{4,0},{8,12},{12,8},{16,20},{20,16},{24,28},{28,24},{32,36},... | collective-permute-start | bytes 589832 | tf_op jit(solution)/shard_map/ppermute | solution.py:384
  75.1 0.1 pad_add_fusion.1.where
  75.2 0.0 collective-permute-done.18.c_core
  75.2 3.7 %early.1 = (f32[1024,512]{1,0:T(8,128)}, f32[1024,128]{1,0:T(8,128)S(1)}, f32[1024,128]{1,0:T(8,128)S(1)}) custom-call(s32[4]{0:T(128)S(1)} %pad_add_fusion.1.where, f32[1024,512]{1,0:T(8,128)} %get-tuple-element.55.y0, bf16[1024,384]{1,0:T(8,128)(2,1)S(1)} %get-tuple-element.32.l_hi, bf16[1024,384]{1,0:T(8,128)(2,1)S(1)} %get-tuple-element.33.l_lo, ...), custom_call_target="tpu_custom_call" | custom-call | flops 603979776 | bytes 3145728 | tf_op jit(solution)/shard_map/early/pallas_call | solution.py:353
  79.0 1.7 %shard_map.68.into = f32[1024,512]{1,0:T(8,128)} custom-call(s32[1]{0:T(128)} %bitcast.12.where, bf16[1024,384]{1,0:T(8,128)(2,1)S(1)} %get-tuple-element.32.l_hi, bf16[1024,384]{1,0:T(8,128)(2,1)S(1)} %get-tuple-element.33.l_lo, f32[128,384]{1,0:T(8,128)S(1)} %collective-permute-done.16.c, ...), custom_call_target="tpu_custom_call", output_to_operand_aliasing={{}: (5, {})} | custom-call | flops 301989888 | bytes 1048576 | tf_op jit(solution)/shard_map/pallas_call | solution.py:367
  80.7 1.7 %shard_map.69 = f32[1024,512]{1,0:T(8,128)} custom-call(s32[1]{0:T(128)} %bitcast.where, bf16[1024,384]{1,0:T(8,128)(2,1)S(1)} %get-tuple-element.32.l_hi, bf16[1024,384]{1,0:T(8,128)(2,1)S(1)} %get-tuple-element.33.l_lo, f32[128,384]{1,0:T(8,128)S(1)} %collective-permute-done.17.c, ...), custom_call_target="tpu_custom_call", output_to_operand_aliasing={{}: (5, {})} | custom-call | flops 301989888 | bytes 1048576 | tf_op jit(solution)/shard_map/pallas_call | solution.py:367
  (12 shorter events, 0.2 us)
Async XLA Ops:
  9.7 4.6 %collective-permute-start = (f32[256,384]{1,0:T(8,128)S(1)}, f32[256,384]{1,0:T(8,128)S(1)}, u32[]{:S(2)}, u32[]{:S(2)}) collective-permute-start(f32[256,384]{1,0:T(8,128)S(1)} %get-tuple-element.38), channel_id=1, source_target_pairs={{0,4},{4,0},{8,12},{12,8},{16,20},{20,16},{24,28},{28,24},{32,36},... | collective-permute-start | bytes 1179656 | tf_op jit(solution)/shard_map/ppermute | solution.py:384
  14.3 16.9 %collective-permute-start.1 = (f32[128,384]{1,0:T(8,128)S(1)}, f32[128,384]{1,0:T(8,128)S(1)}, u32[]{:S(2)}, u32[]{:S(2)}) collective-permute-start(f32[128,384]{1,0:T(8,128)S(1)} %get-tuple-element.40), channel_id=1, source_target_pairs={{0,8},{4,12},{8,0},{12,4},{16,24},{20,28},{24,16},{28,20},{32,40},... | collective-permute-start | bytes 589832 | tf_op jit(solution)/shard_map/ppermute | solution.py:384
  14.4 7.1 %collective-permute-start.4 = (f32[32,384]{1,0:T(8,128)S(1)}, f32[32,384]{1,0:T(8,128)S(1)}, u32[]{:S(2)}, u32[]{:S(2)}) collective-permute-start(f32[32,384]{1,0:T(8,128)S(1)} %get-tuple-element.44.a), channel_id=1, source_target_pairs={{0,8},{4,12},{8,0},{12,4},{16,24},{20,28},{24,16},{28,20},{32,40},... | collective-permute-start | bytes 147464 | tf_op jit(solution)/shard_map/ppermute | solution.py:384
  21.6 2.2 %collective-permute-start.5 = (f32[16,384]{1,0:T(8,128)S(1)}, f32[16,384]{1,0:T(8,128)S(1)}, u32[]{:S(2)}, u32[]{:S(2)}) collective-permute-start(f32[16,384]{1,0:T(8,128)S(1)} %get-tuple-element.46), channel_id=1, source_target_pairs={{0,4},{4,0},{8,12},{12,8},{16,20},{20,16},{24,28},{28,24},{32,36},... | collective-permute-start | bytes 73736 | tf_op jit(solution)/shard_map/ppermute | solution.py:384
  23.7 3.6 %collective-permute-start.6 = (f32[16,384]{1,0:T(8,128)S(1)}, f32[16,384]{1,0:T(8,128)S(1)}, u32[]{:S(2)}, u32[]{:S(2)}) collective-permute-start(f32[16,384]{1,0:T(8,128)S(1)} %shard_map.59.a), channel_id=1, source_target_pairs={{0,16},{4,20},{8,24},{12,28},{16,0},{20,4},{24,8},{28,12},{32,48},... | collective-permute-start | bytes 73736 | tf_op jit(solution)/shard_map/ppermute | solution.py:384
  27.3 6.1 %collective-permute-start.7 = (f32[16,384]{1,0:T(8,128)S(1)}, f32[16,384]{1,0:T(8,128)S(1)}, u32[]{:S(2)}, u32[]{:S(2)}) collective-permute-start(f32[16,384]{1,0:T(8,128)S(1)} %shard_map.60.a), channel_id=1, source_target_pairs={{0,56},{4,60},{8,48},{12,52},{16,40},{20,44},{24,32},{28,36},{32,2... | collective-permute-start | bytes 73736 | tf_op jit(solution)/shard_map/ppermute | solution.py:384
  31.2 12.9 %collective-permute-start.2 = (f32[64,384]{1,0:T(8,128)S(1)}, f32[64,384]{1,0:T(8,128)S(1)}, u32[]{:S(2)}, u32[]{:S(2)}) collective-permute-start(f32[64,384]{1,0:T(8,128)S(1)} %get-tuple-element.42), channel_id=1, source_target_pairs={{0,16},{4,20},{8,24},{12,28},{16,0},{20,4},{24,8},{28,12},{32,48},... | collective-permute-start | bytes 294920 | tf_op jit(solution)/shard_map/ppermute | solution.py:384
  33.4 4.3 %collective-permute-start.10 = (f32[16,640]{1,0:T(8,128)S(1)}, f32[16,640]{1,0:T(8,128)S(1)}, u32[]{:S(2)}, u32[]{:S(2)}) collective-permute-start(f32[16,640]{1,0:T(8,128)S(1)} %shard_map.61.refs_0_), channel_id=1, source_target_pairs={{0,3},{1,2},{2,1},{3,0},{4,7},{5,6},{6,5},{7,4},{8,11},{9,10},{10,... | collective-permute-start | bytes 122888 | tf_op jit(solution)/shard_map/ppermute | solution.py:384
  35.9 3.1 %collective-permute-start.8 = (f32[16,640]{1,0:T(8,128)S(1)}, f32[16,640]{1,0:T(8,128)S(1)}, u32[]{:S(2)}, u32[]{:S(2)}) collective-permute-start(f32[16,640]{1,0:T(8,128)S(1)} %shard_map.61.refs_0_), channel_id=1, source_target_pairs={{0,1},{1,0},{2,3},{3,2},{4,5},{5,4},{6,7},{7,6},{8,9},{9,8},{10,11... | collective-permute-start | bytes 122888 | tf_op jit(solution)/shard_map/ppermute | solution.py:384
  35.9 4.5 %collective-permute-start.9 = (f32[16,640]{1,0:T(8,128)S(1)}, f32[16,640]{1,0:T(8,128)S(1)}, u32[]{:S(2)}, u32[]{:S(2)}) collective-permute-start(f32[16,640]{1,0:T(8,128)S(1)} %shard_map.61.refs_0_), channel_id=1, source_target_pairs={{0,2},{1,3},{2,0},{3,1},{4,6},{5,7},{6,4},{7,5},{8,10},{9,11},{10,... | collective-permute-start | bytes 122888 | tf_op jit(solution)/shard_map/ppermute | solution.py:384
  40.4 7.8 %collective-permute-start.11 = (f32[64,640]{1,0:T(8,128)S(1)}, f32[64,640]{1,0:T(8,128)S(1)}, u32[]{:S(2)}, u32[]{:S(2)}) collective-permute-start(f32[64,640]{1,0:T(8,128)S(1)} %shard_map.62.mine), channel_id=1, source_target_pairs={{0,4},{4,0},{8,12},{12,8},{16,20},{20,16},{24,28},{28,24},{32,36},... | collective-permute-start | bytes 491528 | tf_op jit(solution)/shard_map/ppermute | solution.py:384
  44.1 5.7 %collective-permute-start.3 = (f32[64,384]{1,0:T(8,128)S(1)}, f32[64,384]{1,0:T(8,128)S(1)}, u32[]{:S(2)}, u32[]{:S(2)}) collective-permute-start(f32[64,384]{1,0:T(8,128)S(1)} %shard_map.57.own), channel_id=1, source_target_pairs={{0,56},{4,60},{8,48},{12,52},{16,40},{20,44},{24,32},{28,36},{32,2... | collective-permute-start | bytes 294920 | tf_op jit(solution)/shard_map/ppermute | solution.py:384
  48.2 3.4 %collective-permute-start.13 = (f32[128,128]{1,0:T(8,128)S(1)}, f32[128,128]{1,0:T(8,128)S(1)}, u32[]{:S(2)}, u32[]{:S(2)}) collective-permute-start(f32[128,128]{1,0:T(8,128)S(1)} %get-tuple-element.50.gram_own), channel_id=1, source_target_pairs={{0,64},{4,68},{8,72},{12,76},{16,80},{20,84},{24,88},{28,92},{32,9... | collective-permute-start | bytes 196616 | tf_op jit(solution)/shard_map/ppermute | solution.py:384
  50.2 3.2 %collective-permute-start.12 = (f32[64,256]{1,0:T(8,128)S(1)}, f32[64,256]{1,0:T(8,128)S(1)}, u32[]{:S(2)}, u32[]{:S(2)}) collective-permute-start(f32[64,256]{1,0:T(8,128)S(1)} %get-tuple-element.48.own), channel_id=1, source_target_pairs={{0,64},{4,68},{8,72},{12,76},{16,80},{20,84},{24,88},{28,92},{32,9... | collective-permute-start | bytes 196616 | tf_op jit(solution)/shard_map/ppermute | solution.py:384
  53.9 4.4 %collective-permute-start.14 = (f32[64,128]{1,0:T(8,128)S(1)}, f32[64,128]{1,0:T(8,128)S(1)}, u32[]{:S(2)}, u32[]{:S(2)}) collective-permute-start(f32[64,128]{1,0:T(8,128)S(1)} %get-tuple-element.51.own), channel_id=1, source_target_pairs={{0,128},{4,132},{8,136},{12,140},{16,144},{20,148},{24,152},{28,15... | collective-permute-start | bytes 98312 | tf_op jit(solution)/shard_map/ppermute | solution.py:384
  58.5 6.0 %collective-permute-start.15 = (f32[64,384]{1,0:T(8,128)S(1)}, f32[64,384]{1,0:T(8,128)S(1)}, u32[]{:S(2)}, u32[]{:S(2)}) collective-permute-start(f32[64,384]{1,0:T(8,128)S(1)} %shard_map.66.mine), channel_id=1, source_target_pairs={{0,16},{4,20},{8,24},{12,28},{16,0},{20,4},{24,8},{28,12},{32,48},... | collective-permute-start | bytes 294920 | tf_op jit(solution)/shard_map/ppermute | solution.py:384
  64.5 9.3 %collective-permute-start.16 = (f32[128,384]{1,0:T(8,128)S(1)}, f32[128,384]{1,0:T(8,128)S(1)}, u32[]{:S(2)}, u32[]{:S(2)}) collective-permute-start(f32[128,384]{1,0:T(8,128)S(1)} %shard_map.67.c), channel_id=1, source_target_pairs={{0,8},{4,12},{8,0},{12,4},{16,24},{20,28},{24,16},{28,20},{32,40},... | collective-permute-start | bytes 589832 | tf_op jit(solution)/shard_map/ppermute | solution.py:384
  66.5 8.7 %collective-permute-start.18 = (f32[128,384]{1,0:T(8,128)S(1)}, f32[128,384]{1,0:T(8,128)S(1)}, u32[]{:S(2)}, u32[]{:S(2)}) collective-permute-start(f32[128,384]{1,0:T(8,128)S(1)} %shard_map.67.c), channel_id=1, source_target_pairs={{0,4},{4,0},{8,12},{12,8},{16,20},{20,16},{24,28},{28,24},{32,36},... | collective-permute-start | bytes 589832 | tf_op jit(solution)/shard_map/ppermute | solution.py:384
  73.8 6.8 %collective-permute-start.17 = (f32[128,384]{1,0:T(8,128)S(1)}, f32[128,384]{1,0:T(8,128)S(1)}, u32[]{:S(2)}, u32[]{:S(2)}) collective-permute-start(f32[128,384]{1,0:T(8,128)S(1)} %collective-permute-done.16.c), channel_id=1, source_target_pairs={{0,4},{4,0},{8,12},{12,8},{16,20},{20,16},{24,28},{28,24},{32,36},... | collective-permute-start | bytes 589832 | tf_op jit(solution)/shard_map/ppermute | solution.py:384
